TPU v7x, 256 devices: a whole 4x4x8 slice. The times are simulated.
256 devices in a mesh: seq: 32 (over y, z), head: 8 (over x, core).
Axes of the slice: x: 4, y: 4, z: 8, core: 2. Of those that a mesh axis runs over, the one named last changes fastest.
Arguments:
- tokens: bfloat16 [32768, 2048], P(('seq', 'head')), may hold values from -6 to 6
- w_in_x: bfloat16 [2048, 4096], P(None, 'head'), may hold values from -0.125 to 0.125
- w_in_z: bfloat16 [2048, 4096], P(None, 'head'), may hold values from -0.125 to 0.125
- w_in_bc: bfloat16 [2048, 256], replicated, may hold values from -0.125 to 0.125
- w_dt: bfloat16 [2048, 64], P(None, 'head'), may hold values from -0.125 to 0.125
- conv_x: float32 [4, 4096], P(None, 'head'), may hold values from -3 to 3
- conv_bc: float32 [4, 256], replicated, may hold values from -3 to 3
- dt_bias: float32 [64], P('head'), may hold values from -1 to 1
- decay_rate: float32 [64], P('head'), may hold values from 1.5258789e-06 to 0.05, as said below
- skip: float32 [64], P('head'), may hold values from 0.5 to 1.5
- norm_gain: float32 [4096], P('head'), may hold values from 0.25 to 1.75
- w_out: bfloat16 [4096, 2048], P('head'), may hold values from -0.09375 to 0.09375
Outputs:
- mixed: bfloat16 [32768, 2048], P(('seq', 'head'))
Inputs may be any that keep to these rules, and one draw needn't show every extreme that they name: `decay_rate`: positive per-head decay rates.
All inputs are finite; a program needn't handle non-finite values.
Results may differ from a plain program's by a relative error of at most 0.013.
Values may be sent and summed in bfloat16 or wider, within the bound.
No kernel may reach another device: no remote copies, remote signals or barrier semaphores. Data moves between devices by JAX's collectives and lax.ppermute only.
A program may use at most 128 MiB of HBM per device.

v0:
```python
import jax
import jax.numpy as jnp
from jax import lax
from jax.sharding import Mesh
from jax.sharding import PartitionSpec as P

SPAN = 256
KERNEL = 4
E = 4096
SEQ = ("seq_0", "seq_1")
SEQ_HEAD = ("seq_0", "seq_1", "head")


highest = lax.Precision.HIGHEST


def passed_along(block, axis, distance):
    devices = range(lax.axis_size(axis))
    route = [(i - distance, i) for i in devices if i - distance in devices]
    return lax.ppermute(block, axis, route)


def neutral_like(shard, identity):
    return jax.tree.map(
        lambda part, zero: jnp.zeros_like(part) + jnp.asarray(zero, part.dtype), shard, identity
    )


def entering_2(shard, axes, combine, identity):
    before = start = neutral_like(shard, identity)
    running = shard
    for axis in reversed(axes):
        size, index = (lax.axis_size(axis), lax.axis_index(axis))
        pieces = jax.tree.map(lambda part: lax.all_gather(part, axis), running)
        inside, running = (start, start)
        for k in range(size):
            passed = k < index
            running = combine(running, jax.tree.map(lambda part: part[k], pieces))
            inside = jax.tree.map(lambda new, old: jnp.where(passed, new, old), running, inside)
        before = combine(inside, before)
    return before


def sent_to_all(shard, axis):
    size = lax.axis_size(axis)
    return lax.all_to_all(
        jnp.broadcast_to(shard[None], (size, *shard.shape)), axis, 0, 0, tiled=True
    )


def over_copies(shard, axis):
    everything = sent_to_all(shard, axis)
    return jnp.sum(everything, axis=0)


def span_update(state, x_span, step_span, decay_span, b_span, c_span, skip):
    cumul = jnp.cumsum(decay_span, axis=0)
    length = x_span.shape[0]
    lower = jnp.arange(length)[:, None] >= jnp.arange(length)[None, :]
    spread = cumul.T[:, :, None] - cumul.T[:, None, :]
    within = jnp.exp(jnp.where(lower[None], spread, -jnp.inf))
    scores = jnp.dot(c_span, b_span.T, precision=highest)
    scaled = x_span * step_span[:, :, None]
    output = jnp.einsum("hts,shp->thp", within * scores[None], scaled, precision=highest)
    output = (
        output
        + jnp.einsum("tn,hpn->thp", c_span, state, precision=highest) * jnp.exp(cumul)[:, :, None]
    )
    output = output + skip[None, :, None] * x_span
    remain = jnp.exp(cumul[-1][None, :] - cumul)
    fresh = jnp.einsum("shp,sn->hpn", scaled * remain[:, :, None], b_span, precision=highest)
    return (jnp.exp(cumul[-1])[:, None, None] * state + fresh, output, cumul)


def causal_conv(values, before, kernel):
    padded = jnp.concatenate([before, values], axis=0)
    length = values.shape[0]
    result = kernel[0] * padded[0:length]
    for offset in range(1, kernel.shape[0]):
        result = result + kernel[offset] * padded[offset : offset + length]
    return jax.nn.silu(result)


def per_device(
    tokens,
    w_in_x,
    w_in_z,
    w_in_bc,
    w_dt,
    conv_x,
    conv_bc,
    dt_bias,
    decay_rate,
    skip,
    norm_gain,
    w_out,
):
    inner_cols = w_in_x.shape[1]
    head_count = dt_bias.shape[0]
    head_width = inner_cols // head_count
    state_size = w_in_bc.shape[1] // 2
    block_rows = lax.all_gather(tokens, "head", axis=0, tiled=True)
    joined = jnp.concatenate(
        [
            jnp.dot(block_rows, w_in_x, preferred_element_type=jnp.float32),
            jnp.dot(block_rows, w_in_z, preferred_element_type=jnp.float32),
            jnp.dot(block_rows, w_in_bc, preferred_element_type=jnp.float32),
            jnp.dot(block_rows, w_dt, preferred_element_type=jnp.float32),
        ],
        axis=1,
    )
    x_proj = joined[:, :inner_cols]
    gate_proj = joined[:, inner_cols : 2 * inner_cols]
    bc_proj = joined[:, 2 * inner_cols : 2 * inner_cols + 2 * state_size]
    step_raw = joined[:, 2 * inner_cols + 2 * state_size :]
    margin = KERNEL - 1
    x_before, bc_before = passed_along((x_proj[-margin:], bc_proj[-margin:]), SEQ, 1)
    x_conv = causal_conv(x_proj, x_before, conv_x)
    bc_conv = causal_conv(bc_proj, bc_before, conv_bc)
    step_size = jax.nn.softplus(step_raw + dt_bias)
    log_decay = -step_size * decay_rate
    seg_rows = x_proj.shape[0]
    spans = seg_rows // SPAN

    def advance(carry, inputs):
        state, offset = carry
        x_span, step_span, decay_span, bc_span = inputs
        state, output, cumul = span_update(
            state,
            x_span,
            step_span,
            decay_span,
            bc_span[:, :state_size],
            bc_span[:, state_size:],
            skip,
        )
        return ((state, offset + cumul[-1]), (output, cumul + offset))

    empty_state = jnp.zeros((head_count, head_width, state_size), jnp.float32)
    empty_decay = jnp.zeros((head_count,), jnp.float32)
    (final_state, totals), (outputs, cumuls) = lax.scan(
        advance,
        (empty_state, empty_decay),
        (
            x_conv.reshape(spans, SPAN, head_count, head_width),
            step_size.reshape(spans, SPAN, head_count),
            log_decay.reshape(spans, SPAN, head_count),
            bc_conv.reshape(spans, SPAN, 2 * state_size),
        ),
    )
    local_out = outputs.reshape(seg_rows, head_count, head_width)
    segment_cumul = cumuls.reshape(seg_rows, head_count)

    def combine(earlier, later):
        return (earlier[0] + later[0], jnp.exp(later[0])[:, None, None] * earlier[1] + later[1])

    entering = entering_2((totals, final_state), SEQ, combine, (empty_decay, empty_state))[1]
    c_matrix = bc_conv[:, state_size:]
    carried = (
        jnp.einsum("tn,hpn->thp", c_matrix, entering, precision=highest)
        * jnp.exp(segment_cumul)[:, :, None]
    )
    ssd_out = (local_out + carried).reshape(seg_rows, inner_cols)
    gated = ssd_out * jax.nn.silu(gate_proj)
    squares = over_copies(jnp.sum(gated * gated, axis=1), "head")
    normed = (gated * lax.rsqrt(squares / E + 1e-05)[:, None] * norm_gain).astype(jnp.bfloat16)
    result = lax.psum_scatter(
        jnp.dot(normed, w_out, preferred_element_type=jnp.float32).astype(jnp.bfloat16),
        "head",
        scatter_dimension=0,
        tiled=True,
    )
    return result


def solution(mesh):
    torus = Mesh(mesh.devices.reshape(4, 8, mesh.shape["head"]), ("seq_0", "seq_1", "head"))
    placed = (
        P(SEQ_HEAD, None),
        P(None, "head"),
        P(None, "head"),
        P(),
        P(None, "head"),
        P(None, "head"),
        P(),
        P("head"),
        P("head"),
        P("head"),
        P("head"),
        P("head", None),
    )
    return jax.shard_map(
        per_device, mesh=torus, in_specs=placed, out_specs=P(SEQ_HEAD, None), check_vma=False
    )
```

profile of v0, /device:TPU:8, one launch (start us, length us, event | category | flops | bytes accessed | tf_op | source)
XLA Modules:
  0.0 303.0 jit_solution(5351362348094303624)
XLA Ops:
  6.5 0.7 all-gather.7.cloned.1.call-update
  7.3 0.8 fusion.148
  8.2 0.9 fusion.147
  9.0 37.6 %all-gather.7.cloned.1.call-done = bf16[1024,2048]{1,0:T(8,128)(2,1)} async-done(((bf16[128,2048]{1,0:T(8,128)(2,1)}), bf16[1024,2048]{1,0:T(8,128)(2,1)}) %all-gather.7.cloned.1.call-update) | async-done | bytes 4194320 | tf_op jit(solution)/shard_map/all_gather | solution.py:102
  46.7 3.9 %fusion.150 = f32[1024,256]{1,0:T(8,128)S(1)} fusion(bf16[1024,2048]{1,0:T(8,128)(2,1)} %all-gather.7.cloned.1.call-done, bf16[2048,256]{1,0:T(8,128)(2,1)} %param.17), kind=kOutput, calls=%fused_computation.216 | convolution fusion | flops 1073741824 | bytes 6291456 | tf_op jit(solution)/shard_map/dot_general | solution.py:107
  50.6 3.6 %collective-permute-start.1 = (f32[3,256]{1,0:T(4,128)S(1)}, f32[3,256]{1,0:T(4,128)S(1)}, u32[]{:S(2)}, u32[]{:S(2)}) collective-permute-start(f32[3,256]{1,0:T(4,128)S(1)} %slice.215), channel_id=1, source_target_pairs={{0,8},{8,16},{16,24},{24,32},{32,40},{40,48},{48,56},{56,64},{64,7... | collective-permute-start | bytes 9224 | tf_op jit(solution)/shard_map/ppermute | solution.py:20
  54.2 2.3 fusion.149
  56.6 3.5 %collective-permute-start = (f32[3,512]{1,0:T(4,128)S(1)}, f32[3,512]{1,0:T(4,128)S(1)}, u32[]{:S(2)}, u32[]{:S(2)}) collective-permute-start(f32[3,512]{1,0:T(4,128)S(1)} %slice.210), channel_id=1, source_target_pairs={{0,8},{8,16},{16,24},{24,32},{32,40},{40,48},{48,56},{56,64},{64,7... | collective-permute-start | bytes 18440 | tf_op jit(solution)/shard_map/ppermute | solution.py:20
  60.1 1.2 negate_multiply_fusion
  61.3 1.7 divide_multiply_fusion.1
  63.0 1.2 collective-permute-done
  64.2 2.3 divide_multiply_fusion
  66.5 4.4 %reshape.345 = f32[4,256,8,64]{3,2,1,0:T(8,128)} reshape(f32[1024,512]{1,0:T(8,128)} %divide_multiply_fusion) | data formatting | bytes 4194304 | tf_op jit(solution)/shard_map/reshape | solution.py:145
  70.9 3.8 %copy.48 = f32[4,256,8,64]{1,3,2,0:T(8,128)} copy(f32[4,256,8,64]{3,2,1,0:T(8,128)} %reshape.345) | data formatting | bytes 4194304
  74.7 81.7 %while.17 = (s32[]{:T(128)}, f32[8,64,128]{2,1,0:T(8,128)S(1)}, f32[8]{0:T(128)S(1)}, f32[4,256,8,64]{1,0,3,2:T(4,128)}, f32[4,256,8]{1,2,0:T(8,128)S(1)}, /*ind...) while((s32[]{:T(128)}, f32[8,64,128]{2,1,0:T(8,128)S(1)}, ...), condition=%wide.region_3.4_spmd.clone, body=%wide.region_0.3_spmd.clone.sunk | while | flops 909056064 | bytes 16289238 | solution.py:141
  74.8 0.6 reduce-window.14
  75.7 0.2 slice_reduce_fusion.5
  76.0 1.1 dynamic-slice_bitcast_fusion.8
  77.2 0.4 fusion.181
  77.5 3.5 %fusion.182 = f32[256,8,64]{0,2,1:T(8,128)S(1)} fusion(f32[256,256]{1,0:T(8,128)S(1)} %fusion.181, f32[8,256]{1,0:T(8,128)S(1)} %add_bitcast_fusion.4, pred[256,256]{1,0:T(8,128)(4,1)S(1)} %iota_compare_fusion.2, f32[4,256,8,64]{1,3,2,0:T(8,128)} %get-tuple-element.315, s32[]{:T(128)S(6)} %copy.71, f32[256,8]{0,1:T(8,128)S(1)} %dynamic-slice_bitcast_fusion.7), kind=kOutput, calls=%fused_computation.5.clone.1 | convolution fusion | flops 404357120 | bytes 1400836 | tf_op jit(solution)/shard_map/while/body/eval_jaxpr/hts,shp->thp/dot_general | solution.py:64
  81.0 0.6 fusion.183
  81.6 0.7 convolution_add_fusion.3
  82.3 0.5 copy.63
  82.9 12.3 %dynamic_update_slice.14 = f32[4,256,8,64]{1,0,3,2:T(4,128)} dynamic-update-slice(f32[4,256,8,64]{1,0,3,2:T(4,128)} %get-tuple-element.299, f32[1,256,8,64]{1,0,3,2:T(1,128)S(1)} %copy.63, s32[]{:T(128)S(6)} %copy.71, s32[]{:T(128)} %constant.25.clone.1..sunk, s32[]{:T(128)} %constant.25.clone.1..sunk, s32[]{:T(128)} %constant.25.clone.1..sunk) | dynamic-update-slice | bytes 1048580 | tf_op jit(solution)/shard_map/while/body/jit(dynamic_update_index_in_dim)/dynamic_update_slice | solution.py:141
  95.2 0.6 reduce-window.14
  96.4 1.1 dynamic-slice_bitcast_fusion.8
  97.6 0.4 fusion.181
  97.9 3.5 %fusion.182 = f32[256,8,64]{0,2,1:T(8,128)S(1)} fusion(f32[256,256]{1,0:T(8,128)S(1)} %fusion.181, f32[8,256]{1,0:T(8,128)S(1)} %add_bitcast_fusion.4, pred[256,256]{1,0:T(8,128)(4,1)S(1)} %iota_compare_fusion.2, f32[4,256,8,64]{1,3,2,0:T(8,128)} %get-tuple-element.315, s32[]{:T(128)S(6)} %copy.71, f32[256,8]{0,1:T(8,128)S(1)} %dynamic-slice_bitcast_fusion.7), kind=kOutput, calls=%fused_computation.5.clone.1 | convolution fusion | flops 404357120 | bytes 1400836 | tf_op jit(solution)/shard_map/while/body/eval_jaxpr/hts,shp->thp/dot_general | solution.py:64
  101.4 0.6 fusion.183
  102.0 0.7 convolution_add_fusion.3
  102.7 0.5 copy.63
  103.3 12.3 %dynamic_update_slice.14 = f32[4,256,8,64]{1,0,3,2:T(4,128)} dynamic-update-slice(f32[4,256,8,64]{1,0,3,2:T(4,128)} %get-tuple-element.299, f32[1,256,8,64]{1,0,3,2:T(1,128)S(1)} %copy.63, s32[]{:T(128)S(6)} %copy.71, s32[]{:T(128)} %constant.25.clone.1..sunk, s32[]{:T(128)} %constant.25.clone.1..sunk, s32[]{:T(128)} %constant.25.clone.1..sunk) | dynamic-update-slice | bytes 1048580 | tf_op jit(solution)/shard_map/while/body/jit(dynamic_update_index_in_dim)/dynamic_update_slice | solution.py:141
  115.6 0.6 reduce-window.14
  116.5 0.2 slice_reduce_fusion.5
  116.8 1.1 dynamic-slice_bitcast_fusion.8
  118.0 0.4 fusion.181
  118.4 3.5 %fusion.182 = f32[256,8,64]{0,2,1:T(8,128)S(1)} fusion(f32[256,256]{1,0:T(8,128)S(1)} %fusion.181, f32[8,256]{1,0:T(8,128)S(1)} %add_bitcast_fusion.4, pred[256,256]{1,0:T(8,128)(4,1)S(1)} %iota_compare_fusion.2, f32[4,256,8,64]{1,3,2,0:T(8,128)} %get-tuple-element.315, s32[]{:T(128)S(6)} %copy.71, f32[256,8]{0,1:T(8,128)S(1)} %dynamic-slice_bitcast_fusion.7), kind=kOutput, calls=%fused_computation.5.clone.1 | convolution fusion | flops 404357120 | bytes 1400836 | tf_op jit(solution)/shard_map/while/body/eval_jaxpr/hts,shp->thp/dot_general | solution.py:64
  121.9 0.6 fusion.183
  122.4 0.7 convolution_add_fusion.3
  123.1 0.5 copy.63
  123.7 12.3 %dynamic_update_slice.14 = f32[4,256,8,64]{1,0,3,2:T(4,128)} dynamic-update-slice(f32[4,256,8,64]{1,0,3,2:T(4,128)} %get-tuple-element.299, f32[1,256,8,64]{1,0,3,2:T(1,128)S(1)} %copy.63, s32[]{:T(128)S(6)} %copy.71, s32[]{:T(128)} %constant.25.clone.1..sunk, s32[]{:T(128)} %constant.25.clone.1..sunk, s32[]{:T(128)} %constant.25.clone.1..sunk) | dynamic-update-slice | bytes 1048580 | tf_op jit(solution)/shard_map/while/body/jit(dynamic_update_index_in_dim)/dynamic_update_slice | solution.py:141
  136.0 0.6 reduce-window.14
  137.3 1.1 dynamic-slice_bitcast_fusion.8
  138.4 0.4 fusion.181
  138.8 3.5 %fusion.182 = f32[256,8,64]{0,2,1:T(8,128)S(1)} fusion(f32[256,256]{1,0:T(8,128)S(1)} %fusion.181, f32[8,256]{1,0:T(8,128)S(1)} %add_bitcast_fusion.4, pred[256,256]{1,0:T(8,128)(4,1)S(1)} %iota_compare_fusion.2, f32[4,256,8,64]{1,3,2,0:T(8,128)} %get-tuple-element.315, s32[]{:T(128)S(6)} %copy.71, f32[256,8]{0,1:T(8,128)S(1)} %dynamic-slice_bitcast_fusion.7), kind=kOutput, calls=%fused_computation.5.clone.1 | convolution fusion | flops 404357120 | bytes 1400836 | tf_op jit(solution)/shard_map/while/body/eval_jaxpr/hts,shp->thp/dot_general | solution.py:64
  142.3 0.6 fusion.183
  142.9 0.7 convolution_add_fusion.3
  143.5 0.5 copy.63
  144.1 12.3 %dynamic_update_slice.14 = f32[4,256,8,64]{1,0,3,2:T(4,128)} dynamic-update-slice(f32[4,256,8,64]{1,0,3,2:T(4,128)} %get-tuple-element.299, f32[1,256,8,64]{1,0,3,2:T(1,128)S(1)} %copy.63, s32[]{:T(128)S(6)} %copy.71, s32[]{:T(128)} %constant.25.clone.1..sunk, s32[]{:T(128)} %constant.25.clone.1..sunk, s32[]{:T(128)} %constant.25.clone.1..sunk) | dynamic-update-slice | bytes 1048580 | tf_op jit(solution)/shard_map/while/body/jit(dynamic_update_index_in_dim)/dynamic_update_slice | solution.py:141
  156.4 0.7 copy-done.1
  157.2 0.7 dynamic-slice
  158.5 0.2 dynamic-update-slice
  158.8 15.8 %all-reduce = f32[64]{0:T(128)S(1)} all-reduce(f32[64]{0:T(128)S(1)} %dynamic-update-slice), channel_id=2, replica_groups=mesh['seq_0'=4,'seq_1'=8,'head'=8] {'seq_1'}, use_global_device_ids=true, to_apply=%add | all-reduce | flops 64 | bytes 512
  174.7 21.7 %all-gather.11.cloned.1.call-done = f32[64,64,128]{2,1,0:T(8,128)} async-done(((f32[8,64,128]{2,1,0:T(8,128)}), f32[64,64,128]{2,1,0:T(8,128)}) %all-gather.11.cloned.1.call-update) | async-done | bytes 2097168 | tf_op jit(solution)/shard_map/all_gather | solution.py:34
  196.4 2.4 bitcast_add_fusion
  198.9 7.8 %all-gather.2 = f32[4,1,8]{2,1,0:T(1,128)S(1)} all-gather(f32[1,1,8]{2,1,0:T(1,128)S(1)} %get-tuple-element.197), channel_id=1, replica_groups=mesh['seq_0'=4,'seq_1'=8,'head'=8] {'seq_0'}, dimensions={0}, use_global_device_ids=true | all-gather | bytes 160 | tf_op jit(solution)/shard_map/all_gather | solution.py:34
  206.7 3.3 %reshape.235 = f32[1024,8,64]{0,2,1:T(8,128)} reshape(f32[4,256,8,64]{1,0,3,2:T(4,128)} %get-tuple-element.60) | data formatting | bytes 4194304 | tf_op jit(solution)/shard_map/reshape | solution.py:151
  210.0 13.0 %all-gather.9.cloned.1.call-done = f32[4,8,64,128]{3,2,1,0:T(8,128)} async-done(((f32[1,8,64,128]{3,2,1,0:T(8,128)}), f32[4,8,64,128]{3,2,1,0:T(8,128)}) %all-gather.9.cloned.1.call-update) | async-done | bytes 1048592 | tf_op jit(solution)/shard_map/all_gather | solution.py:34
  223.1 6.3 %multiply_add_fusion = f32[1024,8,64]{0,2,1:T(8,128)} fusion(f32[1024,8,64]{0,2,1:T(8,128)} %reshape.235, f32[1024,8]{0,1:T(8,128)S(1)} %bitcast.186, f32[1024,256]{1,0:T(8,128)} %divide_multiply_fusion.1, f32[4,8,64,128]{3,2,1,0:T(8,128)} %all-gather.9.cloned.1.call-done, f32[64,64,128]{2,1,0:T(8,128)} %all-gather.11.cloned.1.call-done, ...), kind=kOutput, calls=%fused_computation.64 | convolution fusion | flops 808714240 | bytes 7897516 | tf_op jit(solution)/shard_map/tn,hpn->thp/dot_general | solution.py:160
  229.3 2.9 copy.52
  232.2 7.4 %multiply_reduce_fusion = (f32[1024]{0:T(1024)S(1)}, f32[1024,512]{1,0:T(8,128)}) fusion(f32[1024,512]{1,0:T(8,128)} %copy.52, bf16[1024,2048]{1,0:T(8,128)(2,1)} %all-gather.7.cloned.1.call-done, bf16[2048,512]{1,0:T(8,128)(2,1)} %param.16), kind=kOutput, calls=%fused_computation.62 | convolution fusion | flops 2151152640 | bytes 10489856 | tf_op jit(solution)/shard_map/dot_general | solution.py:106
  239.6 9.5 %all_to_all.6 = f32[8,1,1024]{2,1,0:T(1,128)S(1)} all-to-all(f32[8,1,1024]{2,1,0:T(1,128)S(1)} %broadcast_in_dim.43), channel_id=1, replica_groups=mesh['seq_0'=4,'seq_1'=8,'head'=8] {'head'}, dimensions={0} | all-to-all | bytes 65536 | tf_op jit(solution)/shard_map/all_to_all | solution.py:46
  249.2 6.9 %convolution_convert_fusion = bf16[1024,2048]{1,0:T(8,128)(2,1)} fusion(bf16[512,2048]{1,0:T(8,128)(2,1)S(1)} %copy-done, f32[512]{0:T(512)S(1)} %copy-done.9, f32[1024]{0:T(1024)S(1)} %add_rsqrt_fusion, f32[1024,512]{1,0:T(8,128)} %copy.52, f32[1024,512]{1,0:T(8,128)} %get-tuple-element.209), kind=kOutput, calls=%fused_computation.49 | convolution fusion | flops 2153775104 | bytes 10491904 | tf_op jit(solution)/shard_map/dot_general | solution.py:168
  256.1 40.4 %reduce-scatter.2.cloned.1.call-done = bf16[128,2048]{1,0:T(8,128)(2,1)} async-done(((bf16[1024,2048]{1,0:T(8,128)(2,1)}), bf16[128,2048]{1,0:T(8,128)(2,1)}) %reduce-scatter.2.cloned.1.call-update) | async-done | bytes 524304 | tf_op jit(solution)/shard_map/reduce_scatter | solution.py:167
  (95 shorter events, 2.8 us)
Async XLA Ops:
  6.5 242.6 %copy-start = (bf16[512,2048]{1,0:T(8,128)(2,1)S(1)}, bf16[512,2048]{1,0:T(8,128)(2,1)}, u32[]{:S(2)}) copy-start(bf16[512,2048]{1,0:T(8,128)(2,1)} %param.25) | copy-start | bytes 6291460
  6.5 40.1 %all-gather.7.cloned.1.call-start = ((), (), s32[]{:S(2)}) async-start(), calls=%async_computation.2 | async-start | bytes 4718592 | tf_op jit(solution)/shard_map/all_gather | solution.py:102
  7.3 189.1 %all-gather.11.cloned.1.call-start = ((), (), s32[]{:S(2)}) async-start(), calls=%async_computation.5 | async-start | bytes 2359296 | tf_op jit(solution)/shard_map/all_gather | solution.py:34
  46.7 7.5 %copy-start.3 = (bf16[1024,2048]{1,0:T(8,128)(2,1)S(1)}, bf16[1024,2048]{1,0:T(8,128)(2,1)}, u32[]{:S(2)}) copy-start(bf16[1024,2048]{1,0:T(8,128)(2,1)} %all-gather.7.cloned.1.call-done) | copy-start | bytes 12582916
  46.7 7.6 %copy-start.8 = (bf16[2048,512]{1,0:T(8,128)(2,1)S(1)}, bf16[2048,512]{1,0:T(8,128)(2,1)}, u32[]{:S(2)}) copy-start(bf16[2048,512]{1,0:T(8,128)(2,1)} %param.15) | copy-start | bytes 6291460
  50.6 9.5 %copy-start.4 = (bf16[2048,8]{0,1:T(8,128)(2,1)S(1)}, bf16[2048,8]{0,1:T(8,128)(2,1)}, u32[]{:S(2)}) copy-start(bf16[2048,8]{0,1:T(8,128)(2,1)} %param.18) | copy-start | bytes 98308
  50.6 9.5 %copy-start.6 = (f32[8]{0:T(128)S(1)}, f32[8]{0:T(128)}, u32[]{:S(2)}) copy-start(f32[8]{0:T(128)} %param.22) | copy-start | bytes 100
  50.6 9.5 %copy-start.7 = (f32[8]{0:T(128)S(1)}, f32[8]{0:T(128)}, u32[]{:S(2)}) copy-start(f32[8]{0:T(128)} %param.21) | copy-start | bytes 100
  50.6 10.7 %collective-permute-start.1 = (f32[3,256]{1,0:T(4,128)S(1)}, f32[3,256]{1,0:T(4,128)S(1)}, u32[]{:S(2)}, u32[]{:S(2)}) collective-permute-start(f32[3,256]{1,0:T(4,128)S(1)} %slice.215), channel_id=1, source_target_pairs={{0,8},{8,16},{16,24},{24,32},{32,40},{40,48},{48,56},{56,64},{64,7... | collective-permute-start | bytes 9224 | tf_op jit(solution)/shard_map/ppermute | solution.py:20
  56.6 7.7 %collective-permute-start = (f32[3,512]{1,0:T(4,128)S(1)}, f32[3,512]{1,0:T(4,128)S(1)}, u32[]{:S(2)}, u32[]{:S(2)}) collective-permute-start(f32[3,512]{1,0:T(4,128)S(1)} %slice.210), channel_id=1, source_target_pairs={{0,8},{8,16},{16,24},{24,32},{32,40},{40,48},{48,56},{56,64},{64,7... | collective-permute-start | bytes 18440 | tf_op jit(solution)/shard_map/ppermute | solution.py:20
  70.9 3.8 %copy-start.5 = (f32[8]{0:T(128)S(1)}, f32[8]{0:T(128)}, u32[]{:S(2)}) copy-start(f32[8]{0:T(128)} %param.23) | copy-start | bytes 100
  74.7 82.5 %copy-start.10 = (u32[256]{0:T(256)S(1)}, u32[256]{0:T(256)}, u32[]{:S(2)}) copy-start(u32[256]{0:T(256)} %constant.70) | copy-start | bytes 3076
  76.0 5.0 %copy-start.2 = (f32[4,256,8,64]{1,3,2,0:T(8,128)S(1)}, f32[4,256,8,64]{1,3,2,0:T(8,128)}, u32[]{:S(2)}) copy-start(f32[4,256,8,64]{1,3,2,0:T(8,128)} %get-tuple-element.315) | copy-start | bytes 6291460 | tf_op jit(solution)/shard_map/while
  96.4 5.0 %copy-start.2 = (f32[4,256,8,64]{1,3,2,0:T(8,128)S(1)}, f32[4,256,8,64]{1,3,2,0:T(8,128)}, u32[]{:S(2)}) copy-start(f32[4,256,8,64]{1,3,2,0:T(8,128)} %get-tuple-element.315) | copy-start | bytes 6291460 | tf_op jit(solution)/shard_map/while
  116.8 5.0 %copy-start.2 = (f32[4,256,8,64]{1,3,2,0:T(8,128)S(1)}, f32[4,256,8,64]{1,3,2,0:T(8,128)}, u32[]{:S(2)}) copy-start(f32[4,256,8,64]{1,3,2,0:T(8,128)} %get-tuple-element.315) | copy-start | bytes 6291460 | tf_op jit(solution)/shard_map/while
  137.3 5.0 %copy-start.2 = (f32[4,256,8,64]{1,3,2,0:T(8,128)S(1)}, f32[4,256,8,64]{1,3,2,0:T(8,128)}, u32[]{:S(2)}) copy-start(f32[4,256,8,64]{1,3,2,0:T(8,128)} %get-tuple-element.315) | copy-start | bytes 6291460 | tf_op jit(solution)/shard_map/while
  156.4 0.7 copy-start.1
  157.1 65.9 %all-gather.9.cloned.1.call-start = ((), (), s32[]{:S(2)}) async-start(), calls=%async_computation.3 | async-start | bytes 1310720 | tf_op jit(solution)/shard_map/all_gather | solution.py:34
  198.8 97.6 %reduce-scatter.2.cloned.1.call-start = ((), (), s32[]{:S(2)}) async-start(), calls=%async_computation.4 | async-start | bytes 4718592 | tf_op jit(solution)/shard_map/reduce_scatter | solution.py:167
  232.2 17.0 %copy-start.9 = (f32[512]{0:T(512)S(1)}, f32[512]{0:T(512)}, u32[]{:S(2)}) copy-start(f32[512]{0:T(512)} %param.24) | copy-start | bytes 6148
Sparse Core Ops, SparseCore 0:
  9.2 37.4 all-gather.6
  157.3 39.0 all-gather.10
  199.0 24.0 all-gather.8
  256.2 40.2 reduce-scatter.1
where the time goes:
time: 305 us; the launch traced here: 303 us
  waiting for transfers between devices  115 us (38%)
  local copies, waits for them, and re-layouts  75.1 us (25%)
  matrix products  48.5 us (16%)
  blocking collectives  33.1 us (11%)
  between operations  14 us (5%)
  other arithmetic  10.2 us (3%)
  starting transfers between devices  7.17 us (2%)
    dynamic_update_slice x8, local copies, waits for them, and re-layouts, per_device(): lax.scan(advance, (empty_state, empty_decay), (x_conv.reshape(spans, SPAN...  51.4 us
    reduce_scatter x1, waiting for transfers between devices, per_device(): lax.psum_scatter(jnp.dot(normed, w_out, preferred_element_type=jnp.float3...  40.4 us
    all_gather x1, waiting for transfers between devices, per_device(): block_rows = lax.all_gather(tokens, 'head', axis=0, tiled=True)  37.6 us
    all_gather x2, waiting for transfers between devices, entering_2(): pieces = jax.tree.map(lambda part: lax.all_gather(part, axis), running)  34.7 us
    unnamed x1, blocking collectives  15.8 us
    dot_general x4, matrix products, span_update(): jnp.einsum('hts,shp->thp', within * scores[None], scaled, precision=highest)  13.9 us
    all_to_all x1, blocking collectives, sent_to_all(): lax.all_to_all(jnp.broadcast_to(shard[None], (size, *shard.shape)), axis,...  9.5 us
    all_gather x1, blocking collectives, entering_2(): pieces = jax.tree.map(lambda part: lax.all_gather(part, axis), running)  7.78 us
  transfers between devices with their start and end apart: 6, of which 5 were waited for; matrix products, arithmetic and copies ran while one was open for 4% of the time, Pallas kernels for 0%

commit v1 on v0

v1 whole, which is shorter than its diff:
```python
import jax
import jax.numpy as jnp
from jax import lax
from jax.experimental import pallas as pl
from jax.experimental.pallas import tpu as pltpu
from jax.sharding import Mesh
from jax.sharding import PartitionSpec as P


E = 4096
Q = 128
KERNEL = 4
SEQ = ("y", "z")
ALL = ("y", "z", "x", "c")
F32 = jnp.float32
BF16 = jnp.bfloat16
highest = lax.Precision.HIGHEST


def silu(v):
    half = 0.5 * v
    return half + half * jnp.tanh(half)


def shift(block, axis, distance):
    size = lax.axis_size(axis)
    return lax.ppermute(block, axis, [(i, (i + distance) % size) for i in range(size)])


def later(block, axis, distance):
    size = lax.axis_size(axis)
    return lax.ppermute(block, axis, [(i, i + distance) for i in range(size - distance)])


def fold(values, heads, chunk):
    lanes = values.shape[1]
    high = values.astype(BF16).astype(F32)
    low = values - high
    first = pltpu.roll(high, -chunk * heads % lanes, 1) if chunk else high
    second = pltpu.roll(low, (heads - chunk * heads) % lanes, 1) if chunk != 1 else low
    lane = lax.broadcasted_iota(jnp.int32, values.shape, 1)
    return jnp.where(lane < heads, first, second).astype(BF16)


def widen(values, heads, chunk, spread):
    return jnp.dot(fold(values, heads, chunk), spread, preferred_element_type=F32)


def spread_of(heads, width):
    line = lax.broadcasted_iota(jnp.int32, (Q, width), 0)
    lane = lax.broadcasted_iota(jnp.int32, (Q, width), 1)
    hit = (line % heads == lane // (width // heads)) & (line < 2 * heads)
    return jnp.where(hit, 1.0, 0.0).astype(BF16)


def lanes_of(scalars, heads, limit):
    lane = lax.broadcasted_iota(jnp.int32, (1, Q), 1)
    row = jnp.zeros((1, Q), F32)
    for head in range(heads):
        row = jnp.where(lane % heads == head, scalars[head], row)
    return jnp.where(lane < limit, row, 0.0)


def starts_of(chunks):
    size = chunks // 2
    x_at, c_at = lax.axis_index("x"), lax.axis_index("c")
    places = []
    for distance in (0, size - 1, 1, 2):
        moved = x_at + distance
        place = jnp.where(moved >= size, moved - size, moved) * 2
        places += [(place + c_at) * Q, (place + 1 - c_at) * Q]
    return places


def three_rows(whole):
    row = lax.broadcasted_iota(jnp.int32, whole.shape, 0) % 16
    high = whole.astype(BF16).astype(F32)
    middle = (whole - high).astype(BF16).astype(F32)
    low = whole - high - middle
    return jnp.where(
        row == 0, high, jnp.where(row == 1, middle, jnp.where(row == 2, low, 0.0))
    ).astype(BF16)


def summary_kernel(heads, chunks):
    def kernel(
        bias, rate, g0, g1, g2, g3, halo, taps_x, taps_bc,
        xc_out, bc_out, dt_out, cum_out, last_out, window, scaled,
    ):
        width = xc_out.shape[1]
        conv_cols = width + bc_out.shape[1]
        starts = starts_of(chunks)
        for group, ref in enumerate((g0, g1, g2, g3)):
            for member in range(2):
                at = pl.multiple_of(starts[2 * group + member] + 8, 8)
                window[pl.ds(at, Q), :] = ref[member * Q : member * Q + Q, :]
        window[0:8, :conv_cols] = halo[...]
        spread = spread_of(heads, width)
        row = lax.broadcasted_iota(jnp.int32, (Q, Q), 0)
        col = lax.broadcasted_iota(jnp.int32, (Q, Q), 1)
        tri = jnp.where(row >= col, 1.0, 0.0)
        taps = jnp.concatenate([taps_x[...], taps_bc[...]], axis=1)
        lane = lax.broadcasted_iota(jnp.int32, (Q, Q), 1)
        raw = jnp.zeros((Q, Q), F32)
        for chunk in range(chunks):
            lo = 8 + chunk * Q
            part = window[lo : lo + Q, conv_cols:]
            part = pltpu.roll(part, chunk * heads, 1) if chunk else part
            raw = jnp.where(lane // heads == chunk, part, raw)
        raw = raw + lanes_of(bias, heads, chunks * heads)
        dt = jnp.maximum(raw, 0.0) + jnp.log1p(jnp.exp(-jnp.abs(raw)))
        log_decay = -dt * lanes_of(rate, heads, chunks * heads)
        cumul = jnp.dot(tri, log_decay, precision=highest, preferred_element_type=F32)
        dt_out[...] = dt
        cum_out[...] = cumul
        total = cumul[Q - 1 : Q, :]
        suffix = jnp.zeros((8, Q), F32)
        wide_total = jnp.broadcast_to(total, (8, Q))
        for k in range(1, chunks):
            suffix = suffix + pltpu.roll(wide_total, Q - k * heads, 1)
        suffix = suffix[0:1, :]
        weight = dt * jnp.exp(jnp.minimum(total - cumul + suffix, 0.0))
        for chunk in range(chunks):
            lo = 8 + chunk * Q
            conv = taps[3:4, :] * window[lo : lo + Q, :conv_cols]
            for back in range(1, KERNEL):
                conv += taps[3 - back : 4 - back, :] * window[lo - back : lo - back + Q, :conv_cols]
            act = silu(conv)
            xc_out[lo - 8 : lo - 8 + Q, :] = act[:, :width].astype(BF16)
            bc_out[lo - 8 : lo - 8 + Q, :] = act[:, width:].astype(BF16)
            wide = widen(weight, heads, chunk, spread)
            scaled[lo - 8 : lo - 8 + Q, :] = (act[:, :width] * wide).astype(BF16)
        last_out[:, :width] = lax.dot_general(
            bc_out[:, :Q], scaled[...], (((0,), (0,)), ((), ())), preferred_element_type=F32
        ).astype(BF16)
        last_out[:, width:] = three_rows(jnp.broadcast_to(total + suffix, (Q, Q)))

    return kernel


def vmem_specs(count, scalars=1):
    return [pl.BlockSpec(memory_space=pltpu.SMEM)] * scalars + [
        pl.BlockSpec(memory_space=pltpu.VMEM)
    ] * count


def summarize(bias, rate, groups, halo, taps_x, taps_bc, heads, width, bc_cols):
    rows = 8 * Q
    return pl.pallas_call(
        summary_kernel(heads, rows // Q),
        in_specs=vmem_specs(7, 2),
        out_shape=[
            jax.ShapeDtypeStruct((rows, width), BF16),
            jax.ShapeDtypeStruct((rows, bc_cols), BF16),
            jax.ShapeDtypeStruct((Q, Q), F32),
            jax.ShapeDtypeStruct((Q, Q), F32),
            jax.ShapeDtypeStruct((Q, width + Q), BF16),
        ],
        scratch_shapes=[
            pltpu.VMEM((rows + 8, groups[0].shape[1]), F32),
            pltpu.VMEM((rows, width), BF16),
        ],
        cost_estimate=pl.CostEstimate(
            flops=3_000_000_000, bytes_accessed=8_000_000, transcendentals=1_000_000
        ),
        name="summarize",
    )(bias, rate, *groups, halo, taps_x, taps_bc)


def inside_kernel(heads, chunks):
    def kernel(
        skip, g0, g1, g2, g3, xc, bc, dt_in, cum_in,
        ig_out, fz_out, sloc_out, growth_out, gate, flipped, decays, state,
    ):
        width = xc.shape[1]
        pair = 2 * (width // heads)
        spread = spread_of(heads, width)
        starts = starts_of(chunks)
        for group, ref in enumerate((g0, g1, g2, g3)):
            for member in range(2):
                at = pl.multiple_of(starts[2 * group + member], Q)
                gate[pl.ds(at, Q), :] = ref[member * Q : member * Q + Q, :]
        row = lax.broadcasted_iota(jnp.int32, (Q, Q), 0)
        col = lax.broadcasted_iota(jnp.int32, (Q, Q), 1)
        lower = row >= col
        lane = lax.broadcasted_iota(jnp.int32, (Q, pair), 1)
        zero = jnp.zeros((Q, pair), BF16)
        cumul = cum_in[...]
        flipped[...] = cumul.T
        total = cumul[Q - 1 : Q, :]
        wide_total = jnp.broadcast_to(total, (8, Q))
        prefix = jnp.zeros((8, Q), F32)
        for k in range(1, chunks):
            prefix = prefix + pltpu.roll(wide_total, k * heads, 1)
        grown = jnp.exp(prefix)
        decay = jnp.exp(wide_total)
        rows8 = lax.broadcasted_iota(jnp.int32, (8, Q), 0)
        grown_rows = jnp.zeros((8, Q), F32)
        decay_rows = jnp.zeros((8, Q), F32)
        for chunk in range(chunks):
            turn = -chunk * heads % Q
            grown_rows = jnp.where(
                rows8 == chunk, pltpu.roll(grown, turn, 1) if turn else grown, grown_rows
            )
            decay_rows = jnp.where(
                rows8 == chunk, pltpu.roll(decay, turn, 1) if turn else decay, decay_rows
            )
        growth_out[...] = widen(grown_rows, heads, 0, spread)
        decays[...] = widen(decay_rows, heads, 0, spread)
        state[...] = jnp.zeros((Q, width), F32)

        @pl.loop(0, chunks)
        def _(chunk):
            at = pl.ds(pl.multiple_of(chunk * Q, Q), Q)
            turn = lax.rem(Q - chunk * heads, Q)
            dt = pltpu.roll(dt_in[...], turn, 1)
            cumul = pltpu.roll(cum_in[...], turn, 1)
            rows = flipped[pl.ds(pl.multiple_of(chunk * heads, heads), heads), :]
            b_rows = bc[at, :Q]
            c_rows = bc[at, Q:]
            x = xc[at, :].astype(F32)
            sloc_out[chunk] = state[...].astype(BF16)
            weight = dt * jnp.exp(jnp.minimum(cumul[Q - 1 : Q, :] - cumul, 0.0))
            kept = (x * widen(weight, heads, 0, spread)).astype(BF16)
            fresh = lax.dot_general(
                b_rows, kept, (((0,), (0,)), ((), ())), preferred_element_type=F32
            )
            state[...] = decays[pl.ds(chunk, 1), :] * state[...] + fresh
            scores = lax.dot_general(
                c_rows, b_rows, (((1,), (1,)), ((), ())), preferred_element_type=F32
            )
            scores = jnp.where(lower, scores, 0.0)
            scaled = (x * widen(dt, heads, 0, spread)).astype(BF16)
            act = silu(gate[at, :])
            fz_out[at, :] = (widen(jnp.exp(cumul), heads, 0, spread) * act).astype(BF16)
            for first in range(0, heads, 2):
                parts = []
                for head in (first, first + 1):
                    gap = cumul[:, head : head + 1] - rows[head : head + 1, :]
                    parts.append((scores * jnp.exp(jnp.minimum(gap, 0.0))).astype(BF16))
                lo = (first // 2) * pair
                block = scaled[:, lo : lo + pair]
                stacked = jnp.concatenate(
                    [
                        jnp.where(lane < pair // 2, block, zero),
                        jnp.where(lane < pair // 2, zero, block),
                    ],
                    axis=0,
                )
                out = jnp.dot(
                    jnp.concatenate(parts, axis=1), stacked, preferred_element_type=F32
                )
                coefficient = jnp.where(lane < pair // 2, skip[first], skip[first + 1])
                out = out + coefficient * x[:, lo : lo + pair]
                ig_out[at, lo : lo + pair] = (out * act[:, lo : lo + pair]).astype(BF16)

    return kernel


def inside(skip, groups, xc, bc, dt, cumul, heads):
    rows, width = xc.shape
    chunks = rows // Q
    return pl.pallas_call(
        inside_kernel(heads, chunks),
        in_specs=vmem_specs(8),
        out_shape=[
            jax.ShapeDtypeStruct((rows, width), BF16),
            jax.ShapeDtypeStruct((rows, width), BF16),
            jax.ShapeDtypeStruct((chunks, Q, width), BF16),
            jax.ShapeDtypeStruct((8, width), F32),
        ],
        scratch_shapes=[
            pltpu.VMEM((rows, width), F32),
            pltpu.VMEM((Q, Q), F32),
            pltpu.VMEM((8, width), F32),
            pltpu.VMEM((Q, width), F32),
        ],
        cost_estimate=pl.CostEstimate(
            flops=8_000_000_000, bytes_accessed=8_000_000, transcendentals=2_000_000
        ),
        name="inside",
    )(skip, *groups, xc, bc, dt, cumul)


def finish_kernel(sel, c_rows, ig, fz, sloc, growth, entering, out):
    start = entering[...].astype(F32)
    first = 2 * pl.program_id(0)
    for i in range(2):
        chunk = 2 * (first + i) + sel[0]
        state = sloc[i, 0].astype(F32) + growth[pl.ds(chunk, 1), :] * start
        carried = jnp.dot(c_rows[i, 0], state.astype(BF16), preferred_element_type=F32)
        out[i * Q : i * Q + Q, :] = (
            ig[i, 0].astype(F32) + carried * fz[i, 0].astype(F32)
        ).astype(BF16)


def finish(sel, bc, ig, fz, sloc, growth, entering):
    rows, width = ig.shape
    pairs = rows // Q // 2
    paired = lambda block: block.reshape(pairs, 2, Q, -1)
    block = pl.BlockSpec((2, 1, Q, width), lambda i, sel: (i, sel[0], 0, 0))
    return pl.pallas_call(
        finish_kernel,
        grid_spec=pltpu.PrefetchScalarGridSpec(
            num_scalar_prefetch=1,
            grid=(pairs // 2,),
            in_specs=[
                pl.BlockSpec((2, 1, Q, Q), lambda i, sel: (i, sel[0], 0, 1)),
                block,
                block,
                block,
                pl.BlockSpec(growth.shape, lambda i, sel: (0, 0)),
                pl.BlockSpec(entering.shape, lambda i, sel: (0, 0)),
            ],
            out_specs=pl.BlockSpec((2 * Q, width), lambda i, sel: (i, 0)),
        ),
        out_shape=jax.ShapeDtypeStruct((rows // 2, width), BF16),
        cost_estimate=pl.CostEstimate(
            flops=1_500_000_000, bytes_accessed=3_000_000, transcendentals=0
        ),
        name="finish",
    )(sel, paired(bc), paired(ig), paired(fz), paired(sloc), growth, entering)


def row_kernel(heads):
    def kernel(pieces, before_out, growth_out, row_out):
        width = before_out.shape[2]
        spread = spread_of(heads, width)
        count = pieces.shape[0]
        rows8 = lax.broadcasted_iota(jnp.int32, (8, Q), 0)
        parts = jnp.zeros((8, Q), F32)
        sums = jnp.zeros((8, Q), F32)
        total = jnp.zeros((1, Q), F32)
        for k in range(count):
            tail = pieces[k, :, width:].astype(F32)
            part = tail[0:1] + tail[1:2] + tail[2:3]
            parts = jnp.where(rows8 == k, part, parts)
            sums = jnp.where(rows8 == k, total, sums)
            total = total + part
        growth_out[...] = widen(jnp.exp(sums), heads, 0, spread)
        decay = widen(jnp.exp(parts), heads, 0, spread)
        state = jnp.zeros(before_out.shape[1:], F32)
        for k in range(count):
            before_out[k] = state
            state = decay[k : k + 1] * state + pieces[k, :, :width].astype(F32)
        row_out[:, :width] = state.astype(BF16)
        row_out[:, width:] = three_rows(jnp.broadcast_to(total, (16, Q)))

    return kernel


def row_scan(pieces, heads):
    count, rows, cols = pieces.shape
    width = cols - Q
    return pl.pallas_call(
        row_kernel(heads),
        in_specs=vmem_specs(1, 0),
        out_shape=[
            jax.ShapeDtypeStruct((count, rows, width), F32),
            jax.ShapeDtypeStruct((8, width), F32),
            jax.ShapeDtypeStruct((rows, cols), BF16),
        ],
        name="row_scan",
    )(pieces)


def join_kernel(heads):
    def kernel(near, middle, far, before, growth, out):
        width = out.shape[2]
        spread = spread_of(heads, width)

        def log_of(piece):
            tail = piece[:, width:].astype(F32)
            return tail[0:1] + tail[1:2] + tail[2:3]

        rows8 = lax.broadcasted_iota(jnp.int32, (8, Q), 0)
        logs = jnp.where(rows8 == 0, log_of(near), log_of(middle))
        decay = widen(jnp.exp(logs), heads, 0, spread)
        entering = far[:, :width].astype(F32)
        entering = decay[1:2] * entering + middle[:, :width].astype(F32)
        entering = decay[0:1] * entering + near[:, :width].astype(F32)
        for k in range(out.shape[0]):
            out[k] = (before[k] + growth[k : k + 1] * entering).astype(BF16)

    return kernel


def join_rows(near, middle, far, before, growth, heads):
    count, rows, width = before.shape
    return pl.pallas_call(
        join_kernel(heads),
        in_specs=vmem_specs(5, 0),
        out_shape=jax.ShapeDtypeStruct((count, rows, width), BF16),
        name="join_rows",
    )(near, middle, far, before, growth)


def per_device(
    tokens, w_in_x, w_in_z, w_in_bc, w_dt, conv_x, conv_bc,
    dt_bias, decay_rate, skip, norm_gain, w_out,
):
    width = w_in_x.shape[1]
    heads = dt_bias.shape[0]
    bc_cols = w_in_bc.shape[1]
    own_rows, d_model = tokens.shape
    half = own_rows // 2
    x_size = lax.axis_size("x")
    x_at = lax.axis_index("x")
    c_at = lax.axis_index("c")
    swap = lambda block: shift(block, "c", 1)

    top, bottom = tokens[:half], tokens[half:]

    def named(block, distance, axis="x"):
        return shift(block, axis, distance)

    left_top = named(top, 1)
    right_bottom = named(bottom, -1)
    left_bottom = named(bottom, 1)
    right_top = named(top, -1)
    far_top = named(left_top, 1)
    far_bottom = named(right_bottom, -1)

    w_first = jnp.concatenate(
        [w_in_x, w_in_bc, w_dt, jnp.zeros((d_model, Q - heads), BF16)], axis=1
    )
    groups = (
        (0, (tokens, swap(tokens))),
        (
            -1,
            (
                left_top,
                left_bottom,
                named(left_top, 1, "c"),
                named(left_bottom, 1, "c"),
            ),
        ),
        (
            1,
            (
                right_top,
                right_bottom,
                named(right_top, 1, "c"),
                named(right_bottom, 1, "c"),
            ),
        ),
        (2, (far_top, far_bottom, swap(far_top), swap(far_bottom))),
    )
    conv_cols = width + bc_cols
    pairs, firsts = [], []
    edge = jnp.zeros((8, conv_cols), F32)
    for distance, blocks in groups:
        pair = jnp.concatenate(blocks, axis=0)
        first = jnp.dot(pair, w_first, preferred_element_type=F32)
        ends = [first[m * Q + Q - 8 : m * Q + Q, :conv_cols] for m in range(2)]
        is_last = (x_at + distance) % x_size == x_size - 1
        edge = jnp.where(is_last, jnp.where(c_at == 1, ends[0], ends[1]), edge)
        pairs.append(pair)
        firsts.append(first)
    halo = later(edge, SEQ, 1)
    xc, bc, dt, cumul, last = summarize(
        dt_bias, decay_rate, firsts, halo, conv_x, conv_bc, heads, width, bc_cols
    )
    pairs[3], w_out, last = lax.optimization_barrier((pairs[3], w_out, last))
    z_size = lax.axis_size("z")
    pieces = lax.all_to_all(
        last.reshape(z_size, Q // z_size, width + Q), "z", 0, 0, tiled=True
    )
    seconds = [jnp.dot(pair, w_in_z, preferred_element_type=F32) for pair in pairs]
    d_half = d_model // 2
    own_low, own_high = [
        (part.astype(F32) * norm_gain[:, None]).astype(BF16)
        for part in (w_out[:, :d_half], w_out[:, d_half:])
    ]
    w_low = (own_low, swap(own_low))
    w_high = (own_high, swap(own_high))
    ig, fz, sloc, growth = inside(skip, seconds, xc, bc, dt, cumul, heads)
    before, row_growth, row_total = row_scan(pieces, heads)
    near = later(row_total, "y", 1)
    middle = later(row_total, "y", 2)
    far = later(row_total, "y", 3)
    joined = join_rows(near, middle, far, before, row_growth, heads)
    entering = lax.all_to_all(joined, "z", 0, 0, tiled=True).reshape(Q, width)

    core = c_at.astype(jnp.int32)[None]
    away = finish(1 - core, bc, ig, fz, sloc, growth, entering)
    arrived = swap(away)
    kept = finish(core, bc, ig, fz, sloc, growth, entering)
    both = [block.reshape(x_size, own_rows, width) for block in (kept, arrived)]

    def partial(distance, weights, added=None):
        at = (x_at + distance) % x_size
        blocks = [lax.dynamic_index_in_dim(part, at, 0, keepdims=False) for part in both]
        result = sum(
            jnp.dot(block, weight, preferred_element_type=F32)
            for block, weight in zip(blocks, weights)
        )
        if added is not None:
            result = result + added.astype(F32)
        return result

    def sent(distance, weights, way, added=None):
        part = partial(distance, weights, added).astype(BF16)
        return named(part, way)

    far_low = sent(2, w_low, 1)
    far_high = sent(2, w_high, -1)
    right_high = sent(1, w_high, 1)
    left_low = sent(-1, w_low, -1)
    squares = sum(jnp.sum(jnp.square(part.astype(F32)), axis=2) for part in both)
    squares = lax.all_to_all(squares, "x", 0, 0, tiled=True)
    right_low = sent(1, w_low, 1, far_low)
    left_high = sent(-1, w_high, -1, far_high)
    low = partial(0, w_low)
    high = partial(0, w_high)
    return close(squares, low, high, right_low, left_low, right_high, left_high)


def close_kernel(squares, low, high, right_low, left_low, right_high, left_high, out):
    rows, half = low.shape
    total = jnp.sum(squares[...], axis=0, keepdims=True)
    scale = lax.rsqrt(jnp.broadcast_to(total, (rows, rows)).T / E + 1e-05)
    sides = ((low, right_low, left_low), (high, right_high, left_high))
    for side, (own, first, second) in enumerate(sides):
        for lo in range(0, half, rows):
            at = slice(lo, lo + rows)
            value = own[:, at] + first[:, at].astype(F32) + second[:, at].astype(F32)
            out[:, side * half + lo : side * half + lo + rows] = (value * scale).astype(BF16)


def close(squares, low, high, *parts):
    return pl.pallas_call(
        close_kernel,
        in_specs=vmem_specs(7, 0),
        out_shape=jax.ShapeDtypeStruct((low.shape[0], 2 * low.shape[1]), BF16),
        name="close",
    )(squares, low, high, *parts)


def solution(mesh):
    torus = Mesh(mesh.devices.reshape(4, 8, 4, 2), ALL)
    head = ("x", "c")
    placed = (
        P(ALL, None),
        P(None, head),
        P(None, head),
        P(),
        P(None, head),
        P(None, head),
        P(),
        P(head),
        P(head),
        P(head),
        P(head),
        P(head, None),
    )
    return jax.shard_map(
        per_device, mesh=torus, in_specs=placed, out_specs=P(ALL, None), check_vma=False
    )
```

time: 305 us -> 162 us (0.53)
  waiting for transfers between devices: 115 us -> 23.6 us
  local copies, waits for them, and re-layouts: 75.1 us -> 11.1 us
  starting transfers between devices: 7.17 us -> 44.7 us
  blocking collectives: 33.1 us -> 0 us
  Pallas kernels: 0 us -> 27.9 us
  between operations: 14 us -> 0.49 us
  matrix products: 48.5 us -> 44.2 us
    all_gather x3 -> x0, waiting for transfers between devices: 72.3 us -> none  [the longest x1 37.6 us: per_device(): block_rows = lax.all_gather(tokens, 'head', axis=0, tiled=True)]
    dynamic_update_slice x8 -> x0, local copies, waits for them, and re-layouts: 51.4 us -> none  [per_device(): lax.scan(advance, (empty_state, empty_decay), (x_conv.reshape(spans, SPAN...]
    reduce_scatter x1 -> x0, waiting for transfers between devices: 40.4 us -> none  [per_device(): lax.psum_scatter(jnp.dot(normed, w_out, preferred_element_type=jnp.float3...]
    pallas_call x0 -> x7, Pallas kernels: none -> 27.9 us  [the longest x1 10.1 us: inside(): pl.pallas_call(inside_kernel(heads, chunks), in_specs=vmem_specs(8), out_...]
    ppermute x2 -> x26, starting transfers between devices: 7.05 us -> 32 us  [the longest x22 20.7 us: shift(): lax.ppermute(block, axis, [(i, (i + distance) % size) for i in range(size)])]
    unnamed x1 -> x0, blocking collectives: 15.8 us -> none
    ppermute x2 -> x26, waiting for transfers between devices: 1.24 us -> 15.7 us  [the longest x22 11.1 us: shift(): lax.ppermute(block, axis, [(i, (i + distance) % size) for i in range(size)])]
    all_to_all x0 -> x3, starting transfers between devices: none -> 12.8 us  [the longest x1 6.07 us: per_device(): lax.all_to_all(last.reshape(z_size, Q // z_size, width + Q), 'z', 0, 0, t...]
  transfers between devices with their start and end apart: 6 -> 29, of which waited for: 5 -> 10; matrix products, arithmetic and copies ran while one was open for 4% -> 35% of each run, Pallas kernels for 0% -> 11%
where the time goes in v1:
time: 162 us; the launch traced here: 159 us
  starting transfers between devices  44.7 us (28%)
  matrix products  44.2 us (27%)
  Pallas kernels  27.9 us (17%)
  waiting for transfers between devices  23.6 us (15%)
  local copies, waits for them, and re-layouts  11.1 us (7%)
  other arithmetic  7.49 us (5%)
    dot_general x16, matrix products, partial(): jnp.dot(block, weight, preferred_element_type=F32)  32.9 us
    ppermute x22, starting transfers between devices, shift(): lax.ppermute(block, axis, [(i, (i + distance) % size) for i in range(size)])  20.7 us
    ppermute x4, starting transfers between devices, later(): lax.ppermute(block, axis, [(i, i + distance) for i in range(size - distan...  11.2 us
    ppermute x22, waiting for transfers between devices, shift(): lax.ppermute(block, axis, [(i, (i + distance) % size) for i in range(size)])  11.1 us
    pallas_call x1, Pallas kernels, inside(): pl.pallas_call(inside_kernel(heads, chunks), in_specs=vmem_specs(8), out_...  10.1 us
    all_to_all x1, waiting for transfers between devices, per_device(): lax.all_to_all(last.reshape(z_size, Q // z_size, width + Q), 'z', 0, 0, t...  7.92 us
    unnamed x69, local copies, waits for them, and re-layouts  7.51 us
    pallas_call x1, Pallas kernels, summarize(): pl.pallas_call(summary_kernel(heads, rows // Q), in_specs=vmem_specs(7, 2...  6.5 us
  transfers between devices with their start and end apart: 29, of which 10 were waited for; matrix products, arithmetic and copies ran while one was open for 35% of the time, Pallas kernels for 11%

profile of v1, /device:TPU:8, one launch (start us, length us, event | category | flops | bytes accessed | tf_op | source)
XLA Modules:
  0.0 159.5 jit_solution(7266005815312658039)
XLA Ops:
  0.0 2.0 %fusion.68 = (bf16[64,2048]{1,0:T(8,128)(2,1)}, bf16[64,2048]{1,0:T(8,128)(2,1)}) fusion(bf16[128,2048]{1,0:T(8,128)(2,1)} %param.12), kind=kLoop, calls=%fused_computation.99 | loop fusion | bytes 1048576 | tf_op jit(solution)/shard_map/slice | solution.py:412
  2.0 2.8 %collective-permute-start.6 = (bf16[64,2048]{1,0:T(8,128)(2,1)}, bf16[64,2048]{1,0:T(8,128)(2,1)S(1)}, u32[]{:S(2)}, u32[]{:S(2)}) collective-permute-start(bf16[64,2048]{1,0:T(8,128)(2,1)} %get-tuple-element.37), channel_id=1, source_target_pairs={{0,6},{2,0},{4,2},{6,4},{1,7},{3,1},{5,3},{7,5},{8,14},{10,8},{12,... | collective-permute-start | bytes 786440 | tf_op jit(solution)/shard_map/ppermute | solution.py:27
  4.8 3.2 %collective-permute-start.5 = (bf16[64,2048]{1,0:T(8,128)(2,1)}, bf16[64,2048]{1,0:T(8,128)(2,1)}, u32[]{:S(2)}, u32[]{:S(2)}) collective-permute-start(bf16[64,2048]{1,0:T(8,128)(2,1)} %get-tuple-element.38), channel_id=1, source_target_pairs={{0,6},{2,0},{4,2},{6,4},{1,7},{3,1},{5,3},{7,5},{8,14},{10,8},{12,... | collective-permute-start | bytes 786440 | tf_op jit(solution)/shard_map/ppermute | solution.py:27
  8.0 1.0 copy.14
  9.2 3.6 %maximum_maximum_fusion = bf16[2048,896]{1,0:T(8,128)(2,1)} fusion(bf16[2048,8]{1,0:T(8,128)(2,1)S(1)} %copy.14, bf16[2048,256]{1,0:T(8,128)(2,1)} %param.15, bf16[2048,512]{1,0:T(8,128)(2,1)} %param.13, bf16[896]{0:T(1024)(128)(2,1)S(1)} %pad.3.clone), kind=kLoop, calls=%fused_computation | loop fusion | flops 14680064 | bytes 6850304 | tf_op jit(solution)/shard_map/concatenate | solution.py:424
  12.8 3.3 %collective-permute-start.10 = (bf16[64,2048]{1,0:T(8,128)(2,1)S(1)}, bf16[64,2048]{1,0:T(8,128)(2,1)S(1)}, u32[]{:S(2)}, u32[]{:S(2)}) collective-permute-start(bf16[64,2048]{1,0:T(8,128)(2,1)S(1)} %collective-permute-done.6), channel_id=1, source_target_pairs={{0,6},{2,0},{4,2},{6,4},{1,7},{3,1},{5,3},{7,5},{8,14},{10,8},{12,... | collective-permute-start | bytes 786440 | tf_op jit(solution)/shard_map/ppermute | solution.py:27
  16.4 3.3 %collective-permute-done.1 = bf16[64,2048]{1,0:T(8,128)(2,1)} collective-permute-done((bf16[64,2048]{1,0:T(8,128)(2,1)}, bf16[64,2048]{1,0:T(8,128)(2,1)}, u32[]{:S(2)}, u32[]{:S(2)}) %collective-permute-start.1) | collective-permute-done | bytes 262176 | tf_op jit(solution)/shard_map/ppermute | solution.py:27
  19.7 1.0 constant_dynamic-update-slice_fusion.5
  20.7 1.0 constant_dynamic-update-slice_fusion.4
  22.2 1.0 constant_dynamic-update-slice_fusion.9
  24.3 1.3 fusion.70.g1
  25.6 1.6 %fusion.74.g1 = f32[256,512]{1,0:T(8,128)} fusion(bf16[256,2048]{1,0:T(8,128)(2,1)S(1)} %constant_dynamic-update-slice_fusion.2, bf16[2048,512]{1,0:T(8,128)(2,1)S(1)} %copy-done), kind=kOutput, calls=%fused_computation.105 | convolution fusion | flops 536870912 | bytes 3670016 | tf_op jit(solution)/shard_map/dot_general | solution.py:469
  27.3 1.3 fusion.71.g2
  28.6 1.4 constant_dynamic-update-slice_fusion
  30.0 1.3 fusion.69.g0
  31.3 1.6 %fusion.75.g2 = f32[256,512]{1,0:T(8,128)} fusion(bf16[256,2048]{1,0:T(8,128)(2,1)S(1)} %constant_dynamic-update-slice_fusion.6, bf16[2048,512]{1,0:T(8,128)(2,1)S(1)} %copy-done), kind=kOutput, calls=%fused_computation.106 | convolution fusion | flops 536870912 | bytes 3670016 | tf_op jit(solution)/shard_map/dot_general | solution.py:469
  32.9 1.2 collective-permute-done.9
  34.7 0.9 collective-permute-done.11
  36.0 1.3 fusion.72.g3
  37.3 3.8 %collective-permute-start.13 = (f32[8,768]{1,0:T(8,128)S(1)}, f32[8,768]{1,0:T(8,128)S(1)}, u32[]{:S(2)}, u32[]{:S(2)}) collective-permute-start(f32[8,768]{1,0:T(8,128)S(1)} %fusion.51), channel_id=1, source_target_pairs={{0,8},{8,16},{16,24},{24,32},{32,40},{40,48},{48,56},{56,64},{64,7... | collective-permute-start | bytes 73736 | tf_op jit(solution)/shard_map/ppermute | solution.py:32
  41.2 1.5 fusion.73.g0
  42.7 4.1 %collective-permute-done.13.halo = f32[8,768]{1,0:T(8,128)S(1)} collective-permute-done((f32[8,768]{1,0:T(8,128)S(1)}, f32[8,768]{1,0:T(8,128)S(1)}, u32[]{:S(2)}, u32[]{:S(2)}) %collective-permute-start.13) | collective-permute-done | bytes 24608 | tf_op jit(solution)/shard_map/ppermute | solution.py:32
  47.4 6.5 %summarize.1 = (bf16[1024,512]{1,0:T(8,128)(2,1)}, bf16[1024,256]{1,0:T(8,128)(2,1)}, f32[128,128]{1,0:T(8,128)}, f32[128,128]{1,0:T(8,128)}, bf16[128,640]{1,0:T(8,128)(2,1)}) custom-call(f32[8]{0:T(128)} %bias.1, f32[8]{0:T(128)} %rate.1, f32[256,896]{1,0:T(8,128)} %copy-done.25, f32[256,896]{1,0:T(8,128)} %copy-done.23, f32[256,896]{1,0:T(8,128)} %copy-done.24, ...), custom_call_target="tpu_custom_call" | custom-call | flops 3000000000 | bytes 8000000 | tf_op jit(solution)/shard_map/summarize/pallas_call | solution.py:149
  53.9 6.1 %all-to-all-start = ((bf16[8,16,640]{2,1,0:T(8,128)(2,1)}), bf16[8,16,640]{2,1,0:T(8,128)(2,1)S(1)}, u32[]{:S(2)}, u32[]{:S(2)}) async-start(bf16[8,16,640]{2,1,0:T(8,128)(2,1)} %bitcast.99), calls=%async_computation | async-start | bytes 327680 | tf_op jit(solution)/shard_map/all_to_all | solution.py:466
  60.0 1.5 fusion.76.g3
  61.5 7.9 %all-to-all-done.pieces = bf16[8,16,640]{2,1,0:T(8,128)(2,1)S(1)} async-done(((bf16[8,16,640]{2,1,0:T(8,128)(2,1)}), bf16[8,16,640]{2,1,0:T(8,128)(2,1)S(1)}, u32[]{:S(2)}, u32[]{:S(2)}) %all-to-all-start) | async-done | bytes 163872 | tf_op jit(solution)/shard_map/all_to_all | solution.py:466
  69.4 0.7 copy-done.12
  70.1 1.9 %row_scan.1 = (f32[8,16,512]{2,1,0:T(8,128)}, f32[8,512]{1,0:T(8,128)}, bf16[16,640]{1,0:T(8,128)(2,1)}) custom-call(bf16[8,16,640]{2,1,0:T(8,128)(2,1)} %copy-done.12), custom_call_target="tpu_custom_call" | custom-call | tf_op jit(solution)/shard_map/row_scan/pallas_call | solution.py:355
  71.9 0.7 collective-permute-start.16
  72.6 4.8 %collective-permute-start.15 = (bf16[16,640]{1,0:T(8,128)(2,1)}, bf16[16,640]{1,0:T(8,128)(2,1)S(1)}, u32[]{:S(2)}, u32[]{:S(2)}) collective-permute-start(bf16[16,640]{1,0:T(8,128)(2,1)} %get-tuple-element.31), channel_id=1, source_target_pairs={{0,128},{64,192},{1,129},{65,193},{2,130},{66,194},{3,131},{67,195... | collective-permute-start | bytes 61448 | tf_op jit(solution)/shard_map/ppermute | solution.py:32
  77.4 1.9 %collective-permute-start.14 = (bf16[16,640]{1,0:T(8,128)(2,1)}, bf16[16,640]{1,0:T(8,128)(2,1)S(1)}, u32[]{:S(2)}, u32[]{:S(2)}) collective-permute-start(bf16[16,640]{1,0:T(8,128)(2,1)} %get-tuple-element.31), channel_id=1, source_target_pairs={{0,64},{64,128},{128,192},{1,65},{65,129},{129,193},{2,66},{66,130... | collective-permute-start | bytes 61448 | tf_op jit(solution)/shard_map/ppermute | solution.py:32
  79.4 2.9 %multiply_convert_fusion = (bf16[512,1024]{1,0:T(8,128)(2,1)}, bf16[512,1024]{1,0:T(8,128)(2,1)S(1)}) fusion(bf16[512,2048]{1,0:T(8,128)(2,1)} %param.23, f32[512]{0:T(512)S(1)} %copy-done.27), kind=kLoop, calls=%fused_computation.1 | loop fusion | flops 3145728 | bytes 4196352 | tf_op jit(solution)/shard_map/convert_element_type | solution.py:472
  83.9 1.8 %join_rows.1 = bf16[8,16,512]{2,1,0:T(8,128)(2,1)} custom-call(bf16[16,640]{1,0:T(8,128)(2,1)} %copy-done.21, bf16[16,640]{1,0:T(8,128)(2,1)} %copy-done.20, bf16[16,640]{1,0:T(8,128)(2,1)} %copy-done.19, f32[8,16,512]{2,1,0:T(8,128)} %get-tuple-element.32.before, f32[8,512]{1,0:T(8,128)} %get-tuple-element.33.growth), custom_call_target="tpu_custom_call" | custom-call | tf_op jit(solution)/shard_map/join_rows/pallas_call | solution.py:390
  85.8 3.4 %all-to-all-start.1 = ((bf16[8,16,512]{2,1,0:T(8,128)(2,1)}), bf16[8,16,512]{2,1,0:T(8,128)(2,1)S(1)}, u32[]{:S(2)}, u32[]{:S(2)}) async-start(bf16[8,16,512]{2,1,0:T(8,128)(2,1)} %join_rows.1), calls=%async_computation.1 | async-start | bytes 262144 | tf_op jit(solution)/shard_map/all_to_all | solution.py:483
  89.1 10.1 %inside.1 = (bf16[1024,512]{1,0:T(8,128)(2,1)}, bf16[1024,512]{1,0:T(8,128)(2,1)}, bf16[8,128,512]{2,1,0:T(8,128)(2,1)}, f32[8,512]{1,0:T(8,128)}) custom-call(f32[8]{0:T(128)} %skip.1, f32[256,512]{1,0:T(8,128)} %fusion.73.g0, f32[256,512]{1,0:T(8,128)} %fusion.74.g1, f32[256,512]{1,0:T(8,128)} %fusion.75.g2, f32[256,512]{1,0:T(8,128)} %fusion.76.g3, ...), custom_call_target="tpu_custom_call" | custom-call | flops 8000000000 | bytes 8000000 | tf_op jit(solution)/shard_map/inside/pallas_call | solution.py:263
  100.0 2.5 %finish.2 = bf16[512,512]{1,0:T(8,128)(2,1)} custom-call(s32[1]{0:T(128)} %bitcast.sel, bf16[4,2,128,256]{3,2,1,0:T(8,128)(2,1)} %bitcast.109, bf16[4,2,128,512]{3,2,1,0:T(8,128)(2,1)} %bitcast.103, bf16[4,2,128,512]{3,2,1,0:T(8,128)(2,1)} %bitcast.105, bf16[4,2,128,512]{3,2,1,0:T(8,128)(2,1)} %bitcast.107, f32[8,512]{1,0:T(8,128)} %get-tuple-element.29.growth, ...), custom_call_target="tpu_custom_call" | custom-call | flops 1500000000 | bytes 3000000 | tf_op jit(solution)/shard_map/finish/pallas_call | solution.py:302
  102.4 2.4 %fusion.10 = f32[128,1024]{1,0:T(8,128)} fusion(bf16[512,1024]{1,0:T(8,128)(2,1)} %get-tuple-element.35, bf16[4,128,512]{2,1,0:T(8,128)(2,1)} %bitcast.91, s32[]{:T(128)S(6)} %select_n.124), kind=kOutput, calls=%fused_computation.23 | convolution fusion | flops 134217728 | bytes 1703940 | tf_op jit(solution)/shard_map/dot_general | solution.py:495
  104.8 2.0 %fusion.12 = f32[128,1024]{1,0:T(8,128)} fusion(bf16[512,1024]{1,0:T(8,128)(2,1)S(1)} %get-tuple-element.36, bf16[4,128,512]{2,1,0:T(8,128)(2,1)} %bitcast.92, s32[]{:T(128)S(6)} %select_n.124), kind=kOutput, calls=%fused_computation.25 | convolution fusion | flops 134217728 | bytes 1703940 | tf_op jit(solution)/shard_map/dot_general | solution.py:495
  106.8 2.5 %fusion.16 = f32[128,1024]{1,0:T(8,128)} fusion(bf16[512,1024]{1,0:T(8,128)(2,1)} %get-tuple-element.35, bf16[4,128,512]{2,1,0:T(8,128)(2,1)} %bitcast.93, s32[]{:T(128)S(6)} %select_n.123), kind=kOutput, calls=%fused_computation.29 | convolution fusion | flops 134217728 | bytes 1703940 | tf_op jit(solution)/shard_map/dot_general | solution.py:495
  109.3 2.1 %fusion.18 = f32[128,1024]{1,0:T(8,128)} fusion(bf16[512,1024]{1,0:T(8,128)(2,1)S(1)} %get-tuple-element.36, bf16[4,128,512]{2,1,0:T(8,128)(2,1)} %bitcast.94, s32[]{:T(128)S(6)} %select_n.123), kind=kOutput, calls=%fused_computation.31 | convolution fusion | flops 134217728 | bytes 1703940 | tf_op jit(solution)/shard_map/dot_general | solution.py:495
  111.4 2.5 %finish.3 = bf16[512,512]{1,0:T(8,128)(2,1)} custom-call(s32[1]{0:T(128)S(6)} %sub.3.sel, bf16[4,2,128,256]{3,2,1,0:T(8,128)(2,1)} %bitcast.110, bf16[4,2,128,512]{3,2,1,0:T(8,128)(2,1)} %bitcast.104, bf16[4,2,128,512]{3,2,1,0:T(8,128)(2,1)} %bitcast.106, bf16[4,2,128,512]{3,2,1,0:T(8,128)(2,1)} %bitcast.108, f32[8,512]{1,0:T(8,128)} %get-tuple-element.29.growth, ...), custom_call_target="tpu_custom_call" | custom-call | flops 1500000000 | bytes 3000000 | tf_op jit(solution)/shard_map/finish/pallas_call | solution.py:302
  113.9 2.5 %fusion.22 = f32[128,1024]{1,0:T(8,128)} fusion(bf16[512,1024]{1,0:T(8,128)(2,1)} %get-tuple-element.35, bf16[4,128,512]{2,1,0:T(8,128)(2,1)} %bitcast.95, s32[]{:T(128)S(6)} %select_n.122), kind=kOutput, calls=%fused_computation.35 | convolution fusion | flops 134217728 | bytes 1703940 | tf_op jit(solution)/shard_map/dot_general | solution.py:495
  116.4 2.0 %fusion.24 = f32[128,1024]{1,0:T(8,128)} fusion(bf16[512,1024]{1,0:T(8,128)(2,1)S(1)} %get-tuple-element.36, bf16[4,128,512]{2,1,0:T(8,128)(2,1)} %bitcast.96, s32[]{:T(128)S(6)} %select_n.122), kind=kOutput, calls=%fused_computation.37 | convolution fusion | flops 134217728 | bytes 1703940 | tf_op jit(solution)/shard_map/dot_general | solution.py:495
  118.4 2.4 %fusion.28 = f32[128,1024]{1,0:T(8,128)} fusion(bf16[512,1024]{1,0:T(8,128)(2,1)} %get-tuple-element.35, bf16[4,128,512]{2,1,0:T(8,128)(2,1)} %bitcast.97, s32[]{:T(128)S(6)} %select_n.121), kind=kOutput, calls=%fused_computation.41 | convolution fusion | flops 134217728 | bytes 1703940 | tf_op jit(solution)/shard_map/dot_general | solution.py:495
  121.0 1.1 fusion.30
  122.1 0.8 copy-done.1
  123.7 3.3 %all-to-all-start.2 = ((f32[4,1,128]{2,1,0:T(1,128)}), f32[4,1,128]{2,1,0:T(1,128)S(1)}, u32[]{:S(2)}, u32[]{:S(2)}) async-start(f32[4,1,128]{2,1,0:T(1,128)} %bitcast.7), calls=%async_computation.2 | async-start | bytes 4096 | tf_op jit(solution)/shard_map/all_to_all | solution.py:511
  127.1 2.6 %fusion.6 = bf16[128,1024]{1,0:T(8,128)(2,1)} fusion(f32[128,1024]{1,0:T(8,128)} %fusion.22, bf16[512,1024]{1,0:T(8,128)(2,1)} %collective-permute-done.19, bf16[4,128,512]{2,1,0:T(8,128)(2,1)} %bitcast.83, s32[]{:T(128)S(6)} %select_n.122), kind=kOutput, calls=%fused_computation.17 | convolution fusion | flops 134479872 | bytes 1966084 | tf_op jit(solution)/shard_map/dot_general | solution.py:495
  129.7 2.0 %collective-permute-start.23 = (bf16[128,1024]{1,0:T(8,128)(2,1)}, bf16[128,1024]{1,0:T(8,128)(2,1)S(1)}, u32[]{:S(2)}, u32[]{:S(2)}) collective-permute-start(bf16[128,1024]{1,0:T(8,128)(2,1)} %fusion.6), channel_id=1, source_target_pairs={{0,2},{2,4},{4,6},{6,0},{1,3},{3,5},{5,7},{7,1},{8,10},{10,12},{12... | collective-permute-start | bytes 786440 | tf_op jit(solution)/shard_map/ppermute | solution.py:27
  131.7 1.7 %fusion.7 = bf16[128,1024]{1,0:T(8,128)(2,1)S(1)} fusion(f32[128,1024]{1,0:T(8,128)} %fusion.16, bf16[512,1024]{1,0:T(8,128)(2,1)} %collective-permute-done.19, bf16[4,128,512]{2,1,0:T(8,128)(2,1)} %bitcast.84, s32[]{:T(128)S(6)} %select_n.123), kind=kOutput, calls=%fused_computation.18 | convolution fusion | flops 134479872 | bytes 1966084 | tf_op jit(solution)/shard_map/dot_general | solution.py:495
  133.4 1.4 collective-permute-start.24
  134.7 1.6 fusion.4
  136.3 0.8 collective-permute-start.20
  137.1 1.5 fusion.5
  138.7 2.6 %collective-permute-start.22 = (bf16[128,1024]{1,0:T(8,128)(2,1)S(1)}, bf16[128,1024]{1,0:T(8,128)(2,1)S(1)}, u32[]{:S(2)}, u32[]{:S(2)}) collective-permute-start(bf16[128,1024]{1,0:T(8,128)(2,1)S(1)} %fusion.5), channel_id=1, source_target_pairs={{0,6},{2,0},{4,2},{6,4},{1,7},{3,1},{5,3},{7,5},{8,14},{10,8},{12,... | collective-permute-start | bytes 786440 | tf_op jit(solution)/shard_map/ppermute | solution.py:27
  141.3 2.4 %convolution_add_fusion.6.high = f32[128,1024]{1,0:T(8,128)} fusion(f32[128,1024]{1,0:T(8,128)S(1)} %copy-done.10, bf16[512,1024]{1,0:T(8,128)(2,1)} %collective-permute-done.19, bf16[4,128,512]{2,1,0:T(8,128)(2,1)S(1)} %bitcast.87, s32[]{:T(128)S(6)} %select_n.121), kind=kOutput, calls=%fused_computation.9 | convolution fusion | flops 134348800 | bytes 2228228 | tf_op jit(solution)/shard_map/dot_general | solution.py:495
  143.6 1.5 fusion.2
  145.2 0.8 collective-permute-start.25
  146.0 2.3 %fusion.3 = bf16[128,1024]{1,0:T(8,128)(2,1)} fusion(f32[128,1024]{1,0:T(8,128)S(1)} %copy-done.7, bf16[512,1024]{1,0:T(8,128)(2,1)} %collective-permute-done.18, bf16[128,1024]{1,0:T(8,128)(2,1)S(1)} %collective-permute-done.20, bf16[4,128,512]{2,1,0:T(8,128)(2,1)S(1)} %bitcast.89, s32[]{:T(128)S(6)} %select_n.122), kind=kOutput, calls=%fused_computation.14 | convolution fusion | flops 134742016 | bytes 2228228 | tf_op jit(solution)/shard_map/dot_general | solution.py:495
  148.3 1.3 collective-permute-start.21
  149.6 2.3 %convolution_add_fusion.7.low = f32[128,1024]{1,0:T(8,128)} fusion(f32[128,1024]{1,0:T(8,128)S(1)} %copy-done.5, bf16[512,1024]{1,0:T(8,128)(2,1)} %collective-permute-done.18, bf16[4,128,512]{2,1,0:T(8,128)(2,1)S(1)} %bitcast.90, s32[]{:T(128)S(6)} %select_n.121), kind=kOutput, calls=%fused_computation.10 | convolution fusion | flops 134348800 | bytes 2228228 | tf_op jit(solution)/shard_map/dot_general | solution.py:495
  151.9 0.8 collective-permute-done.25.left_high
  152.8 4.1 %collective-permute-done.21.right_low = bf16[128,1024]{1,0:T(8,128)(2,1)} collective-permute-done((bf16[128,1024]{1,0:T(8,128)(2,1)}, bf16[128,1024]{1,0:T(8,128)(2,1)}, u32[]{:S(2)}, u32[]{:S(2)}) %collective-permute-start.21) | collective-permute-done | bytes 262176 | tf_op jit(solution)/shard_map/ppermute | solution.py:27
  156.9 2.6 %close.1 = bf16[128,2048]{1,0:T(8,128)(2,1)} custom-call(f32[4,128]{1,0:T(4,128)} %bitcast.102, f32[128,1024]{1,0:T(8,128)} %convolution_add_fusion.7.low, f32[128,1024]{1,0:T(8,128)} %convolution_add_fusion.6.high, bf16[128,1024]{1,0:T(8,128)(2,1)} %collective-permute-done.21.right_low, bf16[128,1024]{1,0:T(8,128)(2,1)} %copy-done.14, ...), custom_call_target="tpu_custom_call" | custom-call | tf_op jit(solution)/shard_map/close/pallas_call | solution.py:532
  (107 shorter events, 7.0 us)
Async XLA Ops:
  0.0 25.6 %copy-start = (bf16[2048,512]{1,0:T(8,128)(2,1)S(1)}, bf16[2048,512]{1,0:T(8,128)(2,1)}, u32[]{:S(2)}) copy-start(bf16[2048,512]{1,0:T(8,128)(2,1)} %param.14) | copy-start | bytes 6291460
  2.0 10.8 %collective-permute-start.6 = (bf16[64,2048]{1,0:T(8,128)(2,1)}, bf16[64,2048]{1,0:T(8,128)(2,1)S(1)}, u32[]{:S(2)}, u32[]{:S(2)}) collective-permute-start(bf16[64,2048]{1,0:T(8,128)(2,1)} %get-tuple-element.37), channel_id=1, source_target_pairs={{0,6},{2,0},{4,2},{6,4},{1,7},{3,1},{5,3},{7,5},{8,14},{10,8},{12,... | collective-permute-start | bytes 786440 | tf_op jit(solution)/shard_map/ppermute | solution.py:27
  4.8 11.3 %collective-permute-start.2 = (bf16[64,2048]{1,0:T(8,128)(2,1)}, bf16[64,2048]{1,0:T(8,128)(2,1)}, u32[]{:S(2)}, u32[]{:S(2)}) collective-permute-start(bf16[64,2048]{1,0:T(8,128)(2,1)} %get-tuple-element.37), channel_id=1, source_target_pairs={{0,2},{2,4},{4,6},{6,0},{1,3},{3,5},{5,7},{7,1},{8,10},{10,12},{12... | collective-permute-start | bytes 786440 | tf_op jit(solution)/shard_map/ppermute | solution.py:27
  4.8 16.9 %collective-permute-start.5 = (bf16[64,2048]{1,0:T(8,128)(2,1)}, bf16[64,2048]{1,0:T(8,128)(2,1)}, u32[]{:S(2)}, u32[]{:S(2)}) collective-permute-start(bf16[64,2048]{1,0:T(8,128)(2,1)} %get-tuple-element.38), channel_id=1, source_target_pairs={{0,6},{2,0},{4,2},{6,4},{1,7},{3,1},{5,3},{7,5},{8,14},{10,8},{12,... | collective-permute-start | bytes 786440 | tf_op jit(solution)/shard_map/ppermute | solution.py:27
  8.0 11.7 %collective-permute-start.1 = (bf16[64,2048]{1,0:T(8,128)(2,1)}, bf16[64,2048]{1,0:T(8,128)(2,1)}, u32[]{:S(2)}, u32[]{:S(2)}) collective-permute-start(bf16[64,2048]{1,0:T(8,128)(2,1)} %get-tuple-element.38), channel_id=1, source_target_pairs={{0,2},{2,4},{4,6},{6,0},{1,3},{3,5},{5,7},{7,1},{8,10},{10,12},{12... | collective-permute-start | bytes 786440 | tf_op jit(solution)/shard_map/ppermute | solution.py:27
  8.0 20.5 %collective-permute-start = (bf16[128,2048]{1,0:T(8,128)(2,1)}, bf16[128,2048]{1,0:T(8,128)(2,1)}, u32[]{:S(2)}, u32[]{:S(2)}) collective-permute-start(bf16[128,2048]{1,0:T(8,128)(2,1)} %param.12), channel_id=1, source_target_pairs={{0,1},{1,0},{2,3},{3,2},{4,5},{5,4},{6,7},{7,6},{8,9},{9,8},{10,11... | collective-permute-start | bytes 1572872 | tf_op jit(solution)/shard_map/ppermute | solution.py:27
  9.2 3.6 %copy-start.11 = (bf16[128,2048]{1,0:T(8,128)(2,1)S(1)}, bf16[128,2048]{1,0:T(8,128)(2,1)}, u32[]{:S(2)}) copy-start(bf16[128,2048]{1,0:T(8,128)(2,1)} %param.12) | copy-start | bytes 1572868
  12.8 11.6 %copy-start.4 = (bf16[2048,896]{1,0:T(8,128)(2,1)S(1)}, bf16[2048,896]{1,0:T(8,128)(2,1)}, u32[]{:S(2)}) copy-start(bf16[2048,896]{1,0:T(8,128)(2,1)} %maximum_maximum_fusion) | copy-start | bytes 11010052
  12.8 21.3 %collective-permute-start.10 = (bf16[64,2048]{1,0:T(8,128)(2,1)S(1)}, bf16[64,2048]{1,0:T(8,128)(2,1)S(1)}, u32[]{:S(2)}, u32[]{:S(2)}) collective-permute-start(bf16[64,2048]{1,0:T(8,128)(2,1)S(1)} %collective-permute-done.6), channel_id=1, source_target_pairs={{0,6},{2,0},{4,2},{6,4},{1,7},{3,1},{5,3},{7,5},{8,14},{10,8},{12,... | collective-permute-start | bytes 786440 | tf_op jit(solution)/shard_map/ppermute | solution.py:27
  16.1 11.1 %collective-permute-start.8 = (bf16[64,2048]{1,0:T(8,128)(2,1)S(1)}, bf16[64,2048]{1,0:T(8,128)(2,1)S(1)}, u32[]{:S(2)}, u32[]{:S(2)}) collective-permute-start(bf16[64,2048]{1,0:T(8,128)(2,1)S(1)} %collective-permute-done.6), channel_id=1, source_target_pairs={{0,1},{1,0},{2,3},{3,2},{4,5},{5,4},{6,7},{7,6},{8,9},{9,8},{10,11... | collective-permute-start | bytes 786440 | tf_op jit(solution)/shard_map/ppermute | solution.py:27
  19.7 4.3 %collective-permute-start.4 = (bf16[64,2048]{1,0:T(8,128)(2,1)}, bf16[64,2048]{1,0:T(8,128)(2,1)S(1)}, u32[]{:S(2)}, u32[]{:S(2)}) collective-permute-start(bf16[64,2048]{1,0:T(8,128)(2,1)} %collective-permute-done.2), channel_id=1, source_target_pairs={{0,1},{1,0},{2,3},{3,2},{4,5},{5,4},{6,7},{7,6},{8,9},{9,8},{10,11... | collective-permute-start | bytes 786440 | tf_op jit(solution)/shard_map/ppermute | solution.py:27
  21.7 2.0 %collective-permute-start.3 = (bf16[64,2048]{1,0:T(8,128)(2,1)}, bf16[64,2048]{1,0:T(8,128)(2,1)S(1)}, u32[]{:S(2)}, u32[]{:S(2)}) collective-permute-start(bf16[64,2048]{1,0:T(8,128)(2,1)} %collective-permute-done.1), channel_id=1, source_target_pairs={{0,1},{1,0},{2,3},{3,2},{4,5},{5,4},{6,7},{7,6},{8,9},{9,8},{10,11... | collective-permute-start | bytes 786440 | tf_op jit(solution)/shard_map/ppermute | solution.py:27
  23.6 3.6 %collective-permute-start.7 = (bf16[64,2048]{1,0:T(8,128)(2,1)}, bf16[64,2048]{1,0:T(8,128)(2,1)S(1)}, u32[]{:S(2)}, u32[]{:S(2)}) collective-permute-start(bf16[64,2048]{1,0:T(8,128)(2,1)} %collective-permute-done.5), channel_id=1, source_target_pairs={{0,1},{1,0},{2,3},{3,2},{4,5},{5,4},{6,7},{7,6},{8,9},{9,8},{10,11... | collective-permute-start | bytes 786440 | tf_op jit(solution)/shard_map/ppermute | solution.py:27
  24.0 10.0 %collective-permute-start.9 = (bf16[64,2048]{1,0:T(8,128)(2,1)}, bf16[64,2048]{1,0:T(8,128)(2,1)S(1)}, u32[]{:S(2)}, u32[]{:S(2)}) collective-permute-start(bf16[64,2048]{1,0:T(8,128)(2,1)} %collective-permute-done.1), channel_id=1, source_target_pairs={{0,2},{2,4},{4,6},{6,0},{1,3},{3,5},{5,7},{7,1},{8,10},{10,12},{12... | collective-permute-start | bytes 786440 | tf_op jit(solution)/shard_map/ppermute | solution.py:27
  25.6 11.7 %copy-start.23 = (f32[256,896]{1,0:T(8,128)}, f32[256,896]{1,0:T(8,128)S(1)}, u32[]{:S(2)}) copy-start(f32[256,896]{1,0:T(8,128)S(1)} %fusion.70.g1) | copy-start | bytes 2752516
  28.6 8.7 %copy-start.24 = (f32[256,896]{1,0:T(8,128)}, f32[256,896]{1,0:T(8,128)S(1)}, u32[]{:S(2)}) copy-start(f32[256,896]{1,0:T(8,128)S(1)} %fusion.71.g2) | copy-start | bytes 2752516
  31.3 6.0 %copy-start.25 = (f32[256,896]{1,0:T(8,128)}, f32[256,896]{1,0:T(8,128)S(1)}, u32[]{:S(2)}) copy-start(f32[256,896]{1,0:T(8,128)S(1)} %fusion.69.g0) | copy-start | bytes 2752516
  34.1 1.5 collective-permute-start.11
  34.1 1.9 %collective-permute-start.12 = (bf16[64,2048]{1,0:T(8,128)(2,1)S(1)}, bf16[64,2048]{1,0:T(8,128)(2,1)S(1)}, u32[]{:S(2)}, u32[]{:S(2)}) collective-permute-start(bf16[64,2048]{1,0:T(8,128)(2,1)S(1)} %collective-permute-done.10), channel_id=1, source_target_pairs={{0,1},{1,0},{2,3},{3,2},{4,5},{5,4},{6,7},{7,6},{8,9},{9,8},{10,11... | collective-permute-start | bytes 786440 | tf_op jit(solution)/shard_map/ppermute | solution.py:27
  36.0 6.7 %copy-start.17 = (bf16[256,2048]{1,0:T(8,128)(2,1)}, bf16[256,2048]{1,0:T(8,128)(2,1)S(1)}, u32[]{:S(2)}) copy-start(bf16[256,2048]{1,0:T(8,128)(2,1)S(1)} %constant_dynamic-update-slice_fusion.10) | copy-start | bytes 3145732
  37.3 5.4 %copy-start.26 = (f32[256,896]{1,0:T(8,128)}, f32[256,896]{1,0:T(8,128)S(1)}, u32[]{:S(2)}) copy-start(f32[256,896]{1,0:T(8,128)S(1)} %fusion.72.g3) | copy-start | bytes 2752516
  37.3 9.4 %collective-permute-start.13 = (f32[8,768]{1,0:T(8,128)S(1)}, f32[8,768]{1,0:T(8,128)S(1)}, u32[]{:S(2)}, u32[]{:S(2)}) collective-permute-start(f32[8,768]{1,0:T(8,128)S(1)} %fusion.51), channel_id=1, source_target_pairs={{0,8},{8,16},{16,24},{24,32},{32,40},{40,48},{48,56},{56,64},{64,7... | collective-permute-start | bytes 73736 | tf_op jit(solution)/shard_map/ppermute | solution.py:32
  46.8 0.6 copy-start.28
  47.4 12.6 %copy-start.18 = (bf16[256,2048]{1,0:T(8,128)(2,1)S(1)}, bf16[256,2048]{1,0:T(8,128)(2,1)}, u32[]{:S(2)}) copy-start(bf16[256,2048]{1,0:T(8,128)(2,1)} %copy-done.17) | copy-start | bytes 3145732
  53.9 25.5 %copy-start.27 = (f32[512]{0:T(512)S(1)}, f32[512]{0:T(512)}, u32[]{:S(2)}) copy-start(f32[512]{0:T(512)} %param.22) | copy-start | bytes 6148
  53.9 15.5 %all-to-all-start = ((bf16[8,16,640]{2,1,0:T(8,128)(2,1)}), bf16[8,16,640]{2,1,0:T(8,128)(2,1)S(1)}, u32[]{:S(2)}, u32[]{:S(2)}) async-start(bf16[8,16,640]{2,1,0:T(8,128)(2,1)} %bitcast.99), calls=%async_computation | async-start | bytes 327680 | tf_op jit(solution)/shard_map/all_to_all | solution.py:466
  69.4 0.7 copy-start.12
  71.9 10.9 %collective-permute-start.16 = (bf16[16,640]{1,0:T(8,128)(2,1)}, bf16[16,640]{1,0:T(8,128)(2,1)S(1)}, u32[]{:S(2)}, u32[]{:S(2)}) collective-permute-start(bf16[16,640]{1,0:T(8,128)(2,1)} %get-tuple-element.31), channel_id=1, source_target_pairs={{0,192},{1,193},{2,194},{3,195},{4,196},{5,197},{6,198},{7,199},{8... | collective-permute-start | bytes 61448 | tf_op jit(solution)/shard_map/ppermute | solution.py:32
  72.6 10.2 %collective-permute-start.15 = (bf16[16,640]{1,0:T(8,128)(2,1)}, bf16[16,640]{1,0:T(8,128)(2,1)S(1)}, u32[]{:S(2)}, u32[]{:S(2)}) collective-permute-start(bf16[16,640]{1,0:T(8,128)(2,1)} %get-tuple-element.31), channel_id=1, source_target_pairs={{0,128},{64,192},{1,129},{65,193},{2,130},{66,194},{3,131},{67,195... | collective-permute-start | bytes 61448 | tf_op jit(solution)/shard_map/ppermute | solution.py:32
  77.4 5.9 %collective-permute-start.14 = (bf16[16,640]{1,0:T(8,128)(2,1)}, bf16[16,640]{1,0:T(8,128)(2,1)S(1)}, u32[]{:S(2)}, u32[]{:S(2)}) collective-permute-start(bf16[16,640]{1,0:T(8,128)(2,1)} %get-tuple-element.31), channel_id=1, source_target_pairs={{0,64},{64,128},{128,192},{1,65},{65,129},{129,193},{2,66},{66,130... | collective-permute-start | bytes 61448 | tf_op jit(solution)/shard_map/ppermute | solution.py:32
  82.3 44.7 %collective-permute-start.19 = (bf16[512,1024]{1,0:T(8,128)(2,1)}, bf16[512,1024]{1,0:T(8,128)(2,1)}, u32[]{:S(2)}, u32[]{:S(2)}) collective-permute-start(bf16[512,1024]{1,0:T(8,128)(2,1)} %get-tuple-element.35), channel_id=1, source_target_pairs={{0,1},{1,0},{2,3},{3,2},{4,5},{5,4},{6,7},{7,6},{8,9},{9,8},{10,11... | collective-permute-start | bytes 3145736 | tf_op jit(solution)/shard_map/ppermute | solution.py:27
  82.3 52.4 %collective-permute-start.18 = (bf16[512,1024]{1,0:T(8,128)(2,1)S(1)}, bf16[512,1024]{1,0:T(8,128)(2,1)}, u32[]{:S(2)}, u32[]{:S(2)}) collective-permute-start(bf16[512,1024]{1,0:T(8,128)(2,1)S(1)} %get-tuple-element.36), channel_id=1, source_target_pairs={{0,1},{1,0},{2,3},{3,2},{4,5},{5,4},{6,7},{7,6},{8,9},{9,8},{10,11... | collective-permute-start | bytes 3145736 | tf_op jit(solution)/shard_map/ppermute | solution.py:27
  82.8 0.6 copy-start.19
  82.8 0.6 copy-start.20
  83.3 0.6 copy-start.21
  85.8 13.5 %all-to-all-start.1 = ((bf16[8,16,512]{2,1,0:T(8,128)(2,1)}), bf16[8,16,512]{2,1,0:T(8,128)(2,1)S(1)}, u32[]{:S(2)}, u32[]{:S(2)}) async-start(bf16[8,16,512]{2,1,0:T(8,128)(2,1)} %join_rows.1), calls=%async_computation.1 | async-start | bytes 262144 | tf_op jit(solution)/shard_map/all_to_all | solution.py:483
  99.3 0.7 copy-start.16
  113.9 6.9 %copy-start.3 = (bf16[512,512]{1,0:T(8,128)(2,1)S(1)}, bf16[512,512]{1,0:T(8,128)(2,1)}, u32[]{:S(2)}) copy-start(bf16[512,512]{1,0:T(8,128)(2,1)} %finish.2) | copy-start | bytes 1572868
  113.9 8.2 %collective-permute-start.17 = (bf16[512,512]{1,0:T(8,128)(2,1)}, bf16[512,512]{1,0:T(8,128)(2,1)S(1)}, u32[]{:S(2)}, u32[]{:S(2)}) collective-permute-start(bf16[512,512]{1,0:T(8,128)(2,1)} %finish.3), channel_id=1, source_target_pairs={{0,1},{1,0},{2,3},{3,2},{4,5},{5,4},{6,7},{7,6},{8,9},{9,8},{10,11... | collective-permute-start | bytes 1572872 | tf_op jit(solution)/shard_map/ppermute | solution.py:27
  122.1 0.8 copy-start.1
  123.7 28.2 %all-to-all-start.2 = ((f32[4,1,128]{2,1,0:T(1,128)}), f32[4,1,128]{2,1,0:T(1,128)S(1)}, u32[]{:S(2)}, u32[]{:S(2)}) async-start(f32[4,1,128]{2,1,0:T(1,128)} %bitcast.7), calls=%async_computation.2 | async-start | bytes 4096 | tf_op jit(solution)/shard_map/all_to_all | solution.py:511
  127.0 7.7 %copy-start.2 = (bf16[512,512]{1,0:T(8,128)(2,1)S(1)}, bf16[512,512]{1,0:T(8,128)(2,1)}, u32[]{:S(2)}) copy-start(bf16[512,512]{1,0:T(8,128)(2,1)} %copy-done.1) | copy-start | bytes 1572868
  127.0 7.7 %copy-start.9 = (f32[128,1024]{1,0:T(8,128)S(1)}, f32[128,1024]{1,0:T(8,128)}, u32[]{:S(2)}) copy-start(f32[128,1024]{1,0:T(8,128)} %fusion.18) | copy-start | bytes 1572868
  127.0 10.1 %copy-start.8 = (f32[128,1024]{1,0:T(8,128)S(1)}, f32[128,1024]{1,0:T(8,128)}, u32[]{:S(2)}) copy-start(f32[128,1024]{1,0:T(8,128)} %fusion.12) | copy-start | bytes 1572868
  127.0 14.2 %copy-start.10 = (f32[128,1024]{1,0:T(8,128)S(1)}, f32[128,1024]{1,0:T(8,128)}, u32[]{:S(2)}) copy-start(f32[128,1024]{1,0:T(8,128)} %fusion.28) | copy-start | bytes 1572868
  129.7 14.0 %copy-start.6 = (f32[128,1024]{1,0:T(8,128)S(1)}, f32[128,1024]{1,0:T(8,128)}, u32[]{:S(2)}) copy-start(f32[128,1024]{1,0:T(8,128)} %fusion.10) | copy-start | bytes 1572868
  129.7 22.3 %collective-permute-start.23 = (bf16[128,1024]{1,0:T(8,128)(2,1)}, bf16[128,1024]{1,0:T(8,128)(2,1)S(1)}, u32[]{:S(2)}, u32[]{:S(2)}) collective-permute-start(bf16[128,1024]{1,0:T(8,128)(2,1)} %fusion.6), channel_id=1, source_target_pairs={{0,2},{2,4},{4,6},{6,0},{1,3},{3,5},{5,7},{7,1},{8,10},{10,12},{12... | collective-permute-start | bytes 786440 | tf_op jit(solution)/shard_map/ppermute | solution.py:27
  133.4 10.3 %collective-permute-start.24 = (bf16[128,1024]{1,0:T(8,128)(2,1)S(1)}, bf16[128,1024]{1,0:T(8,128)(2,1)S(1)}, u32[]{:S(2)}, u32[]{:S(2)}) collective-permute-start(bf16[128,1024]{1,0:T(8,128)(2,1)S(1)} %fusion.7), channel_id=1, source_target_pairs={{0,6},{2,0},{4,2},{6,4},{1,7},{3,1},{5,3},{7,5},{8,14},{10,8},{12,... | collective-permute-start | bytes 786440 | tf_op jit(solution)/shard_map/ppermute | solution.py:27
  136.3 9.7 %copy-start.7 = (f32[128,1024]{1,0:T(8,128)S(1)}, f32[128,1024]{1,0:T(8,128)}, u32[]{:S(2)}) copy-start(f32[128,1024]{1,0:T(8,128)} %fusion.24) | copy-start | bytes 1572868
  136.3 9.7 %collective-permute-start.20 = (bf16[128,1024]{1,0:T(8,128)(2,1)S(1)}, bf16[128,1024]{1,0:T(8,128)(2,1)S(1)}, u32[]{:S(2)}, u32[]{:S(2)}) collective-permute-start(bf16[128,1024]{1,0:T(8,128)(2,1)S(1)} %fusion.4), channel_id=1, source_target_pairs={{0,2},{2,4},{4,6},{6,0},{1,3},{3,5},{5,7},{7,1},{8,10},{10,12},{12... | collective-permute-start | bytes 786440 | tf_op jit(solution)/shard_map/ppermute | solution.py:27
  138.7 10.9 %copy-start.5 = (f32[128,1024]{1,0:T(8,128)S(1)}, f32[128,1024]{1,0:T(8,128)}, u32[]{:S(2)}) copy-start(f32[128,1024]{1,0:T(8,128)} %fusion.30) | copy-start | bytes 1572868
  138.7 13.2 %collective-permute-start.22 = (bf16[128,1024]{1,0:T(8,128)(2,1)S(1)}, bf16[128,1024]{1,0:T(8,128)(2,1)S(1)}, u32[]{:S(2)}, u32[]{:S(2)}) collective-permute-start(bf16[128,1024]{1,0:T(8,128)(2,1)S(1)} %fusion.5), channel_id=1, source_target_pairs={{0,6},{2,0},{4,2},{6,4},{1,7},{3,1},{5,3},{7,5},{8,14},{10,8},{12,... | collective-permute-start | bytes 786440 | tf_op jit(solution)/shard_map/ppermute | solution.py:27
  145.2 7.6 %collective-permute-start.25 = (bf16[128,1024]{1,0:T(8,128)(2,1)S(1)}, bf16[128,1024]{1,0:T(8,128)(2,1)S(1)}, u32[]{:S(2)}, u32[]{:S(2)}) collective-permute-start(bf16[128,1024]{1,0:T(8,128)(2,1)S(1)} %fusion.2), channel_id=1, source_target_pairs={{0,6},{2,0},{4,2},{6,4},{1,7},{3,1},{5,3},{7,5},{8,14},{10,8},{12,... | collective-permute-start | bytes 786440 | tf_op jit(solution)/shard_map/ppermute | solution.py:27
  148.3 8.6 %collective-permute-start.21 = (bf16[128,1024]{1,0:T(8,128)(2,1)}, bf16[128,1024]{1,0:T(8,128)(2,1)}, u32[]{:S(2)}, u32[]{:S(2)}) collective-permute-start(bf16[128,1024]{1,0:T(8,128)(2,1)} %fusion.3), channel_id=1, source_target_pairs={{0,2},{2,4},{4,6},{6,0},{1,3},{3,5},{5,7},{7,1},{8,10},{10,12},{12... | collective-permute-start | bytes 786440 | tf_op jit(solution)/shard_map/ppermute | solution.py:27
  151.9 5.0 %copy-start.22 = (f32[4,1,128]{2,1,0:T(1,128)}, f32[4,1,128]{2,1,0:T(1,128)S(1)}, u32[]{:S(2)}) copy-start(f32[4,1,128]{2,1,0:T(1,128)S(1)} %all-to-all-done.2) | copy-start | bytes 6148
  151.9 5.0 %copy-start.13 = (bf16[128,1024]{1,0:T(8,128)(2,1)}, bf16[128,1024]{1,0:T(8,128)(2,1)S(1)}, u32[]{:S(2)}) copy-start(bf16[128,1024]{1,0:T(8,128)(2,1)S(1)} %collective-permute-done.23.right_high) | copy-start | bytes 786436
  151.9 4.9 %copy-start.14 = (bf16[128,1024]{1,0:T(8,128)(2,1)}, bf16[128,1024]{1,0:T(8,128)(2,1)S(1)}, u32[]{:S(2)}) copy-start(bf16[128,1024]{1,0:T(8,128)(2,1)S(1)} %collective-permute-done.22.left_low) | copy-start | bytes 786436
  152.8 4.1 %copy-start.15 = (bf16[128,1024]{1,0:T(8,128)(2,1)}, bf16[128,1024]{1,0:T(8,128)(2,1)S(1)}, u32[]{:S(2)}) copy-start(bf16[128,1024]{1,0:T(8,128)(2,1)S(1)} %collective-permute-done.25.left_high) | copy-start | bytes 786436

commit v2 on v1

--- a/solution.py
+++ b/solution.py
@@ -15,6 +15,7 @@
 F32 = jnp.float32
 BF16 = jnp.bfloat16
 highest = lax.Precision.HIGHEST
+LIMIT = pltpu.CompilerParams(vmem_limit_bytes=20 * 1024 * 1024)
 
 
 def silu(v):
@@ -93,8 +94,8 @@
         for group, ref in enumerate((g0, g1, g2, g3)):
             for member in range(2):
                 at = pl.multiple_of(starts[2 * group + member] + 8, 8)
-                window[pl.ds(at, Q), :] = ref[member * Q : member * Q + Q, :]
-        window[0:8, :conv_cols] = halo[...]
+                window[pl.ds(at, Q), :] = ref[member * Q : member * Q + Q, :].astype(F32)
+        window[0:8, :conv_cols] = halo[...].astype(F32)[8:16, :]
         spread = spread_of(heads, width)
         row = lax.broadcasted_iota(jnp.int32, (Q, Q), 0)
         col = lax.broadcasted_iota(jnp.int32, (Q, Q), 1)
@@ -149,6 +150,7 @@
     return pl.pallas_call(
         summary_kernel(heads, rows // Q),
         in_specs=vmem_specs(7, 2),
+        out_specs=vmem_specs(5, 0),
         out_shape=[
             jax.ShapeDtypeStruct((rows, width), BF16),
             jax.ShapeDtypeStruct((rows, bc_cols), BF16),
@@ -163,14 +165,15 @@
         cost_estimate=pl.CostEstimate(
             flops=3_000_000_000, bytes_accessed=8_000_000, transcendentals=1_000_000
         ),
+        compiler_params=LIMIT,
         name="summarize",
     )(bias, rate, *groups, halo, taps_x, taps_bc)
 
 
-def inside_kernel(heads, chunks):
+def inside_kernel(heads, chunks, lead):
     def kernel(
-        skip, g0, g1, g2, g3, xc, bc, dt_in, cum_in,
-        ig_out, fz_out, sloc_out, growth_out, gate, flipped, decays, state,
+        skip, g0, g1, g2, g3, xc, bc, dt_in, cum_in, state_in,
+        ig_out, fz_out, sloc_out, growth_out, state_out, gate,
     ):
         width = xc.shape[1]
         pair = 2 * (width // heads)
@@ -185,9 +188,12 @@
         lower = row >= col
         lane = lax.broadcasted_iota(jnp.int32, (Q, pair), 1)
         zero = jnp.zeros((Q, pair), BF16)
+        dt = dt_in[...]
         cumul = cum_in[...]
-        flipped[...] = cumul.T
+        flipped = cumul.T
         total = cumul[Q - 1 : Q, :]
+        weight = dt * jnp.exp(jnp.minimum(total - cumul, 0.0))
+        reach = jnp.exp(cumul)
         wide_total = jnp.broadcast_to(total, (8, Q))
         prefix = jnp.zeros((8, Q), F32)
         for k in range(1, chunks):
@@ -206,37 +212,34 @@
                 rows8 == chunk, pltpu.roll(decay, turn, 1) if turn else decay, decay_rows
             )
         growth_out[...] = widen(grown_rows, heads, 0, spread)
-        decays[...] = widen(decay_rows, heads, 0, spread)
-        state[...] = jnp.zeros((Q, width), F32)
-
-        @pl.loop(0, chunks)
-        def _(chunk):
-            at = pl.ds(pl.multiple_of(chunk * Q, Q), Q)
-            turn = lax.rem(Q - chunk * heads, Q)
-            dt = pltpu.roll(dt_in[...], turn, 1)
-            cumul = pltpu.roll(cum_in[...], turn, 1)
-            rows = flipped[pl.ds(pl.multiple_of(chunk * heads, heads), heads), :]
-            b_rows = bc[at, :Q]
-            c_rows = bc[at, Q:]
-            x = xc[at, :].astype(F32)
-            sloc_out[chunk] = state[...].astype(BF16)
-            weight = dt * jnp.exp(jnp.minimum(cumul[Q - 1 : Q, :] - cumul, 0.0))
-            kept = (x * widen(weight, heads, 0, spread)).astype(BF16)
-            fresh = lax.dot_general(
-                b_rows, kept, (((0,), (0,)), ((), ())), preferred_element_type=F32
-            )
-            state[...] = decays[pl.ds(chunk, 1), :] * state[...] + fresh
+        decay_wide = widen(decay_rows, heads, 0, spread)
+        state = state_in[...] if lead else jnp.zeros((Q, width), F32)
+        for local in range(chunks // 2):
+            chunk = lead + local
+            at = slice(local * Q, local * Q + Q)
+            place = slice(chunk * Q, chunk * Q + Q)
+            b_rows = bc[place, :Q]
+            c_rows = bc[place, Q:]
+            x = xc[place, :].astype(F32)
+            sloc_out[local] = state.astype(BF16)
+            if chunk < chunks - 1:
+                kept = (x * widen(weight, heads, chunk, spread)).astype(BF16)
+                fresh = lax.dot_general(
+                    b_rows, kept, (((0,), (0,)), ((), ())), preferred_element_type=F32
+                )
+                state = decay_wide[chunk : chunk + 1, :] * state + fresh
             scores = lax.dot_general(
                 c_rows, b_rows, (((1,), (1,)), ((), ())), preferred_element_type=F32
             )
             scores = jnp.where(lower, scores, 0.0)
-            scaled = (x * widen(dt, heads, 0, spread)).astype(BF16)
-            act = silu(gate[at, :])
-            fz_out[at, :] = (widen(jnp.exp(cumul), heads, 0, spread) * act).astype(BF16)
+            scaled = (x * widen(dt, heads, chunk, spread)).astype(BF16)
+            act = silu(gate[chunk * Q : chunk * Q + Q, :].astype(F32))
+            fz_out[at, :] = (widen(reach, heads, chunk, spread) * act).astype(BF16)
             for first in range(0, heads, 2):
                 parts = []
                 for head in (first, first + 1):
-                    gap = cumul[:, head : head + 1] - rows[head : head + 1, :]
+                    k = chunk * heads + head
+                    gap = cumul[:, k : k + 1] - flipped[k : k + 1, :]
                     parts.append((scores * jnp.exp(jnp.minimum(gap, 0.0))).astype(BF16))
                 lo = (first // 2) * pair
                 block = scaled[:, lo : lo + pair]
@@ -253,73 +256,119 @@
                 coefficient = jnp.where(lane < pair // 2, skip[first], skip[first + 1])
                 out = out + coefficient * x[:, lo : lo + pair]
                 ig_out[at, lo : lo + pair] = (out * act[:, lo : lo + pair]).astype(BF16)
+        state_out[...] = state
 
     return kernel
 
 
-def inside(skip, groups, xc, bc, dt, cumul, heads):
+def inside(skip, groups, xc, bc, dt, cumul, state, heads, part):
     rows, width = xc.shape
     chunks = rows // Q
-    return pl.pallas_call(
-        inside_kernel(heads, chunks),
-        in_specs=vmem_specs(8),
+    half = rows // 2
+    return pl.pallas_call(
+        inside_kernel(heads, chunks, part * chunks // 2),
+        in_specs=vmem_specs(9),
+        out_specs=vmem_specs(5, 0),
         out_shape=[
-            jax.ShapeDtypeStruct((rows, width), BF16),
-            jax.ShapeDtypeStruct((rows, width), BF16),
-            jax.ShapeDtypeStruct((chunks, Q, width), BF16),
+            jax.ShapeDtypeStruct((half, width), BF16),
+            jax.ShapeDtypeStruct((half, width), BF16),
+            jax.ShapeDtypeStruct((chunks // 2, Q, width), BF16),
             jax.ShapeDtypeStruct((8, width), F32),
+            jax.ShapeDtypeStruct((Q, width), F32),
         ],
-        scratch_shapes=[
-            pltpu.VMEM((rows, width), F32),
-            pltpu.VMEM((Q, Q), F32),
-            pltpu.VMEM((8, width), F32),
-            pltpu.VMEM((Q, width), F32),
-        ],
+        scratch_shapes=[pltpu.VMEM((rows, width), BF16)],
         cost_estimate=pl.CostEstimate(
-            flops=8_000_000_000, bytes_accessed=8_000_000, transcendentals=2_000_000
-        ),
+            flops=4_000_000_000, bytes_accessed=5_000_000, transcendentals=1_000_000
+        ),
+        compiler_params=LIMIT,
         name="inside",
-    )(skip, *groups, xc, bc, dt, cumul)
-
-
-def finish_kernel(sel, c_rows, ig, fz, sloc, growth, entering, out):
-    start = entering[...].astype(F32)
-    first = 2 * pl.program_id(0)
-    for i in range(2):
-        chunk = 2 * (first + i) + sel[0]
-        state = sloc[i, 0].astype(F32) + growth[pl.ds(chunk, 1), :] * start
-        carried = jnp.dot(c_rows[i, 0], state.astype(BF16), preferred_element_type=F32)
-        out[i * Q : i * Q + Q, :] = (
-            ig[i, 0].astype(F32) + carried * fz[i, 0].astype(F32)
-        ).astype(BF16)
-
-
-def finish(sel, bc, ig, fz, sloc, growth, entering):
-    rows, width = ig.shape
-    pairs = rows // Q // 2
-    paired = lambda block: block.reshape(pairs, 2, Q, -1)
-    block = pl.BlockSpec((2, 1, Q, width), lambda i, sel: (i, sel[0], 0, 0))
-    return pl.pallas_call(
-        finish_kernel,
-        grid_spec=pltpu.PrefetchScalarGridSpec(
-            num_scalar_prefetch=1,
-            grid=(pairs // 2,),
-            in_specs=[
-                pl.BlockSpec((2, 1, Q, Q), lambda i, sel: (i, sel[0], 0, 1)),
-                block,
-                block,
-                block,
-                pl.BlockSpec(growth.shape, lambda i, sel: (0, 0)),
-                pl.BlockSpec(entering.shape, lambda i, sel: (0, 0)),
-            ],
-            out_specs=pl.BlockSpec((2 * Q, width), lambda i, sel: (i, 0)),
-        ),
-        out_shape=jax.ShapeDtypeStruct((rows // 2, width), BF16),
+    )(skip, *groups, xc, bc, dt, cumul, state)
+
+
+def finish_kernel(away):
+    def kernel(bc, ig0, fz0, sloc0, ig1, fz1, sloc1, growth, entering, out):
+        start = entering[...].astype(F32)
+        c_at = lax.axis_index("c")
+        offset = 1 - c_at if away else c_at
+        for i in range(4):
+            ig, fz, sloc = ((ig0, fz0, sloc0), (ig1, fz1, sloc1))[i // 2]
+            chunk = 2 * i + offset
+            local = 2 * (i % 2) + offset
+            at = pl.ds(pl.multiple_of(local * Q, Q), Q)
+            state = sloc[local].astype(F32) + growth[pl.ds(chunk, 1), :] * start
+            c_rows = bc[pl.ds(pl.multiple_of(chunk * Q, Q), Q), Q:]
+            carried = jnp.dot(c_rows, state.astype(BF16), preferred_element_type=F32)
+            out[i * Q : i * Q + Q, :] = (
+                ig[at, :].astype(F32) + carried * fz[at, :].astype(F32)
+            ).astype(BF16)
+
+    return kernel
+
+
+def finish(away, bc, early, late, growth, entering):
+    shape = (bc.shape[0] // 2, entering.shape[1])
+    return pl.pallas_call(
+        finish_kernel(away),
+        in_specs=vmem_specs(9, 0),
+        out_specs=pl.BlockSpec(memory_space=pltpu.VMEM),
+        out_shape=jax.ShapeDtypeStruct(shape, BF16),
         cost_estimate=pl.CostEstimate(
             flops=1_500_000_000, bytes_accessed=3_000_000, transcendentals=0
         ),
+        compiler_params=LIMIT,
         name="finish",
-    )(sel, paired(bc), paired(ig), paired(fz), paired(sloc), growth, entering)
+    )(bc, *early, *late, growth, entering)
+
+
+def project_kernel(distances):
+    def kernel(kept, arrived, own_low, other_low, own_high, other_high, *refs):
+        lows, highs = refs[: len(distances)], refs[len(distances) : -1]
+        rows_in = refs[-1]
+        width = kept.shape[1]
+        size = kept.shape[0] // Q
+        columns = own_low.shape[1]
+        x_at = lax.axis_index("x")
+        for place, distance in enumerate(distances):
+            moved = x_at + distance
+            block = jnp.where(moved >= size, moved - size, moved)
+            at = pl.ds(pl.multiple_of(block * Q, Q), Q)
+            lines = slice(place * Q, place * Q + Q)
+            rows_in[lines, :width] = kept[at, :]
+            rows_in[lines, width:] = arrived[at, :]
+            wide = rows_in[lines, :].astype(F32)
+            each = jnp.sum(wide * wide, axis=1, keepdims=True)
+            lows[place][:, columns:] = jnp.broadcast_to(each, (Q, Q)).astype(BF16)
+        for own, other, outs in ((own_low, other_low, lows), (own_high, other_high, highs)):
+            for lo in range(0, columns, 256):
+                tile = slice(lo, lo + 256)
+                result = jnp.dot(rows_in[:, :width], own[:, tile], preferred_element_type=F32)
+                result += jnp.dot(rows_in[:, width:], other[:, tile], preferred_element_type=F32)
+                result = result.astype(BF16)
+                for place, out in enumerate(outs):
+                    out[:, tile] = result[place * Q : place * Q + Q, :]
+
+    return kernel
+
+
+def project(kept, arrived, weights, distances):
+    width = kept.shape[1]
+    columns = weights[0].shape[1]
+    count = len(distances)
+    vmem = pl.BlockSpec(memory_space=pltpu.VMEM)
+    low = jax.ShapeDtypeStruct((Q, columns + Q), BF16)
+    high = jax.ShapeDtypeStruct((Q, columns), BF16)
+    return pl.pallas_call(
+        project_kernel(distances),
+        in_specs=[vmem] * 6,
+        out_specs=[vmem] * (2 * count),
+        out_shape=[low] * count + [high] * count,
+        scratch_shapes=[pltpu.VMEM((count * Q, 2 * width), BF16)],
+        cost_estimate=pl.CostEstimate(
+            flops=1_000_000_000 * count, bytes_accessed=5_000_000, transcendentals=0
+        ),
+        compiler_params=LIMIT,
+        name="project",
+    )(kept, arrived, *weights)
 
 
 def row_kernel(heads):
@@ -360,6 +409,7 @@
             jax.ShapeDtypeStruct((8, width), F32),
             jax.ShapeDtypeStruct((rows, cols), BF16),
         ],
+        compiler_params=LIMIT,
         name="row_scan",
     )(pieces)
 
@@ -391,6 +441,7 @@
         join_kernel(heads),
         in_specs=vmem_specs(5, 0),
         out_shape=jax.ShapeDtypeStruct((count, rows, width), BF16),
+        compiler_params=LIMIT,
         name="join_rows",
     )(near, middle, far, before, growth)
 
@@ -428,31 +479,24 @@
         (0, (tokens, swap(tokens))),
         (
             -1,
-            (
-                left_top,
-                left_bottom,
-                named(left_top, 1, "c"),
-                named(left_bottom, 1, "c"),
-            ),
+            (left_top, left_bottom, named(left_top, 1, "c"), named(left_bottom, 1, "c")),
         ),
         (
             1,
-            (
-                right_top,
-                right_bottom,
-                named(right_top, 1, "c"),
-                named(right_bottom, 1, "c"),
-            ),
-        ),
-        (2, (far_top, far_bottom, swap(far_top), swap(far_bottom))),
+            (right_top, right_bottom, named(right_top, 1, "c"), named(right_bottom, 1, "c")),
+        ),
+        (
+            2,
+            (far_top, far_bottom, named(far_top, 1, "c"), named(far_bottom, 1, "c")),
+        ),
     )
     conv_cols = width + bc_cols
     pairs, firsts = [], []
-    edge = jnp.zeros((8, conv_cols), F32)
+    edge = jnp.zeros((16, conv_cols), BF16)
     for distance, blocks in groups:
         pair = jnp.concatenate(blocks, axis=0)
-        first = jnp.dot(pair, w_first, preferred_element_type=F32)
-        ends = [first[m * Q + Q - 8 : m * Q + Q, :conv_cols] for m in range(2)]
+        first = jnp.dot(pair, w_first, preferred_element_type=F32).astype(BF16)
+        ends = [first[m * Q + Q - 16 : m * Q + Q, :conv_cols] for m in range(2)]
         is_last = (x_at + distance) % x_size == x_size - 1
         edge = jnp.where(is_last, jnp.where(c_at == 1, ends[0], ends[1]), edge)
         pairs.append(pair)
@@ -461,20 +505,24 @@
     xc, bc, dt, cumul, last = summarize(
         dt_bias, decay_rate, firsts, halo, conv_x, conv_bc, heads, width, bc_cols
     )
-    pairs[3], w_out, last = lax.optimization_barrier((pairs[3], w_out, last))
+    pairs[3], last = lax.optimization_barrier((pairs[3], last))
     z_size = lax.axis_size("z")
     pieces = lax.all_to_all(
         last.reshape(z_size, Q // z_size, width + Q), "z", 0, 0, tiled=True
     )
-    seconds = [jnp.dot(pair, w_in_z, preferred_element_type=F32) for pair in pairs]
+    seconds = []
+    for pair in pairs:
+        second = jnp.dot(pair, w_in_z, preferred_element_type=F32)
+        seconds.append(second.astype(BF16))
     d_half = d_model // 2
-    own_low, own_high = [
+    gained = [
         (part.astype(F32) * norm_gain[:, None]).astype(BF16)
         for part in (w_out[:, :d_half], w_out[:, d_half:])
     ]
-    w_low = (own_low, swap(own_low))
-    w_high = (own_high, swap(own_high))
-    ig, fz, sloc, growth = inside(skip, seconds, xc, bc, dt, cumul, heads)
+    weights = [(part, swap(part)) for part in gained]
+    *early, _, halfway = inside(skip, seconds, xc, bc, dt, cumul, dt, heads, 0)
+    pieces, early = lax.optimization_barrier((pieces, early))
+    *late, growth, _ = inside(skip, seconds, xc, bc, dt, cumul, halfway, heads, 1)
     before, row_growth, row_total = row_scan(pieces, heads)
     near = later(row_total, "y", 1)
     middle = later(row_total, "y", 2)
@@ -482,59 +530,47 @@
     joined = join_rows(near, middle, far, before, row_growth, heads)
     entering = lax.all_to_all(joined, "z", 0, 0, tiled=True).reshape(Q, width)
 
-    core = c_at.astype(jnp.int32)[None]
-    away = finish(1 - core, bc, ig, fz, sloc, growth, entering)
+    away = finish(True, bc, early, late, growth, entering)
     arrived = swap(away)
-    kept = finish(core, bc, ig, fz, sloc, growth, entering)
-    both = [block.reshape(x_size, own_rows, width) for block in (kept, arrived)]
-
-    def partial(distance, weights, added=None):
-        at = (x_at + distance) % x_size
-        blocks = [lax.dynamic_index_in_dim(part, at, 0, keepdims=False) for part in both]
-        result = sum(
-            jnp.dot(block, weight, preferred_element_type=F32)
-            for block, weight in zip(blocks, weights)
-        )
-        if added is not None:
-            result = result + added.astype(F32)
-        return result
-
-    def sent(distance, weights, way, added=None):
-        part = partial(distance, weights, added).astype(BF16)
-        return named(part, way)
-
-    far_low = sent(2, w_low, 1)
-    far_high = sent(2, w_high, -1)
-    right_high = sent(1, w_high, 1)
-    left_low = sent(-1, w_low, -1)
-    squares = sum(jnp.sum(jnp.square(part.astype(F32)), axis=2) for part in both)
-    squares = lax.all_to_all(squares, "x", 0, 0, tiled=True)
-    right_low = sent(1, w_low, 1, far_low)
-    left_high = sent(-1, w_high, -1, far_high)
-    low = partial(0, w_low)
-    high = partial(0, w_high)
-    return close(squares, low, high, right_low, left_low, right_high, left_high)
-
-
-def close_kernel(squares, low, high, right_low, left_low, right_high, left_high, out):
-    rows, half = low.shape
-    total = jnp.sum(squares[...], axis=0, keepdims=True)
-    scale = lax.rsqrt(jnp.broadcast_to(total, (rows, rows)).T / E + 1e-05)
+    kept = finish(False, bc, early, late, growth, entering)
+    weights = [*weights[0], *weights[1]]
+    far_low, far_high = project(kept, arrived, weights, (2,))
+    right_low, left_low, low, right_high, left_high, high = project(
+        kept, arrived, weights, (1, x_size - 1, 0)
+    )
+    far_low = named(far_low, 1)
+    far_high = named(far_high, -1)
+    right_high = named(right_high, 1)
+    left_low = named(left_low, -1)
+    right_low = (right_low.astype(F32) + far_low.astype(F32)).astype(BF16)
+    right_low = named(right_low, 1)
+    left_high = (left_high.astype(F32) + far_high.astype(F32)).astype(BF16)
+    left_high = named(left_high, -1)
+    return close(low, high, right_low, left_low, right_high, left_high)
+
+
+def close_kernel(low, high, right_low, left_low, right_high, left_high, out):
+    _, half = high.shape
+    past = slice(half, half + Q)
+    total = low[:, past].astype(F32) + right_low[:, past].astype(F32)
+    total += left_low[:, past].astype(F32)
+    scale = lax.rsqrt(total / E + 1e-05)
     sides = ((low, right_low, left_low), (high, right_high, left_high))
     for side, (own, first, second) in enumerate(sides):
-        for lo in range(0, half, rows):
-            at = slice(lo, lo + rows)
-            value = own[:, at] + first[:, at].astype(F32) + second[:, at].astype(F32)
-            out[:, side * half + lo : side * half + lo + rows] = (value * scale).astype(BF16)
-
-
-def close(squares, low, high, *parts):
+        for lo in range(0, half, Q):
+            at = slice(lo, lo + Q)
+            value = own[:, at].astype(F32) + first[:, at].astype(F32) + second[:, at].astype(F32)
+            out[:, side * half + lo : side * half + lo + Q] = (value * scale).astype(BF16)
+
+
+def close(low, high, *parts):
     return pl.pallas_call(
         close_kernel,
-        in_specs=vmem_specs(7, 0),
-        out_shape=jax.ShapeDtypeStruct((low.shape[0], 2 * low.shape[1]), BF16),
+        in_specs=vmem_specs(6, 0),
+        out_shape=jax.ShapeDtypeStruct((high.shape[0], 2 * high.shape[1]), BF16),
+        compiler_params=LIMIT,
         name="close",
-    )(squares, low, high, *parts)
+    )(low, high, *parts)
 
 
 def solution(mesh):

time: 162 us -> 140 us (0.86)
  the two profiles are of different devices: /device:TPU:8 before, /device:TPU:38 now
where the time goes in v2:
time: 140 us; the launch traced here: 139 us
  starting transfers between devices  50.6 us (36%)
  local copies, waits for them, and re-layouts  31.2 us (22%)
  waiting for transfers between devices  24 us (17%)
  Pallas kernels  19.7 us (14%)
  matrix products  9.44 us (7%)
  other arithmetic  3.09 us (2%)
    unnamed x97, local copies, waits for them, and re-layouts  29 us
    ppermute x22, waiting for transfers between devices, shift(): lax.ppermute(block, axis, [(i, (i + distance) % size) for i in range(size)])  22.8 us
    ppermute x22, starting transfers between devices, shift(): lax.ppermute(block, axis, [(i, (i + distance) % size) for i in range(size)])  20.7 us
    ppermute x4, starting transfers between devices, later(): lax.ppermute(block, axis, [(i, i + distance) for i in range(size - distan...  12.8 us
    all_to_all x1, starting transfers between devices, per_device(): lax.all_to_all(last.reshape(z_size, Q // z_size, width + Q), 'z', 0, 0, t...  9.91 us
    all_to_all x1, starting transfers between devices, per_device(): entering = lax.all_to_all(joined, 'z', 0, 0, tiled=True).reshape(Q, width)  7.21 us
    pallas_call x2, Pallas kernels, project(): pl.pallas_call(project_kernel(distances), in_specs=[vmem] * 6, out_specs=...  6.27 us
    pallas_call x2, Pallas kernels, inside(): pl.pallas_call(inside_kernel(heads, chunks, part * chunks // 2), in_specs...  5.82 us
  transfers between devices with their start and end apart: 28, of which 11 were waited for; matrix products, arithmetic and copies ran while one was open for 12% of the time, Pallas kernels for 8%

profile of v2, /device:TPU:38, one launch (start us, length us, event | category | flops | bytes accessed | tf_op | source)
XLA Modules:
  0.0 138.6 jit_solution(15917422611890917921)
XLA Ops:
  0.0 2.0 %fusion.4 = (bf16[64,2048]{1,0:T(8,128)(2,1)}, bf16[64,2048]{1,0:T(8,128)(2,1)}) fusion(bf16[128,2048]{1,0:T(8,128)(2,1)} %param.12), kind=kLoop, calls=%fused_computation.35 | loop fusion | bytes 1048576 | tf_op jit(solution)/shard_map/slice | solution.py:463
  2.0 0.8 collective-permute-start.6
  2.8 2.4 %collective-permute-start.2 = (bf16[64,2048]{1,0:T(8,128)(2,1)}, bf16[64,2048]{1,0:T(8,128)(2,1)S(1)}, u32[]{:S(2)}, u32[]{:S(2)}) collective-permute-start(bf16[64,2048]{1,0:T(8,128)(2,1)} %get-tuple-element.67), channel_id=1, source_target_pairs={{0,2},{2,4},{4,6},{6,0},{1,3},{3,5},{5,7},{7,1},{8,10},{10,12},{12... | collective-permute-start | bytes 786440 | tf_op jit(solution)/shard_map/ppermute | solution.py:28
  5.3 2.0 %collective-permute-start.5 = (bf16[64,2048]{1,0:T(8,128)(2,1)}, bf16[64,2048]{1,0:T(8,128)(2,1)}, u32[]{:S(2)}, u32[]{:S(2)}) collective-permute-start(bf16[64,2048]{1,0:T(8,128)(2,1)} %get-tuple-element.68), channel_id=1, source_target_pairs={{0,6},{2,0},{4,2},{6,4},{1,7},{3,1},{5,3},{7,5},{8,14},{10,8},{12,... | collective-permute-start | bytes 786440 | tf_op jit(solution)/shard_map/ppermute | solution.py:28
  7.3 1.0 copy.13
  8.4 1.2 constant_dynamic-update-slice_fusion.1
  9.6 3.1 %collective-permute-done.6 = bf16[64,2048]{1,0:T(8,128)(2,1)} collective-permute-done((bf16[64,2048]{1,0:T(8,128)(2,1)}, bf16[64,2048]{1,0:T(8,128)(2,1)}, u32[]{:S(2)}, u32[]{:S(2)}) %collective-permute-start.6) | collective-permute-done | bytes 262176 | tf_op jit(solution)/shard_map/ppermute | solution.py:28
  12.7 3.8 %collective-permute-done.1 = bf16[64,2048]{1,0:T(8,128)(2,1)} collective-permute-done((bf16[64,2048]{1,0:T(8,128)(2,1)}, bf16[64,2048]{1,0:T(8,128)(2,1)}, u32[]{:S(2)}, u32[]{:S(2)}) %collective-permute-start.1) | collective-permute-done | bytes 262176 | tf_op jit(solution)/shard_map/ppermute | solution.py:28
  16.6 1.0 constant_dynamic-update-slice_fusion.5
  17.6 0.8 collective-permute-done.5
  18.3 1.0 constant_dynamic-update-slice_fusion.9
  19.3 1.0 constant_dynamic-update-slice_fusion.8
  20.9 3.2 %collective-permute-start.9 = (bf16[64,2048]{1,0:T(8,128)(2,1)}, bf16[64,2048]{1,0:T(8,128)(2,1)S(1)}, u32[]{:S(2)}, u32[]{:S(2)}) collective-permute-start(bf16[64,2048]{1,0:T(8,128)(2,1)} %collective-permute-done.1), channel_id=1, source_target_pairs={{0,2},{2,4},{4,6},{6,0},{1,3},{3,5},{5,7},{7,1},{8,10},{10,12},{12... | collective-permute-start | bytes 786440 | tf_op jit(solution)/shard_map/ppermute | solution.py:28
  24.2 1.3 convolution_convert_fusion.2.g1
  26.3 1.3 convolution_convert_fusion.1.g2
  27.7 1.3 convolution_convert_fusion.3.g0
  29.7 0.9 collective-permute-done.9
  31.3 0.9 collective-permute-done.11
  32.6 1.3 convolution_convert_fusion.g3
  34.0 3.8 %collective-permute-start.13 = (bf16[16,768]{1,0:T(8,128)(2,1)S(1)}, bf16[16,768]{1,0:T(8,128)(2,1)S(1)}, u32[]{:S(2)}, u32[]{:S(2)}) collective-permute-start(bf16[16,768]{1,0:T(8,128)(2,1)S(1)} %fusion.3), channel_id=1, source_target_pairs={{0,8},{8,16},{16,24},{24,32},{32,40},{40,48},{48,56},{56,64},{64,7... | collective-permute-start | bytes 73736 | tf_op jit(solution)/shard_map/ppermute | solution.py:33
  38.6 1.2 collective-permute-done.13.halo
  39.8 4.7 %summarize.1 = (bf16[1024,512]{1,0:T(8,128)(2,1)S(1)}, bf16[1024,256]{1,0:T(8,128)(2,1)S(1)}, f32[128,128]{1,0:T(8,128)S(1)}, f32[128,128]{1,0:T(8,128)S(1)}, bf16[128,640]{1,0:T(8,128)(2,1)}) custom-call(f32[8]{0:T(128)S(1)} %copy-done.3, f32[8]{0:T(128)S(1)} %copy-done.4, bf16[256,896]{1,0:T(8,128)(2,1)S(1)} %convolution_convert_fusion.3.g0, ...), custom_call_target="tpu_custom_call" | custom-call | flops 3000000000 | bytes 8000000 | tf_op jit(solution)/shard_map/summarize/pallas_call | solution.py:150
  44.5 0.8 copy-done.12
  45.3 1.0 copy-done.28
  46.3 9.9 %all-to-all-start = ((bf16[8,16,640]{2,1,0:T(8,128)(2,1)}), bf16[8,16,640]{2,1,0:T(8,128)(2,1)S(1)}, u32[]{:S(2)}, u32[]{:S(2)}) async-start(bf16[8,16,640]{2,1,0:T(8,128)(2,1)} %bitcast), calls=%async_computation | async-start | bytes 327680 | tf_op jit(solution)/shard_map/all_to_all | solution.py:510
  56.2 2.0 %convolution_convert_fusion.4.g3 = bf16[256,512]{1,0:T(8,128)(2,1)S(1)} fusion(bf16[256,2048]{1,0:T(8,128)(2,1)} %copy-done.39, bf16[2048,512]{1,0:T(8,128)(2,1)S(1)} %copy-done), kind=kOutput, calls=%fused_computation.7 | convolution fusion | flops 537001984 | bytes 3407872 | tf_op jit(solution)/shard_map/dot_general | solution.py:515
  58.3 2.9 %inside.2 = (bf16[512,512]{1,0:T(8,128)(2,1)S(1)}, bf16[512,512]{1,0:T(8,128)(2,1)S(1)}, bf16[4,128,512]{2,1,0:T(8,128)(2,1)S(1)}, f32[8,512]{1,0:T(8,128)}, f32[128,512]{1,0:T(8,128)S(1)}) custom-call(f32[8]{0:T(128)S(1)} %copy-done.5, bf16[256,512]{1,0:T(8,128)(2,1)S(1)} %convolution_convert_fusion.7.g0, ...), custom_call_target="tpu_custom_call" | custom-call | flops 4000000000 | bytes 5000000 | tf_op jit(solution)/shard_map/inside/pallas_call | solution.py:268
  61.3 0.8 copy-done.16
  62.1 0.8 copy-done.18
  62.9 0.8 copy-done.20
  64.7 4.9 %collective-permute-start.16 = (bf16[16,640]{1,0:T(8,128)(2,1)S(1)}, bf16[16,640]{1,0:T(8,128)(2,1)S(1)}, u32[]{:S(2)}, u32[]{:S(2)}) collective-permute-start(bf16[16,640]{1,0:T(8,128)(2,1)S(1)} %get-tuple-element.54), channel_id=1, source_target_pairs={{0,192},{1,193},{2,194},{3,195},{4,196},{5,197},{6,198},{7,199},{8... | collective-permute-start | bytes 61448 | tf_op jit(solution)/shard_map/ppermute | solution.py:33
  69.6 1.3 collective-permute-start.15
  70.9 2.8 %collective-permute-start.14 = (bf16[16,640]{1,0:T(8,128)(2,1)S(1)}, bf16[16,640]{1,0:T(8,128)(2,1)S(1)}, u32[]{:S(2)}, u32[]{:S(2)}) collective-permute-start(bf16[16,640]{1,0:T(8,128)(2,1)S(1)} %get-tuple-element.54), channel_id=1, source_target_pairs={{0,64},{64,128},{128,192},{1,65},{65,129},{129,193},{2,66},{66,130... | collective-permute-start | bytes 61448 | tf_op jit(solution)/shard_map/ppermute | solution.py:33
  73.7 2.9 %multiply_convert_fusion = (bf16[512,1024]{1,0:T(8,128)(2,1)S(1)}, bf16[512,1024]{1,0:T(8,128)(2,1)}) fusion(bf16[512,2048]{1,0:T(8,128)(2,1)} %param.23, f32[512]{0:T(512)S(1)} %copy-done.40), kind=kLoop, calls=%fused_computation.1 | loop fusion | flops 3145728 | bytes 4196352 | tf_op jit(solution)/shard_map/convert_element_type | solution.py:519
  77.1 0.9 join_rows.1
  78.0 7.2 %all-to-all-start.1 = ((bf16[8,16,512]{2,1,0:T(8,128)(2,1)}), bf16[8,16,512]{2,1,0:T(8,128)(2,1)S(1)}, u32[]{:S(2)}, u32[]{:S(2)}) async-start(bf16[8,16,512]{2,1,0:T(8,128)(2,1)} %join_rows.1), calls=%async_computation.1 | async-start | bytes 262144 | tf_op jit(solution)/shard_map/all_to_all | solution.py:531
  85.2 0.9 copy-done.7
  86.2 0.9 copy-done.9
  87.1 0.9 copy-done.11
  88.1 1.0 copy-done.14
  89.1 1.2 copy-done.30
  90.3 0.9 copy-done.34
  91.3 0.8 copy-done.36
  92.1 0.8 copy-done.38
  93.0 2.9 %inside.3 = (bf16[512,512]{1,0:T(8,128)(2,1)S(1)}, bf16[512,512]{1,0:T(8,128)(2,1)S(1)}, bf16[4,128,512]{2,1,0:T(8,128)(2,1)S(1)}, f32[8,512]{1,0:T(8,128)S(1)}, f32[128,512]{1,0:T(8,128)}) custom-call(f32[8]{0:T(128)S(1)} %copy-done.5, bf16[256,512]{1,0:T(8,128)(2,1)S(1)} %copy-done.9, bf16[256,512]{1,0:T(8,128)(2,1)S(1)} %convolution_convert_fusion.6.g1, ...), custom_call_target="tpu_custom_call" | custom-call | flops 4000000000 | bytes 5000000 | tf_op jit(solution)/shard_map/inside/pallas_call | solution.py:268
  95.9 0.8 copy-done.22
  96.7 0.8 copy-done.24
  98.9 1.0 copy-done.15
  99.9 1.0 copy-done.17
  101.0 1.0 copy-done.19
  102.0 1.0 copy-done.21
  103.0 1.0 copy-done.23
  104.1 1.0 copy-done.25
  105.1 1.0 copy-done.27
  107.7 1.5 %collective-permute-done.17.arrived = bf16[512,512]{1,0:T(8,128)(2,1)S(1)} collective-permute-done((bf16[512,512]{1,0:T(8,128)(2,1)S(1)}, bf16[512,512]{1,0:T(8,128)(2,1)S(1)}, u32[]{:S(2)}, u32[]{:S(2)}) %collective-permute-start.17) | collective-permute-done | bytes 524320 | tf_op jit(solution)/shard_map/ppermute | solution.py:28
  109.2 2.6 %project.3 = (bf16[128,1152]{1,0:T(8,128)(2,1)S(1)}, bf16[128,1024]{1,0:T(8,128)(2,1)S(1)}) custom-call(bf16[512,512]{1,0:T(8,128)(2,1)S(1)} %finish.2.kept, bf16[512,512]{1,0:T(8,128)(2,1)S(1)} %collective-permute-done.17.arrived, bf16[512,1024]{1,0:T(8,128)(2,1)} %get-tuple-element.66.own_low, bf16[512,1024]{1,0:T(8,128)(2,1)} %collective-permute-done.18.other_low, ...), custom_call_target="tpu_custom_call" | custom-call | flops 1000000000 | bytes 5000000 | tf_op jit(solution)/shard_map/project/pallas_call | solution.py:360
  111.8 3.7 %collective-permute-start.20 = (bf16[128,1152]{1,0:T(8,128)(2,1)S(1)}, bf16[128,1152]{1,0:T(8,128)(2,1)S(1)}, u32[]{:S(2)}, u32[]{:S(2)}) collective-permute-start(bf16[128,1152]{1,0:T(8,128)(2,1)S(1)} %get-tuple-element.60), channel_id=1, source_target_pairs={{0,2},{2,4},{4,6},{6,0},{1,3},{3,5},{5,7},{7,1},{8,10},{10,12},{12... | collective-permute-start | bytes 884744 | tf_op jit(solution)/shard_map/ppermute | solution.py:28
  115.5 3.7 %project.2 = (bf16[128,1152]{1,0:T(8,128)(2,1)S(1)}, bf16[128,1152]{1,0:T(8,128)(2,1)S(1)}, bf16[128,1152]{1,0:T(8,128)(2,1)S(1)}, bf16[128,1024]{1,0:T(8,128)(2...) custom-call(bf16[512,512]{1,0:T(8,128)(2,1)S(1)} %finish.2.kept, ...), custom_call_target="tpu_custom_call" | custom-call | flops 3000000000 | bytes 5000000 | tf_op jit(solution)/shard_map/project/pallas_call | solution.py:360
  119.2 3.3 %collective-permute-start.23 = (bf16[128,1024]{1,0:T(8,128)(2,1)S(1)}, bf16[128,1024]{1,0:T(8,128)(2,1)S(1)}, u32[]{:S(2)}, u32[]{:S(2)}) collective-permute-start(bf16[128,1024]{1,0:T(8,128)(2,1)S(1)} %get-tuple-element.62), channel_id=1, source_target_pairs={{0,2},{2,4},{4,6},{6,0},{1,3},{3,5},{5,7},{7,1},{8,10},{10,12},{12... | collective-permute-start | bytes 786440 | tf_op jit(solution)/shard_map/ppermute | solution.py:28
  122.6 3.3 %collective-permute-start.21 = (bf16[128,1152]{1,0:T(8,128)(2,1)S(1)}, bf16[128,1152]{1,0:T(8,128)(2,1)S(1)}, u32[]{:S(2)}, u32[]{:S(2)}) collective-permute-start(bf16[128,1152]{1,0:T(8,128)(2,1)S(1)} %add_convert_fusion), channel_id=1, source_target_pairs={{0,2},{2,4},{4,6},{6,0},{1,3},{3,5},{5,7},{7,1},{8,10},{10,12},{12... | collective-permute-start | bytes 884744 | tf_op jit(solution)/shard_map/ppermute | solution.py:28
  126.1 3.1 %collective-permute-done.23.right_high = bf16[128,1024]{1,0:T(8,128)(2,1)S(1)} collective-permute-done((bf16[128,1024]{1,0:T(8,128)(2,1)S(1)}, bf16[128,1024]{1,0:T(8,128)(2,1)S(1)}, u32[]{:S(2)}, u32[]{:S(2)}) %collective-permute-start.23) | collective-permute-done | bytes 262176 | tf_op jit(solution)/shard_map/ppermute | solution.py:28
  129.2 4.4 %collective-permute-done.22.left_low = bf16[128,1152]{1,0:T(8,128)(2,1)S(1)} collective-permute-done((bf16[128,1152]{1,0:T(8,128)(2,1)S(1)}, bf16[128,1152]{1,0:T(8,128)(2,1)S(1)}, u32[]{:S(2)}, u32[]{:S(2)}) %collective-permute-start.22) | collective-permute-done | bytes 294944 | tf_op jit(solution)/shard_map/ppermute | solution.py:28
  133.6 3.9 %collective-permute-done.25.left_high = bf16[128,1024]{1,0:T(8,128)(2,1)S(1)} collective-permute-done((bf16[128,1024]{1,0:T(8,128)(2,1)S(1)}, bf16[128,1024]{1,0:T(8,128)(2,1)S(1)}, u32[]{:S(2)}, u32[]{:S(2)}) %collective-permute-start.25) | collective-permute-done | bytes 262176 | tf_op jit(solution)/shard_map/ppermute | solution.py:28
  137.5 1.1 close.1
  (118 shorter events, 8.7 us)
Async XLA Ops:
  0.0 25.5 %copy-start = (bf16[2048,512]{1,0:T(8,128)(2,1)S(1)}, bf16[2048,512]{1,0:T(8,128)(2,1)}, u32[]{:S(2)}) copy-start(bf16[2048,512]{1,0:T(8,128)(2,1)} %param.14) | copy-start | bytes 6291460
  2.0 10.7 %collective-permute-start.6 = (bf16[64,2048]{1,0:T(8,128)(2,1)}, bf16[64,2048]{1,0:T(8,128)(2,1)}, u32[]{:S(2)}, u32[]{:S(2)}) collective-permute-start(bf16[64,2048]{1,0:T(8,128)(2,1)} %get-tuple-element.67), channel_id=1, source_target_pairs={{0,6},{2,0},{4,2},{6,4},{1,7},{3,1},{5,3},{7,5},{8,14},{10,8},{12,... | collective-permute-start | bytes 786440 | tf_op jit(solution)/shard_map/ppermute | solution.py:28
  2.8 9.9 %collective-permute-start.2 = (bf16[64,2048]{1,0:T(8,128)(2,1)}, bf16[64,2048]{1,0:T(8,128)(2,1)S(1)}, u32[]{:S(2)}, u32[]{:S(2)}) collective-permute-start(bf16[64,2048]{1,0:T(8,128)(2,1)} %get-tuple-element.67), channel_id=1, source_target_pairs={{0,2},{2,4},{4,6},{6,0},{1,3},{3,5},{5,7},{7,1},{8,10},{10,12},{12... | collective-permute-start | bytes 786440 | tf_op jit(solution)/shard_map/ppermute | solution.py:28
  5.3 11.3 %collective-permute-start.1 = (bf16[64,2048]{1,0:T(8,128)(2,1)}, bf16[64,2048]{1,0:T(8,128)(2,1)}, u32[]{:S(2)}, u32[]{:S(2)}) collective-permute-start(bf16[64,2048]{1,0:T(8,128)(2,1)} %get-tuple-element.68), channel_id=1, source_target_pairs={{0,2},{2,4},{4,6},{6,0},{1,3},{3,5},{5,7},{7,1},{8,10},{10,12},{12... | collective-permute-start | bytes 786440 | tf_op jit(solution)/shard_map/ppermute | solution.py:28
  5.3 13.1 %collective-permute-start.5 = (bf16[64,2048]{1,0:T(8,128)(2,1)}, bf16[64,2048]{1,0:T(8,128)(2,1)}, u32[]{:S(2)}, u32[]{:S(2)}) collective-permute-start(bf16[64,2048]{1,0:T(8,128)(2,1)} %get-tuple-element.68), channel_id=1, source_target_pairs={{0,6},{2,0},{4,2},{6,4},{1,7},{3,1},{5,3},{7,5},{8,14},{10,8},{12,... | collective-permute-start | bytes 786440 | tf_op jit(solution)/shard_map/ppermute | solution.py:28
  7.3 20.3 %collective-permute-start = (bf16[128,2048]{1,0:T(8,128)(2,1)}, bf16[128,2048]{1,0:T(8,128)(2,1)S(1)}, u32[]{:S(2)}, u32[]{:S(2)}) collective-permute-start(bf16[128,2048]{1,0:T(8,128)(2,1)} %param.12), channel_id=1, source_target_pairs={{0,1},{1,0},{2,3},{3,2},{4,5},{5,4},{6,7},{7,6},{8,9},{9,8},{10,11... | collective-permute-start | bytes 1572872 | tf_op jit(solution)/shard_map/ppermute | solution.py:28
  8.4 15.7 %copy-start.41 = (bf16[2048,512]{1,0:T(8,128)(2,1)S(1)}, bf16[2048,512]{1,0:T(8,128)(2,1)}, u32[]{:S(2)}) copy-start(bf16[2048,512]{1,0:T(8,128)(2,1)} %param.13) | copy-start | bytes 6291460
  8.4 15.7 %copy-start.42 = (bf16[2048,256]{1,0:T(8,128)(2,1)S(1)}, bf16[2048,256]{1,0:T(8,128)(2,1)}, u32[]{:S(2)}) copy-start(bf16[2048,256]{1,0:T(8,128)(2,1)} %param.15) | copy-start | bytes 3145732
  12.7 18.0 %collective-permute-start.10 = (bf16[64,2048]{1,0:T(8,128)(2,1)}, bf16[64,2048]{1,0:T(8,128)(2,1)S(1)}, u32[]{:S(2)}, u32[]{:S(2)}) collective-permute-start(bf16[64,2048]{1,0:T(8,128)(2,1)} %collective-permute-done.6), channel_id=1, source_target_pairs={{0,6},{2,0},{4,2},{6,4},{1,7},{3,1},{5,3},{7,5},{8,14},{10,8},{12,... | collective-permute-start | bytes 786440 | tf_op jit(solution)/shard_map/ppermute | solution.py:28
  12.7 13.5 %collective-permute-start.8 = (bf16[64,2048]{1,0:T(8,128)(2,1)}, bf16[64,2048]{1,0:T(8,128)(2,1)S(1)}, u32[]{:S(2)}, u32[]{:S(2)}) collective-permute-start(bf16[64,2048]{1,0:T(8,128)(2,1)} %collective-permute-done.6), channel_id=1, source_target_pairs={{0,1},{1,0},{2,3},{3,2},{4,5},{5,4},{6,7},{7,6},{8,9},{9,8},{10,11... | collective-permute-start | bytes 786440 | tf_op jit(solution)/shard_map/ppermute | solution.py:28
  16.5 4.4 %collective-permute-start.4 = (bf16[64,2048]{1,0:T(8,128)(2,1)S(1)}, bf16[64,2048]{1,0:T(8,128)(2,1)S(1)}, u32[]{:S(2)}, u32[]{:S(2)}) collective-permute-start(bf16[64,2048]{1,0:T(8,128)(2,1)S(1)} %collective-permute-done.2), channel_id=1, source_target_pairs={{0,1},{1,0},{2,3},{3,2},{4,5},{5,4},{6,7},{7,6},{8,9},{9,8},{10,11... | collective-permute-start | bytes 786440 | tf_op jit(solution)/shard_map/ppermute | solution.py:28
  18.3 1.9 %collective-permute-start.3 = (bf16[64,2048]{1,0:T(8,128)(2,1)}, bf16[64,2048]{1,0:T(8,128)(2,1)S(1)}, u32[]{:S(2)}, u32[]{:S(2)}) collective-permute-start(bf16[64,2048]{1,0:T(8,128)(2,1)} %collective-permute-done.1), channel_id=1, source_target_pairs={{0,1},{1,0},{2,3},{3,2},{4,5},{5,4},{6,7},{7,6},{8,9},{9,8},{10,11... | collective-permute-start | bytes 786440 | tf_op jit(solution)/shard_map/ppermute | solution.py:28
  20.3 5.9 %collective-permute-start.7 = (bf16[64,2048]{1,0:T(8,128)(2,1)}, bf16[64,2048]{1,0:T(8,128)(2,1)S(1)}, u32[]{:S(2)}, u32[]{:S(2)}) collective-permute-start(bf16[64,2048]{1,0:T(8,128)(2,1)} %collective-permute-done.5), channel_id=1, source_target_pairs={{0,1},{1,0},{2,3},{3,2},{4,5},{5,4},{6,7},{7,6},{8,9},{9,8},{10,11... | collective-permute-start | bytes 786440 | tf_op jit(solution)/shard_map/ppermute | solution.py:28
  20.9 9.7 %collective-permute-start.9 = (bf16[64,2048]{1,0:T(8,128)(2,1)}, bf16[64,2048]{1,0:T(8,128)(2,1)S(1)}, u32[]{:S(2)}, u32[]{:S(2)}) collective-permute-start(bf16[64,2048]{1,0:T(8,128)(2,1)} %collective-permute-done.1), channel_id=1, source_target_pairs={{0,2},{2,4},{4,6},{6,0},{1,3},{3,5},{5,7},{7,1},{8,10},{10,12},{12... | collective-permute-start | bytes 786440 | tf_op jit(solution)/shard_map/ppermute | solution.py:28
  29.7 28.5 %copy-start.6 = (bf16[256,512]{1,0:T(8,128)(2,1)}, bf16[256,512]{1,0:T(8,128)(2,1)S(1)}, u32[]{:S(2)}) copy-start(bf16[256,512]{1,0:T(8,128)(2,1)S(1)} %convolution_convert_fusion.5.g2) | copy-start | bytes 786436
  30.7 1.5 %collective-permute-start.11 = (bf16[64,2048]{1,0:T(8,128)(2,1)S(1)}, bf16[64,2048]{1,0:T(8,128)(2,1)S(1)}, u32[]{:S(2)}, u32[]{:S(2)}) collective-permute-start(bf16[64,2048]{1,0:T(8,128)(2,1)S(1)} %collective-permute-done.9), channel_id=1, source_target_pairs={{0,1},{1,0},{2,3},{3,2},{4,5},{5,4},{6,7},{7,6},{8,9},{9,8},{10,11... | collective-permute-start | bytes 786440 | tf_op jit(solution)/shard_map/ppermute | solution.py:28
  30.7 1.9 %collective-permute-start.12 = (bf16[64,2048]{1,0:T(8,128)(2,1)S(1)}, bf16[64,2048]{1,0:T(8,128)(2,1)S(1)}, u32[]{:S(2)}, u32[]{:S(2)}) collective-permute-start(bf16[64,2048]{1,0:T(8,128)(2,1)S(1)} %collective-permute-done.10), channel_id=1, source_target_pairs={{0,1},{1,0},{2,3},{3,2},{4,5},{5,4},{6,7},{7,6},{8,9},{9,8},{10,11... | collective-permute-start | bytes 786440 | tf_op jit(solution)/shard_map/ppermute | solution.py:28
  32.6 1.3 copy-start.39
  33.9 5.8 %copy-start.1 = (f32[4,512]{1,0:T(4,128)S(1)}, f32[4,512]{1,0:T(4,128)}, u32[]{:S(2)}) copy-start(f32[4,512]{1,0:T(4,128)} %taps_x.1) | copy-start | bytes 24580
  34.0 5.8 %copy-start.2 = (f32[4,256]{1,0:T(4,128)S(1)}, f32[4,256]{1,0:T(4,128)}, u32[]{:S(2)}) copy-start(f32[4,256]{1,0:T(4,128)} %taps_bc.1) | copy-start | bytes 12292
  34.0 5.8 %copy-start.3 = (f32[8]{0:T(128)S(1)}, f32[8]{0:T(128)}, u32[]{:S(2)}) copy-start(f32[8]{0:T(128)} %bias.1) | copy-start | bytes 100
  34.0 5.8 %copy-start.4 = (f32[8]{0:T(128)S(1)}, f32[8]{0:T(128)}, u32[]{:S(2)}) copy-start(f32[8]{0:T(128)} %rate.1) | copy-start | bytes 100
  34.0 5.7 %collective-permute-start.13 = (bf16[16,768]{1,0:T(8,128)(2,1)S(1)}, bf16[16,768]{1,0:T(8,128)(2,1)S(1)}, u32[]{:S(2)}, u32[]{:S(2)}) collective-permute-start(bf16[16,768]{1,0:T(8,128)(2,1)S(1)} %fusion.3), channel_id=1, source_target_pairs={{0,8},{8,16},{16,24},{24,32},{32,40},{40,48},{48,56},{56,64},{64,7... | collective-permute-start | bytes 73736 | tf_op jit(solution)/shard_map/ppermute | solution.py:33
  38.6 19.7 %copy-start.8 = (bf16[256,512]{1,0:T(8,128)(2,1)}, bf16[256,512]{1,0:T(8,128)(2,1)S(1)}, u32[]{:S(2)}) copy-start(bf16[256,512]{1,0:T(8,128)(2,1)S(1)} %convolution_convert_fusion.7.g0) | copy-start | bytes 786436
  45.3 1.0 copy-start.28
  46.3 15.0 %copy-start.35 = (f32[128,128]{1,0:T(8,128)}, f32[128,128]{1,0:T(8,128)S(1)}, u32[]{:S(2)}) copy-start(f32[128,128]{1,0:T(8,128)S(1)} %get-tuple-element.40.dt_in.state_in) | copy-start | bytes 196612
  46.3 15.0 %copy-start.37 = (f32[128,128]{1,0:T(8,128)}, f32[128,128]{1,0:T(8,128)S(1)}, u32[]{:S(2)}) copy-start(f32[128,128]{1,0:T(8,128)S(1)} %get-tuple-element.41.cum_in) | copy-start | bytes 196612
  46.3 12.0 %copy-start.5 = (f32[8]{0:T(128)S(1)}, f32[8]{0:T(128)}, u32[]{:S(2)}) copy-start(f32[8]{0:T(128)} %skip.3) | copy-start | bytes 100
  46.3 18.2 %all-to-all-start = ((bf16[8,16,640]{2,1,0:T(8,128)(2,1)}), bf16[8,16,640]{2,1,0:T(8,128)(2,1)S(1)}, u32[]{:S(2)}, u32[]{:S(2)}) async-start(bf16[8,16,640]{2,1,0:T(8,128)(2,1)} %bitcast), calls=%async_computation | async-start | bytes 327680 | tf_op jit(solution)/shard_map/all_to_all | solution.py:510
  56.2 2.1 %copy-start.13 = (bf16[1024,256]{1,0:T(8,128)(2,1)S(1)}, bf16[1024,256]{1,0:T(8,128)(2,1)}, u32[]{:S(2)}) copy-start(bf16[1024,256]{1,0:T(8,128)(2,1)} %copy-done.12) | copy-start | bytes 1572868
  56.2 2.1 %copy-start.29 = (bf16[1024,512]{1,0:T(8,128)(2,1)S(1)}, bf16[1024,512]{1,0:T(8,128)(2,1)}, u32[]{:S(2)}) copy-start(bf16[1024,512]{1,0:T(8,128)(2,1)} %copy-done.28) | copy-start | bytes 3145732
  58.2 3.0 %copy-start.10 = (bf16[256,512]{1,0:T(8,128)(2,1)}, bf16[256,512]{1,0:T(8,128)(2,1)S(1)}, u32[]{:S(2)}) copy-start(bf16[256,512]{1,0:T(8,128)(2,1)S(1)} %convolution_convert_fusion.4.g3) | copy-start | bytes 786436
  58.3 15.4 %copy-start.40 = (f32[512]{0:T(512)S(1)}, f32[512]{0:T(512)}, u32[]{:S(2)}) copy-start(f32[512]{0:T(512)} %param.22) | copy-start | bytes 6148
  61.3 0.8 copy-start.16
  62.1 0.8 copy-start.18
  62.9 0.8 copy-start.20
  64.7 12.5 %collective-permute-start.16 = (bf16[16,640]{1,0:T(8,128)(2,1)S(1)}, bf16[16,640]{1,0:T(8,128)(2,1)S(1)}, u32[]{:S(2)}, u32[]{:S(2)}) collective-permute-start(bf16[16,640]{1,0:T(8,128)(2,1)S(1)} %get-tuple-element.54), channel_id=1, source_target_pairs={{0,192},{1,193},{2,194},{3,195},{4,196},{5,197},{6,198},{7,199},{8... | collective-permute-start | bytes 61448 | tf_op jit(solution)/shard_map/ppermute | solution.py:33
  69.6 7.5 %collective-permute-start.15 = (bf16[16,640]{1,0:T(8,128)(2,1)S(1)}, bf16[16,640]{1,0:T(8,128)(2,1)S(1)}, u32[]{:S(2)}, u32[]{:S(2)}) collective-permute-start(bf16[16,640]{1,0:T(8,128)(2,1)S(1)} %get-tuple-element.54), channel_id=1, source_target_pairs={{0,128},{64,192},{1,129},{65,193},{2,130},{66,194},{3,131},{67,195... | collective-permute-start | bytes 61448 | tf_op jit(solution)/shard_map/ppermute | solution.py:33
  70.9 6.2 %collective-permute-start.14 = (bf16[16,640]{1,0:T(8,128)(2,1)S(1)}, bf16[16,640]{1,0:T(8,128)(2,1)S(1)}, u32[]{:S(2)}, u32[]{:S(2)}) collective-permute-start(bf16[16,640]{1,0:T(8,128)(2,1)S(1)} %get-tuple-element.54), channel_id=1, source_target_pairs={{0,64},{64,128},{128,192},{1,65},{65,129},{129,193},{2,66},{66,130... | collective-permute-start | bytes 61448 | tf_op jit(solution)/shard_map/ppermute | solution.py:33
  76.6 31.1 %collective-permute-start.19 = (bf16[512,1024]{1,0:T(8,128)(2,1)S(1)}, bf16[512,1024]{1,0:T(8,128)(2,1)}, u32[]{:S(2)}, u32[]{:S(2)}) collective-permute-start(bf16[512,1024]{1,0:T(8,128)(2,1)S(1)} %get-tuple-element.65.own_high), channel_id=1, source_target_pairs={{0,1},{1,0},{2,3},{3,2},{4,5},{5,4},{6,7},{7,6},{8,9},{9,8},{10,11... | collective-permute-start | bytes 3145736 | tf_op jit(solution)/shard_map/ppermute | solution.py:28
  76.6 31.1 %collective-permute-start.18 = (bf16[512,1024]{1,0:T(8,128)(2,1)}, bf16[512,1024]{1,0:T(8,128)(2,1)}, u32[]{:S(2)}, u32[]{:S(2)}) collective-permute-start(bf16[512,1024]{1,0:T(8,128)(2,1)} %get-tuple-element.66.own_low), channel_id=1, source_target_pairs={{0,1},{1,0},{2,3},{3,2},{4,5},{5,4},{6,7},{7,6},{8,9},{9,8},{10,11... | collective-permute-start | bytes 3145736 | tf_op jit(solution)/shard_map/ppermute | solution.py:28
  78.0 20.9 %all-to-all-start.1 = ((bf16[8,16,512]{2,1,0:T(8,128)(2,1)}), bf16[8,16,512]{2,1,0:T(8,128)(2,1)S(1)}, u32[]{:S(2)}, u32[]{:S(2)}) async-start(bf16[8,16,512]{2,1,0:T(8,128)(2,1)} %join_rows.1), calls=%async_computation.1 | async-start | bytes 262144 | tf_op jit(solution)/shard_map/all_to_all | solution.py:531
  85.2 0.9 copy-start.7
  86.2 0.9 copy-start.9
  87.1 0.9 copy-start.11
  88.1 1.0 copy-start.14
  89.1 1.2 copy-start.30
  90.3 0.9 copy-start.34
  91.3 0.8 copy-start.36
  92.1 0.8 copy-start.38
  98.9 1.0 copy-start.15
  99.9 1.0 copy-start.17
  101.0 1.0 copy-start.19
  102.0 1.0 copy-start.21
  103.0 1.0 copy-start.23
  104.1 1.0 copy-start.25
  105.1 1.0 copy-start.27
  107.2 2.0 %collective-permute-start.17 = (bf16[512,512]{1,0:T(8,128)(2,1)S(1)}, bf16[512,512]{1,0:T(8,128)(2,1)S(1)}, u32[]{:S(2)}, u32[]{:S(2)}) collective-permute-start(bf16[512,512]{1,0:T(8,128)(2,1)S(1)} %finish.3), channel_id=1, source_target_pairs={{0,1},{1,0},{2,3},{3,2},{4,5},{5,4},{6,7},{7,6},{8,9},{9,8},{10,11... | collective-permute-start | bytes 1572872 | tf_op jit(solution)/shard_map/ppermute | solution.py:28
  111.8 10.7 %collective-permute-start.20 = (bf16[128,1152]{1,0:T(8,128)(2,1)S(1)}, bf16[128,1152]{1,0:T(8,128)(2,1)S(1)}, u32[]{:S(2)}, u32[]{:S(2)}) collective-permute-start(bf16[128,1152]{1,0:T(8,128)(2,1)S(1)} %get-tuple-element.60), channel_id=1, source_target_pairs={{0,2},{2,4},{4,6},{6,0},{1,3},{3,5},{5,7},{7,1},{8,10},{10,12},{12... | collective-permute-start | bytes 884744 | tf_op jit(solution)/shard_map/ppermute | solution.py:28
  115.5 10.4 %collective-permute-start.24 = (bf16[128,1024]{1,0:T(8,128)(2,1)S(1)}, bf16[128,1024]{1,0:T(8,128)(2,1)S(1)}, u32[]{:S(2)}, u32[]{:S(2)}) collective-permute-start(bf16[128,1024]{1,0:T(8,128)(2,1)S(1)} %get-tuple-element.64), channel_id=1, source_target_pairs={{0,6},{2,0},{4,2},{6,4},{1,7},{3,1},{5,3},{7,5},{8,14},{10,8},{12,... | collective-permute-start | bytes 786440 | tf_op jit(solution)/shard_map/ppermute | solution.py:28
  119.2 10.0 %collective-permute-start.23 = (bf16[128,1024]{1,0:T(8,128)(2,1)S(1)}, bf16[128,1024]{1,0:T(8,128)(2,1)S(1)}, u32[]{:S(2)}, u32[]{:S(2)}) collective-permute-start(bf16[128,1024]{1,0:T(8,128)(2,1)S(1)} %get-tuple-element.62), channel_id=1, source_target_pairs={{0,2},{2,4},{4,6},{6,0},{1,3},{3,5},{5,7},{7,1},{8,10},{10,12},{12... | collective-permute-start | bytes 786440 | tf_op jit(solution)/shard_map/ppermute | solution.py:28
  122.5 11.1 %collective-permute-start.22 = (bf16[128,1152]{1,0:T(8,128)(2,1)S(1)}, bf16[128,1152]{1,0:T(8,128)(2,1)S(1)}, u32[]{:S(2)}, u32[]{:S(2)}) collective-permute-start(bf16[128,1152]{1,0:T(8,128)(2,1)S(1)} %get-tuple-element.61), channel_id=1, source_target_pairs={{0,6},{2,0},{4,2},{6,4},{1,7},{3,1},{5,3},{7,5},{8,14},{10,8},{12,... | collective-permute-start | bytes 884744 | tf_op jit(solution)/shard_map/ppermute | solution.py:28
  122.6 15.0 %collective-permute-start.21 = (bf16[128,1152]{1,0:T(8,128)(2,1)S(1)}, bf16[128,1152]{1,0:T(8,128)(2,1)S(1)}, u32[]{:S(2)}, u32[]{:S(2)}) collective-permute-start(bf16[128,1152]{1,0:T(8,128)(2,1)S(1)} %add_convert_fusion), channel_id=1, source_target_pairs={{0,2},{2,4},{4,6},{6,0},{1,3},{3,5},{5,7},{7,1},{8,10},{10,12},{12... | collective-permute-start | bytes 884744 | tf_op jit(solution)/shard_map/ppermute | solution.py:28
  126.0 11.5 %collective-permute-start.25 = (bf16[128,1024]{1,0:T(8,128)(2,1)S(1)}, bf16[128,1024]{1,0:T(8,128)(2,1)S(1)}, u32[]{:S(2)}, u32[]{:S(2)}) collective-permute-start(bf16[128,1024]{1,0:T(8,128)(2,1)S(1)} %add_convert_fusion.1), channel_id=1, source_target_pairs={{0,6},{2,0},{4,2},{6,4},{1,7},{3,1},{5,3},{7,5},{8,14},{10,8},{12,... | collective-permute-start | bytes 786440 | tf_op jit(solution)/shard_map/ppermute | solution.py:28
  (7 other events, 5.2 us)

commit v3 on v2

--- a/solution.py
+++ b/solution.py
@@ -165,7 +165,6 @@
         cost_estimate=pl.CostEstimate(
             flops=3_000_000_000, bytes_accessed=8_000_000, transcendentals=1_000_000
         ),
-        compiler_params=LIMIT,
         name="summarize",
     )(bias, rate, *groups, halo, taps_x, taps_bc)
 
@@ -217,10 +216,9 @@
         for local in range(chunks // 2):
             chunk = lead + local
             at = slice(local * Q, local * Q + Q)
-            place = slice(chunk * Q, chunk * Q + Q)
-            b_rows = bc[place, :Q]
-            c_rows = bc[place, Q:]
-            x = xc[place, :].astype(F32)
+            b_rows = bc[at, :Q]
+            c_rows = bc[at, Q:]
+            x = xc[at, :].astype(F32)
             sloc_out[local] = state.astype(BF16)
             if chunk < chunks - 1:
                 kept = (x * widen(weight, heads, chunk, spread)).astype(BF16)
@@ -265,59 +263,67 @@
     rows, width = xc.shape
     chunks = rows // Q
     half = rows // 2
+    whole = lambda array: pl.BlockSpec(array.shape, lambda i: (0, 0))
+    near = lambda array: pl.BlockSpec((half, array.shape[1]), lambda i: (part, 0))
+    shapes = [
+        jax.ShapeDtypeStruct((half, width), BF16),
+        jax.ShapeDtypeStruct((half, width), BF16),
+        jax.ShapeDtypeStruct((chunks // 2, Q, width), BF16),
+        jax.ShapeDtypeStruct((8, width), F32),
+        jax.ShapeDtypeStruct((Q, width), F32),
+    ]
     return pl.pallas_call(
         inside_kernel(heads, chunks, part * chunks // 2),
-        in_specs=vmem_specs(9),
-        out_specs=vmem_specs(5, 0),
-        out_shape=[
-            jax.ShapeDtypeStruct((half, width), BF16),
-            jax.ShapeDtypeStruct((half, width), BF16),
-            jax.ShapeDtypeStruct((chunks // 2, Q, width), BF16),
-            jax.ShapeDtypeStruct((8, width), F32),
-            jax.ShapeDtypeStruct((Q, width), F32),
+        grid=(1,),
+        in_specs=[pl.BlockSpec(memory_space=pltpu.SMEM)]
+        + [whole(group) for group in groups]
+        + [near(xc), near(bc), whole(dt), whole(cumul), whole(state)],
+        out_specs=[
+            pl.BlockSpec(shape.shape, lambda i, n=len(shape.shape): (0,) * n) for shape in shapes
         ],
+        out_shape=shapes,
         scratch_shapes=[pltpu.VMEM((rows, width), BF16)],
         cost_estimate=pl.CostEstimate(
             flops=4_000_000_000, bytes_accessed=5_000_000, transcendentals=1_000_000
         ),
-        compiler_params=LIMIT,
         name="inside",
     )(skip, *groups, xc, bc, dt, cumul, state)
 
 
-def finish_kernel(away):
-    def kernel(bc, ig0, fz0, sloc0, ig1, fz1, sloc1, growth, entering, out):
-        start = entering[...].astype(F32)
-        c_at = lax.axis_index("c")
-        offset = 1 - c_at if away else c_at
-        for i in range(4):
-            ig, fz, sloc = ((ig0, fz0, sloc0), (ig1, fz1, sloc1))[i // 2]
-            chunk = 2 * i + offset
-            local = 2 * (i % 2) + offset
-            at = pl.ds(pl.multiple_of(local * Q, Q), Q)
-            state = sloc[local].astype(F32) + growth[pl.ds(chunk, 1), :] * start
-            c_rows = bc[pl.ds(pl.multiple_of(chunk * Q, Q), Q), Q:]
-            carried = jnp.dot(c_rows, state.astype(BF16), preferred_element_type=F32)
-            out[i * Q : i * Q + Q, :] = (
-                ig[at, :].astype(F32) + carried * fz[at, :].astype(F32)
-            ).astype(BF16)
-
-    return kernel
-
-
-def finish(away, bc, early, late, growth, entering):
-    shape = (bc.shape[0] // 2, entering.shape[1])
+def finish_kernel(sel, c_rows, ig0, fz0, sloc0, ig1, fz1, sloc1, growth, entering, out):
+    start = entering[...].astype(F32)
+    for i in range(4):
+        ig, fz, sloc = ((ig0, fz0, sloc0), (ig1, fz1, sloc1))[i // 2]
+        state = sloc[i % 2, 0].astype(F32) + growth[pl.ds(2 * i + sel[0], 1), :] * start
+        carried = jnp.dot(c_rows[i, 0], state.astype(BF16), preferred_element_type=F32)
+        out[i * Q : i * Q + Q, :] = (
+            ig[i % 2, 0].astype(F32) + carried * fz[i % 2, 0].astype(F32)
+        ).astype(BF16)
+
+
+def finish(sel, bc, early, late, growth, entering):
+    rows, width = bc.shape[0], entering.shape[1]
+    paired = lambda block: block.reshape(-1, 2, Q, block.shape[-1])
+    block = pl.BlockSpec((2, 1, Q, width), lambda i, sel: (0, sel[0], 0, 0))
     return pl.pallas_call(
-        finish_kernel(away),
-        in_specs=vmem_specs(9, 0),
-        out_specs=pl.BlockSpec(memory_space=pltpu.VMEM),
-        out_shape=jax.ShapeDtypeStruct(shape, BF16),
+        finish_kernel,
+        grid_spec=pltpu.PrefetchScalarGridSpec(
+            num_scalar_prefetch=1,
+            grid=(1,),
+            in_specs=[pl.BlockSpec((4, 1, Q, Q), lambda i, sel: (0, sel[0], 0, 1))]
+            + [block] * 6
+            + [
+                pl.BlockSpec(growth.shape, lambda i, sel: (0, 0)),
+                pl.BlockSpec(entering.shape, lambda i, sel: (0, 0)),
+            ],
+            out_specs=pl.BlockSpec((rows // 2, width), lambda i, sel: (0, 0)),
+        ),
+        out_shape=jax.ShapeDtypeStruct((rows // 2, width), BF16),
         cost_estimate=pl.CostEstimate(
             flops=1_500_000_000, bytes_accessed=3_000_000, transcendentals=0
         ),
-        compiler_params=LIMIT,
         name="finish",
-    )(bc, *early, *late, growth, entering)
+    )(sel, paired(bc), *map(paired, early), *map(paired, late), growth, entering)
 
 
 def project_kernel(distances):
@@ -530,9 +536,10 @@
     joined = join_rows(near, middle, far, before, row_growth, heads)
     entering = lax.all_to_all(joined, "z", 0, 0, tiled=True).reshape(Q, width)
 
-    away = finish(True, bc, early, late, growth, entering)
+    core = c_at.astype(jnp.int32)[None]
+    away = finish(1 - core, bc, early, late, growth, entering)
     arrived = swap(away)
-    kept = finish(False, bc, early, late, growth, entering)
+    kept = finish(core, bc, early, late, growth, entering)
     weights = [*weights[0], *weights[1]]
     far_low, far_high = project(kept, arrived, weights, (2,))
     right_low, left_low, low, right_high, left_high, high = project(

time: 140 us -> 130 us (0.929)
  the two profiles are of different devices: /device:TPU:38 before, /device:TPU:8 now
where the time goes in v3:
time: 130 us; the launch traced here: 128 us
  starting transfers between devices  43.4 us (33%)
  waiting for transfers between devices  30.6 us (24%)
  Pallas kernels  29.7 us (23%)
  matrix products  11 us (8%)
  local copies, waits for them, and re-layouts  9.79 us (8%)
  other arithmetic  3.1 us (2%)
    ppermute x22, starting transfers between devices, shift(): lax.ppermute(block, axis, [(i, (i + distance) % size) for i in range(size)])  21.9 us
    ppermute x22, waiting for transfers between devices, shift(): lax.ppermute(block, axis, [(i, (i + distance) % size) for i in range(size)])  18.9 us
    ppermute x4, starting transfers between devices, later(): lax.ppermute(block, axis, [(i, i + distance) for i in range(size - distan...  11.2 us
    pallas_call x2, Pallas kernels, inside(): pl.pallas_call(inside_kernel(heads, chunks, part * chunks // 2), grid=(1,...  9.82 us
    unnamed x37, local copies, waits for them, and re-layouts  7.6 us
    pallas_call x2, Pallas kernels, project(): pl.pallas_call(project_kernel(distances), in_specs=[vmem] * 6, out_specs=...  6.57 us
    all_to_all x1, starting transfers between devices, per_device(): lax.all_to_all(last.reshape(z_size, Q // z_size, width + Q), 'z', 0, 0, t...  5.94 us
    pallas_call x1, Pallas kernels, summarize(): pl.pallas_call(summary_kernel(heads, rows // Q), in_specs=vmem_specs(7, 2...  5.84 us
  transfers between devices with their start and end apart: 28, of which 16 were waited for; matrix products, arithmetic and copies ran while one was open for 14% of the time, Pallas kernels for 15%

profile of v3, /device:TPU:8, one launch (start us, length us, event | category | flops | bytes accessed | tf_op | source)
XLA Modules:
  0.0 128.0 jit_solution(10810788568905896341)
XLA Ops:
  0.0 2.0 %fusion.4 = (bf16[64,2048]{1,0:T(8,128)(2,1)}, bf16[64,2048]{1,0:T(8,128)(2,1)}) fusion(bf16[128,2048]{1,0:T(8,128)(2,1)} %param.12), kind=kLoop, calls=%fused_computation.35 | loop fusion | bytes 1048576 | tf_op jit(solution)/shard_map/slice | solution.py:469
  2.0 2.8 %collective-permute-start.6 = (bf16[64,2048]{1,0:T(8,128)(2,1)}, bf16[64,2048]{1,0:T(8,128)(2,1)S(1)}, u32[]{:S(2)}, u32[]{:S(2)}) collective-permute-start(bf16[64,2048]{1,0:T(8,128)(2,1)} %get-tuple-element.67), channel_id=1, source_target_pairs={{0,6},{2,0},{4,2},{6,4},{1,7},{3,1},{5,3},{7,5},{8,14},{10,8},{12,... | collective-permute-start | bytes 786440 | tf_op jit(solution)/shard_map/ppermute | solution.py:28
  4.8 0.8 collective-permute-start.1
  5.5 2.5 %collective-permute-start.5 = (bf16[64,2048]{1,0:T(8,128)(2,1)}, bf16[64,2048]{1,0:T(8,128)(2,1)}, u32[]{:S(2)}, u32[]{:S(2)}) collective-permute-start(bf16[64,2048]{1,0:T(8,128)(2,1)} %get-tuple-element.68), channel_id=1, source_target_pairs={{0,6},{2,0},{4,2},{6,4},{1,7},{3,1},{5,3},{7,5},{8,14},{10,8},{12,... | collective-permute-start | bytes 786440 | tf_op jit(solution)/shard_map/ppermute | solution.py:28
  8.0 1.0 copy.13
  9.2 1.2 constant_dynamic-update-slice_fusion.1
  10.4 1.4 %collective-permute-done.6 = bf16[64,2048]{1,0:T(8,128)(2,1)S(1)} collective-permute-done((bf16[64,2048]{1,0:T(8,128)(2,1)}, bf16[64,2048]{1,0:T(8,128)(2,1)S(1)}, u32[]{:S(2)}, u32[]{:S(2)}) %collective-permute-start.6) | collective-permute-done | bytes 262176 | tf_op jit(solution)/shard_map/ppermute | solution.py:28
  11.8 3.6 %collective-permute-start.10 = (bf16[64,2048]{1,0:T(8,128)(2,1)S(1)}, bf16[64,2048]{1,0:T(8,128)(2,1)S(1)}, u32[]{:S(2)}, u32[]{:S(2)}) collective-permute-start(bf16[64,2048]{1,0:T(8,128)(2,1)S(1)} %collective-permute-done.6), channel_id=1, source_target_pairs={{0,6},{2,0},{4,2},{6,4},{1,7},{3,1},{5,3},{7,5},{8,14},{10,8},{12,... | collective-permute-start | bytes 786440 | tf_op jit(solution)/shard_map/ppermute | solution.py:28
  15.4 0.1 collective-permute-done.2
  15.5 4.2 %collective-permute-done.1 = bf16[64,2048]{1,0:T(8,128)(2,1)} collective-permute-done((bf16[64,2048]{1,0:T(8,128)(2,1)}, bf16[64,2048]{1,0:T(8,128)(2,1)}, u32[]{:S(2)}, u32[]{:S(2)}) %collective-permute-start.1) | collective-permute-done | bytes 262176 | tf_op jit(solution)/shard_map/ppermute | solution.py:28
  19.7 1.0 constant_dynamic-update-slice_fusion.5
  20.7 1.0 constant_dynamic-update-slice_fusion.4
  21.6 0.6 collective-permute-start.3
  22.2 1.0 constant_dynamic-update-slice_fusion.9
  23.2 0.4 collective-permute-done.3
  23.6 0.4 collective-permute-start.7
  24.0 0.3 collective-permute-start.9
  24.3 1.3 %convolution_convert_fusion.2.g1 = bf16[256,896]{1,0:T(8,128)(2,1)S(1)} fusion(bf16[256,2048]{1,0:T(8,128)(2,1)S(1)} %constant_dynamic-update-slice_fusion.2, bf16[2048,8]{1,0:T(8,128)(2,1)S(1)} %copy.13, bf16[2048,256]{1,0:T(8,128)(2,1)S(1)} %copy-done.11, bf16[2048,512]{1,0:T(8,128)(2,1)S(1)} %copy-done.10, bf16[896]{0:T(1024)(128)(2,1)S(1)} %pad.3.clone), kind=kOutput, calls=%fused_computation.5 | convolution fusion | flops 954433536 | bytes 4687616 | tf_op jit(solution)/shard_map/dot_general | solution.py:504
  25.7 1.5 %convolution_convert_fusion.6.g1 = bf16[256,512]{1,0:T(8,128)(2,1)} fusion(bf16[256,2048]{1,0:T(8,128)(2,1)S(1)} %constant_dynamic-update-slice_fusion.2, bf16[2048,512]{1,0:T(8,128)(2,1)S(1)} %copy-done), kind=kOutput, calls=%fused_computation.9 | convolution fusion | flops 537001984 | bytes 3407872 | tf_op jit(solution)/shard_map/dot_general | solution.py:521
  27.2 1.3 %convolution_convert_fusion.1.g2 = bf16[256,896]{1,0:T(8,128)(2,1)S(1)} fusion(bf16[256,2048]{1,0:T(8,128)(2,1)S(1)} %constant_dynamic-update-slice_fusion.6, bf16[2048,8]{1,0:T(8,128)(2,1)S(1)} %copy.13, bf16[2048,256]{1,0:T(8,128)(2,1)S(1)} %copy-done.11, bf16[2048,512]{1,0:T(8,128)(2,1)S(1)} %copy-done.10, bf16[896]{0:T(1024)(128)(2,1)S(1)} %pad.3.clone), kind=kOutput, calls=%fused_computation.4 | convolution fusion | flops 954433536 | bytes 4687616 | tf_op jit(solution)/shard_map/dot_general | solution.py:504
  28.6 1.3 %convolution_convert_fusion.3.g0 = bf16[256,896]{1,0:T(8,128)(2,1)S(1)} fusion(bf16[256,2048]{1,0:T(8,128)(2,1)S(1)} %constant_dynamic-update-slice_fusion, bf16[2048,8]{1,0:T(8,128)(2,1)S(1)} %copy.13, bf16[2048,256]{1,0:T(8,128)(2,1)S(1)} %copy-done.11, bf16[2048,512]{1,0:T(8,128)(2,1)S(1)} %copy-done.10, bf16[896]{0:T(1024)(128)(2,1)S(1)} %pad.3.clone), kind=kOutput, calls=%fused_computation.6 | convolution fusion | flops 954433536 | bytes 4687616 | tf_op jit(solution)/shard_map/dot_general | solution.py:504
  29.9 1.5 %convolution_convert_fusion.5.g2 = bf16[256,512]{1,0:T(8,128)(2,1)} fusion(bf16[256,2048]{1,0:T(8,128)(2,1)S(1)} %constant_dynamic-update-slice_fusion.6, bf16[2048,512]{1,0:T(8,128)(2,1)S(1)} %copy-done), kind=kOutput, calls=%fused_computation.8 | convolution fusion | flops 537001984 | bytes 3407872 | tf_op jit(solution)/shard_map/dot_general | solution.py:521
  31.4 2.6 %collective-permute-done.9 = bf16[64,2048]{1,0:T(8,128)(2,1)S(1)} collective-permute-done((bf16[64,2048]{1,0:T(8,128)(2,1)}, bf16[64,2048]{1,0:T(8,128)(2,1)S(1)}, u32[]{:S(2)}, u32[]{:S(2)}) %collective-permute-start.9) | collective-permute-done | bytes 262176 | tf_op jit(solution)/shard_map/ppermute | solution.py:28
  34.1 0.6 collective-permute-start.12
  34.7 0.9 collective-permute-done.11
  35.6 0.4 collective-permute-done.12
  36.0 1.3 %convolution_convert_fusion.g3 = bf16[256,896]{1,0:T(8,128)(2,1)S(1)} fusion(bf16[256,2048]{1,0:T(8,128)(2,1)S(1)} %constant_dynamic-update-slice_fusion.10, bf16[2048,8]{1,0:T(8,128)(2,1)S(1)} %copy.13, bf16[2048,256]{1,0:T(8,128)(2,1)S(1)} %copy-done.11, bf16[2048,512]{1,0:T(8,128)(2,1)S(1)} %copy-done.10, bf16[896]{0:T(1024)(128)(2,1)S(1)} %pad.3.clone), kind=kOutput, calls=%fused_computation.3 | convolution fusion | flops 954433536 | bytes 4687616 | tf_op jit(solution)/shard_map/dot_general | solution.py:504
  37.4 3.8 %collective-permute-start.13 = (bf16[16,768]{1,0:T(8,128)(2,1)S(1)}, bf16[16,768]{1,0:T(8,128)(2,1)S(1)}, u32[]{:S(2)}, u32[]{:S(2)}) collective-permute-start(bf16[16,768]{1,0:T(8,128)(2,1)S(1)} %fusion.3), channel_id=1, source_target_pairs={{0,8},{8,16},{16,24},{24,32},{32,40},{40,48},{48,56},{56,64},{64,7... | collective-permute-start | bytes 73736 | tf_op jit(solution)/shard_map/ppermute | solution.py:33
  41.2 1.4 %convolution_convert_fusion.7.g0 = bf16[256,512]{1,0:T(8,128)(2,1)} fusion(bf16[256,2048]{1,0:T(8,128)(2,1)S(1)} %constant_dynamic-update-slice_fusion, bf16[2048,512]{1,0:T(8,128)(2,1)S(1)} %copy-done), kind=kOutput, calls=%fused_computation.10 | convolution fusion | flops 537001984 | bytes 3407872 | tf_op jit(solution)/shard_map/dot_general | solution.py:521
  42.6 4.2 %collective-permute-done.13.halo = bf16[16,768]{1,0:T(8,128)(2,1)S(1)} collective-permute-done((bf16[16,768]{1,0:T(8,128)(2,1)S(1)}, bf16[16,768]{1,0:T(8,128)(2,1)S(1)}, u32[]{:S(2)}, u32[]{:S(2)}) %collective-permute-start.13) | collective-permute-done | bytes 24608 | tf_op jit(solution)/shard_map/ppermute | solution.py:33
  46.8 0.6 copy-done.12
  47.4 5.8 %summarize.1 = (bf16[1024,512]{1,0:T(8,128)(2,1)}, bf16[1024,256]{1,0:T(8,128)(2,1)}, f32[128,128]{1,0:T(8,128)}, f32[128,128]{1,0:T(8,128)}, bf16[128,640]{1,0:T(8,128)(2,1)}) custom-call(f32[8]{0:T(128)} %bias.1, f32[8]{0:T(128)} %rate.1, bf16[256,896]{1,0:T(8,128)(2,1)} %copy-done.7, bf16[256,896]{1,0:T(8,128)(2,1)} %copy-done.5, ...), custom_call_target="tpu_custom_call" | custom-call | flops 3000000000 | bytes 8000000 | tf_op jit(solution)/shard_map/summarize/pallas_call | solution.py:150
  53.3 5.9 %all-to-all-start = ((bf16[8,16,640]{2,1,0:T(8,128)(2,1)}), bf16[8,16,640]{2,1,0:T(8,128)(2,1)S(1)}, u32[]{:S(2)}, u32[]{:S(2)}) async-start(bf16[8,16,640]{2,1,0:T(8,128)(2,1)} %bitcast.22), calls=%async_computation | async-start | bytes 327680 | tf_op jit(solution)/shard_map/all_to_all | solution.py:516
  59.2 1.4 %convolution_convert_fusion.4.g3 = bf16[256,512]{1,0:T(8,128)(2,1)} fusion(bf16[256,2048]{1,0:T(8,128)(2,1)S(1)} %copy-done.4, bf16[2048,512]{1,0:T(8,128)(2,1)S(1)} %copy-done), kind=kOutput, calls=%fused_computation.7 | convolution fusion | flops 537001984 | bytes 3407872 | tf_op jit(solution)/shard_map/dot_general | solution.py:521
  60.7 5.0 %inside.2 = (bf16[512,512]{1,0:T(8,128)(2,1)}, bf16[512,512]{1,0:T(8,128)(2,1)}, bf16[4,128,512]{2,1,0:T(8,128)(2,1)}, f32[8,512]{1,0:T(8,128)}, f32[128,512]{1,0:T(8,128)}) custom-call(f32[8]{0:T(128)} %skip.3, bf16[256,512]{1,0:T(8,128)(2,1)} %convolution_convert_fusion.7.g0, bf16[256,512]{1,0:T(8,128)(2,1)} %convolution_convert_fusion.6.g1, ...), custom_call_target="tpu_custom_call" | custom-call | flops 4000000000 | bytes 5000000 | tf_op jit(solution)/shard_map/inside/pallas_call | solution.py:275
  65.7 3.0 %all-to-all-done.pieces = bf16[8,16,640]{2,1,0:T(8,128)(2,1)S(1)} async-done(((bf16[8,16,640]{2,1,0:T(8,128)(2,1)}), bf16[8,16,640]{2,1,0:T(8,128)(2,1)S(1)}, u32[]{:S(2)}, u32[]{:S(2)}) %all-to-all-start) | async-done | bytes 163872 | tf_op jit(solution)/shard_map/all_to_all | solution.py:516
  68.7 0.2 row_scan.1
  68.9 0.7 collective-permute-start.16
  69.6 4.8 %collective-permute-start.15 = (bf16[16,640]{1,0:T(8,128)(2,1)S(1)}, bf16[16,640]{1,0:T(8,128)(2,1)S(1)}, u32[]{:S(2)}, u32[]{:S(2)}) collective-permute-start(bf16[16,640]{1,0:T(8,128)(2,1)S(1)} %get-tuple-element.54), channel_id=1, source_target_pairs={{0,128},{64,192},{1,129},{65,193},{2,130},{66,194},{3,131},{67,195... | collective-permute-start | bytes 61448 | tf_op jit(solution)/shard_map/ppermute | solution.py:33
  74.4 1.9 %collective-permute-start.14 = (bf16[16,640]{1,0:T(8,128)(2,1)S(1)}, bf16[16,640]{1,0:T(8,128)(2,1)S(1)}, u32[]{:S(2)}, u32[]{:S(2)}) collective-permute-start(bf16[16,640]{1,0:T(8,128)(2,1)S(1)} %get-tuple-element.54), channel_id=1, source_target_pairs={{0,64},{64,128},{128,192},{1,65},{65,129},{129,193},{2,66},{66,130... | collective-permute-start | bytes 61448 | tf_op jit(solution)/shard_map/ppermute | solution.py:33
  76.3 2.9 %multiply_convert_fusion = (bf16[512,1024]{1,0:T(8,128)(2,1)S(1)}, bf16[512,1024]{1,0:T(8,128)(2,1)}) fusion(bf16[512,2048]{1,0:T(8,128)(2,1)} %param.23, f32[512]{0:T(512)S(1)} %copy-done.9), kind=kLoop, calls=%fused_computation.1 | loop fusion | flops 3145728 | bytes 4196352 | tf_op jit(solution)/shard_map/convert_element_type | solution.py:525
  79.3 0.5 collective-permute-start.18
  79.8 0.3 collective-permute-done.14.near
  80.1 0.9 join_rows.1
  81.0 4.2 %all-to-all-start.1 = ((bf16[8,16,512]{2,1,0:T(8,128)(2,1)}), bf16[8,16,512]{2,1,0:T(8,128)(2,1)S(1)}, u32[]{:S(2)}, u32[]{:S(2)}) async-start(bf16[8,16,512]{2,1,0:T(8,128)(2,1)} %join_rows.1), calls=%async_computation.1 | async-start | bytes 262144 | tf_op jit(solution)/shard_map/all_to_all | solution.py:537
  85.2 4.8 %inside.3 = (bf16[512,512]{1,0:T(8,128)(2,1)}, bf16[512,512]{1,0:T(8,128)(2,1)}, bf16[4,128,512]{2,1,0:T(8,128)(2,1)}, f32[8,512]{1,0:T(8,128)}, f32[128,512]{1,0:T(8,128)}) custom-call(f32[8]{0:T(128)} %skip.3, bf16[256,512]{1,0:T(8,128)(2,1)} %convolution_convert_fusion.7.g0, bf16[256,512]{1,0:T(8,128)(2,1)} %convolution_convert_fusion.6.g1, ...), custom_call_target="tpu_custom_call" | custom-call | flops 4000000000 | bytes 5000000 | tf_op jit(solution)/shard_map/inside/pallas_call | solution.py:275
  90.0 4.3 %all-to-all-done.1 = bf16[8,16,512]{2,1,0:T(8,128)(2,1)S(1)} async-done(((bf16[8,16,512]{2,1,0:T(8,128)(2,1)}), bf16[8,16,512]{2,1,0:T(8,128)(2,1)S(1)}, u32[]{:S(2)}, u32[]{:S(2)}) %all-to-all-start.1) | async-done | bytes 131104 | tf_op jit(solution)/shard_map/all_to_all | solution.py:537
  94.3 0.7 copy-done.2
  94.9 2.6 %finish.3 = bf16[512,512]{1,0:T(8,128)(2,1)} custom-call(s32[1]{0:T(128)S(6)} %sub.3.sel, bf16[4,2,128,256]{3,2,1,0:T(8,128)(2,1)} %bitcast.25, bf16[2,2,128,512]{3,2,1,0:T(8,128)(2,1)} %bitcast.27, bf16[2,2,128,512]{3,2,1,0:T(8,128)(2,1)} %bitcast.29, bf16[2,2,128,512]{3,2,1,0:T(8,128)(2,1)} %bitcast.31, bf16[2,2,128,512]{3,2,1,0:T(8,128)(2,1)} %bitcast.33, ...), custom_call_target="tpu_custom_call" | custom-call | flops 1500000000 | bytes 3000000 | tf_op jit(solution)/shard_map/finish/pallas_call | solution.py:308
  97.5 2.7 %finish.2.kept = bf16[512,512]{1,0:T(8,128)(2,1)} custom-call(s32[1]{0:T(128)} %bitcast.sel, bf16[4,2,128,256]{3,2,1,0:T(8,128)(2,1)} %bitcast.26, bf16[2,2,128,512]{3,2,1,0:T(8,128)(2,1)} %bitcast.28, bf16[2,2,128,512]{3,2,1,0:T(8,128)(2,1)} %bitcast.30, bf16[2,2,128,512]{3,2,1,0:T(8,128)(2,1)} %bitcast.32, bf16[2,2,128,512]{3,2,1,0:T(8,128)(2,1)} %bitcast.34, ...), custom_call_target="tpu_custom_call" | custom-call | flops 1500000000 | bytes 3000000 | tf_op jit(solution)/shard_map/finish/pallas_call | solution.py:308
  100.2 1.0 copy-done.1
  101.3 2.7 %project.3 = (bf16[128,1152]{1,0:T(8,128)(2,1)S(1)}, bf16[128,1024]{1,0:T(8,128)(2,1)S(1)}) custom-call(bf16[512,512]{1,0:T(8,128)(2,1)S(1)} %copy-done.1, bf16[512,512]{1,0:T(8,128)(2,1)} %collective-permute-done.17.arrived, bf16[512,1024]{1,0:T(8,128)(2,1)} %get-tuple-element.66.own_low, bf16[512,1024]{1,0:T(8,128)(2,1)} %collective-permute-done.18.other_low, ...), custom_call_target="tpu_custom_call" | custom-call | flops 1000000000 | bytes 5000000 | tf_op jit(solution)/shard_map/project/pallas_call | solution.py:366
  104.0 0.1 collective-permute-start.20
  104.1 3.2 %collective-permute-start.24 = (bf16[128,1024]{1,0:T(8,128)(2,1)S(1)}, bf16[128,1024]{1,0:T(8,128)(2,1)S(1)}, u32[]{:S(2)}, u32[]{:S(2)}) collective-permute-start(bf16[128,1024]{1,0:T(8,128)(2,1)S(1)} %get-tuple-element.64), channel_id=1, source_target_pairs={{0,6},{2,0},{4,2},{6,4},{1,7},{3,1},{5,3},{7,5},{8,14},{10,8},{12,... | collective-permute-start | bytes 786440 | tf_op jit(solution)/shard_map/ppermute | solution.py:28
  107.3 3.8 %project.2 = (bf16[128,1152]{1,0:T(8,128)(2,1)S(1)}, bf16[128,1152]{1,0:T(8,128)(2,1)S(1)}, bf16[128,1152]{1,0:T(8,128)(2,1)S(1)}, bf16[128,1024]{1,0:T(8,128)(2...) custom-call(bf16[512,512]{1,0:T(8,128)(2,1)S(1)} %copy-done.1, ...), custom_call_target="tpu_custom_call" | custom-call | flops 3000000000 | bytes 5000000 | tf_op jit(solution)/shard_map/project/pallas_call | solution.py:366
  111.2 3.2 %collective-permute-start.22 = (bf16[128,1152]{1,0:T(8,128)(2,1)S(1)}, bf16[128,1152]{1,0:T(8,128)(2,1)S(1)}, u32[]{:S(2)}, u32[]{:S(2)}) collective-permute-start(bf16[128,1152]{1,0:T(8,128)(2,1)S(1)} %get-tuple-element.61), channel_id=1, source_target_pairs={{0,6},{2,0},{4,2},{6,4},{1,7},{3,1},{5,3},{7,5},{8,14},{10,8},{12,... | collective-permute-start | bytes 884744 | tf_op jit(solution)/shard_map/ppermute | solution.py:28
  114.5 0.3 collective-permute-done.20
  114.8 0.1 collective-permute-start.21
  115.0 3.3 %collective-permute-start.25 = (bf16[128,1024]{1,0:T(8,128)(2,1)S(1)}, bf16[128,1024]{1,0:T(8,128)(2,1)S(1)}, u32[]{:S(2)}, u32[]{:S(2)}) collective-permute-start(bf16[128,1024]{1,0:T(8,128)(2,1)S(1)} %add_convert_fusion.1), channel_id=1, source_target_pairs={{0,6},{2,0},{4,2},{6,4},{1,7},{3,1},{5,3},{7,5},{8,14},{10,8},{12,... | collective-permute-start | bytes 786440 | tf_op jit(solution)/shard_map/ppermute | solution.py:28
  118.3 3.4 %collective-permute-done.23.right_high = bf16[128,1024]{1,0:T(8,128)(2,1)S(1)} collective-permute-done((bf16[128,1024]{1,0:T(8,128)(2,1)S(1)}, bf16[128,1024]{1,0:T(8,128)(2,1)S(1)}, u32[]{:S(2)}, u32[]{:S(2)}) %collective-permute-start.23) | collective-permute-done | bytes 262176 | tf_op jit(solution)/shard_map/ppermute | solution.py:28
  121.6 0.2 collective-permute-done.22.left_low
  121.9 4.3 %collective-permute-done.25.left_high = bf16[128,1024]{1,0:T(8,128)(2,1)S(1)} collective-permute-done((bf16[128,1024]{1,0:T(8,128)(2,1)S(1)}, bf16[128,1024]{1,0:T(8,128)(2,1)S(1)}, u32[]{:S(2)}, u32[]{:S(2)}) %collective-permute-start.25) | collective-permute-done | bytes 262176 | tf_op jit(solution)/shard_map/ppermute | solution.py:28
  126.2 0.7 collective-permute-done.21.right_low
  126.9 1.1 close.1
  (58 shorter events, 0.6 us)
Async XLA Ops:
  0.0 25.7 %copy-start = (bf16[2048,512]{1,0:T(8,128)(2,1)S(1)}, bf16[2048,512]{1,0:T(8,128)(2,1)}, u32[]{:S(2)}) copy-start(bf16[2048,512]{1,0:T(8,128)(2,1)} %param.14) | copy-start | bytes 6291460
  2.0 9.8 %collective-permute-start.6 = (bf16[64,2048]{1,0:T(8,128)(2,1)}, bf16[64,2048]{1,0:T(8,128)(2,1)S(1)}, u32[]{:S(2)}, u32[]{:S(2)}) collective-permute-start(bf16[64,2048]{1,0:T(8,128)(2,1)} %get-tuple-element.67), channel_id=1, source_target_pairs={{0,6},{2,0},{4,2},{6,4},{1,7},{3,1},{5,3},{7,5},{8,14},{10,8},{12,... | collective-permute-start | bytes 786440 | tf_op jit(solution)/shard_map/ppermute | solution.py:28
  4.8 10.7 %collective-permute-start.2 = (bf16[64,2048]{1,0:T(8,128)(2,1)}, bf16[64,2048]{1,0:T(8,128)(2,1)}, u32[]{:S(2)}, u32[]{:S(2)}) collective-permute-start(bf16[64,2048]{1,0:T(8,128)(2,1)} %get-tuple-element.67), channel_id=1, source_target_pairs={{0,2},{2,4},{4,6},{6,0},{1,3},{3,5},{5,7},{7,1},{8,10},{10,12},{12... | collective-permute-start | bytes 786440 | tf_op jit(solution)/shard_map/ppermute | solution.py:28
  4.8 14.9 %collective-permute-start.1 = (bf16[64,2048]{1,0:T(8,128)(2,1)}, bf16[64,2048]{1,0:T(8,128)(2,1)}, u32[]{:S(2)}, u32[]{:S(2)}) collective-permute-start(bf16[64,2048]{1,0:T(8,128)(2,1)} %get-tuple-element.68), channel_id=1, source_target_pairs={{0,2},{2,4},{4,6},{6,0},{1,3},{3,5},{5,7},{7,1},{8,10},{10,12},{12... | collective-permute-start | bytes 786440 | tf_op jit(solution)/shard_map/ppermute | solution.py:28
  5.5 16.1 %collective-permute-start.5 = (bf16[64,2048]{1,0:T(8,128)(2,1)}, bf16[64,2048]{1,0:T(8,128)(2,1)}, u32[]{:S(2)}, u32[]{:S(2)}) collective-permute-start(bf16[64,2048]{1,0:T(8,128)(2,1)} %get-tuple-element.68), channel_id=1, source_target_pairs={{0,6},{2,0},{4,2},{6,4},{1,7},{3,1},{5,3},{7,5},{8,14},{10,8},{12,... | collective-permute-start | bytes 786440 | tf_op jit(solution)/shard_map/ppermute | solution.py:28
  8.0 20.5 %collective-permute-start = (bf16[128,2048]{1,0:T(8,128)(2,1)}, bf16[128,2048]{1,0:T(8,128)(2,1)S(1)}, u32[]{:S(2)}, u32[]{:S(2)}) collective-permute-start(bf16[128,2048]{1,0:T(8,128)(2,1)} %param.12), channel_id=1, source_target_pairs={{0,1},{1,0},{2,3},{3,2},{4,5},{5,4},{6,7},{7,6},{8,9},{9,8},{10,11... | collective-permute-start | bytes 1572872 | tf_op jit(solution)/shard_map/ppermute | solution.py:28
  9.2 15.2 %copy-start.10 = (bf16[2048,512]{1,0:T(8,128)(2,1)S(1)}, bf16[2048,512]{1,0:T(8,128)(2,1)}, u32[]{:S(2)}) copy-start(bf16[2048,512]{1,0:T(8,128)(2,1)} %param.13) | copy-start | bytes 6291460
  9.2 15.2 %copy-start.11 = (bf16[2048,256]{1,0:T(8,128)(2,1)S(1)}, bf16[2048,256]{1,0:T(8,128)(2,1)}, u32[]{:S(2)}) copy-start(bf16[2048,256]{1,0:T(8,128)(2,1)} %param.15) | copy-start | bytes 3145732
  11.8 22.3 %collective-permute-start.10 = (bf16[64,2048]{1,0:T(8,128)(2,1)S(1)}, bf16[64,2048]{1,0:T(8,128)(2,1)S(1)}, u32[]{:S(2)}, u32[]{:S(2)}) collective-permute-start(bf16[64,2048]{1,0:T(8,128)(2,1)S(1)} %collective-permute-done.6), channel_id=1, source_target_pairs={{0,6},{2,0},{4,2},{6,4},{1,7},{3,1},{5,3},{7,5},{8,14},{10,8},{12,... | collective-permute-start | bytes 786440 | tf_op jit(solution)/shard_map/ppermute | solution.py:28
  15.5 11.7 %collective-permute-start.8 = (bf16[64,2048]{1,0:T(8,128)(2,1)S(1)}, bf16[64,2048]{1,0:T(8,128)(2,1)S(1)}, u32[]{:S(2)}, u32[]{:S(2)}) collective-permute-start(bf16[64,2048]{1,0:T(8,128)(2,1)S(1)} %collective-permute-done.6), channel_id=1, source_target_pairs={{0,1},{1,0},{2,3},{3,2},{4,5},{5,4},{6,7},{7,6},{8,9},{9,8},{10,11... | collective-permute-start | bytes 786440 | tf_op jit(solution)/shard_map/ppermute | solution.py:28
  19.7 4.3 %collective-permute-start.4 = (bf16[64,2048]{1,0:T(8,128)(2,1)}, bf16[64,2048]{1,0:T(8,128)(2,1)S(1)}, u32[]{:S(2)}, u32[]{:S(2)}) collective-permute-start(bf16[64,2048]{1,0:T(8,128)(2,1)} %collective-permute-done.2), channel_id=1, source_target_pairs={{0,1},{1,0},{2,3},{3,2},{4,5},{5,4},{6,7},{7,6},{8,9},{9,8},{10,11... | collective-permute-start | bytes 786440 | tf_op jit(solution)/shard_map/ppermute | solution.py:28
  21.6 2.0 %collective-permute-start.3 = (bf16[64,2048]{1,0:T(8,128)(2,1)}, bf16[64,2048]{1,0:T(8,128)(2,1)S(1)}, u32[]{:S(2)}, u32[]{:S(2)}) collective-permute-start(bf16[64,2048]{1,0:T(8,128)(2,1)} %collective-permute-done.1), channel_id=1, source_target_pairs={{0,1},{1,0},{2,3},{3,2},{4,5},{5,4},{6,7},{7,6},{8,9},{9,8},{10,11... | collective-permute-start | bytes 786440 | tf_op jit(solution)/shard_map/ppermute | solution.py:28
  23.6 3.5 %collective-permute-start.7 = (bf16[64,2048]{1,0:T(8,128)(2,1)}, bf16[64,2048]{1,0:T(8,128)(2,1)S(1)}, u32[]{:S(2)}, u32[]{:S(2)}) collective-permute-start(bf16[64,2048]{1,0:T(8,128)(2,1)} %collective-permute-done.5), channel_id=1, source_target_pairs={{0,1},{1,0},{2,3},{3,2},{4,5},{5,4},{6,7},{7,6},{8,9},{9,8},{10,11... | collective-permute-start | bytes 786440 | tf_op jit(solution)/shard_map/ppermute | solution.py:28
  24.0 10.0 %collective-permute-start.9 = (bf16[64,2048]{1,0:T(8,128)(2,1)}, bf16[64,2048]{1,0:T(8,128)(2,1)S(1)}, u32[]{:S(2)}, u32[]{:S(2)}) collective-permute-start(bf16[64,2048]{1,0:T(8,128)(2,1)} %collective-permute-done.1), channel_id=1, source_target_pairs={{0,2},{2,4},{4,6},{6,0},{1,3},{3,5},{5,7},{7,1},{8,10},{10,12},{12... | collective-permute-start | bytes 786440 | tf_op jit(solution)/shard_map/ppermute | solution.py:28
  25.7 11.6 %copy-start.5 = (bf16[256,896]{1,0:T(8,128)(2,1)}, bf16[256,896]{1,0:T(8,128)(2,1)S(1)}, u32[]{:S(2)}) copy-start(bf16[256,896]{1,0:T(8,128)(2,1)S(1)} %convolution_convert_fusion.2.g1) | copy-start | bytes 1376260
  28.5 8.8 %copy-start.6 = (bf16[256,896]{1,0:T(8,128)(2,1)}, bf16[256,896]{1,0:T(8,128)(2,1)S(1)}, u32[]{:S(2)}) copy-start(bf16[256,896]{1,0:T(8,128)(2,1)S(1)} %convolution_convert_fusion.1.g2) | copy-start | bytes 1376260
  29.9 7.4 %copy-start.7 = (bf16[256,896]{1,0:T(8,128)(2,1)}, bf16[256,896]{1,0:T(8,128)(2,1)S(1)}, u32[]{:S(2)}) copy-start(bf16[256,896]{1,0:T(8,128)(2,1)S(1)} %convolution_convert_fusion.3.g0) | copy-start | bytes 1376260
  34.0 1.5 %collective-permute-start.11 = (bf16[64,2048]{1,0:T(8,128)(2,1)S(1)}, bf16[64,2048]{1,0:T(8,128)(2,1)S(1)}, u32[]{:S(2)}, u32[]{:S(2)}) collective-permute-start(bf16[64,2048]{1,0:T(8,128)(2,1)S(1)} %collective-permute-done.9), channel_id=1, source_target_pairs={{0,1},{1,0},{2,3},{3,2},{4,5},{5,4},{6,7},{7,6},{8,9},{9,8},{10,11... | collective-permute-start | bytes 786440 | tf_op jit(solution)/shard_map/ppermute | solution.py:28
  34.1 1.9 %collective-permute-start.12 = (bf16[64,2048]{1,0:T(8,128)(2,1)S(1)}, bf16[64,2048]{1,0:T(8,128)(2,1)S(1)}, u32[]{:S(2)}, u32[]{:S(2)}) collective-permute-start(bf16[64,2048]{1,0:T(8,128)(2,1)S(1)} %collective-permute-done.10), channel_id=1, source_target_pairs={{0,1},{1,0},{2,3},{3,2},{4,5},{5,4},{6,7},{7,6},{8,9},{9,8},{10,11... | collective-permute-start | bytes 786440 | tf_op jit(solution)/shard_map/ppermute | solution.py:28
  36.0 1.4 %copy-start.3 = (bf16[256,2048]{1,0:T(8,128)(2,1)}, bf16[256,2048]{1,0:T(8,128)(2,1)S(1)}, u32[]{:S(2)}) copy-start(bf16[256,2048]{1,0:T(8,128)(2,1)S(1)} %constant_dynamic-update-slice_fusion.10) | copy-start | bytes 3145732
  37.3 5.3 %copy-start.8 = (bf16[256,896]{1,0:T(8,128)(2,1)}, bf16[256,896]{1,0:T(8,128)(2,1)S(1)}, u32[]{:S(2)}) copy-start(bf16[256,896]{1,0:T(8,128)(2,1)S(1)} %convolution_convert_fusion.g3) | copy-start | bytes 1376260
  37.4 9.5 %collective-permute-start.13 = (bf16[16,768]{1,0:T(8,128)(2,1)S(1)}, bf16[16,768]{1,0:T(8,128)(2,1)S(1)}, u32[]{:S(2)}, u32[]{:S(2)}) collective-permute-start(bf16[16,768]{1,0:T(8,128)(2,1)S(1)} %fusion.3), channel_id=1, source_target_pairs={{0,8},{8,16},{16,24},{24,32},{32,40},{40,48},{48,56},{56,64},{64,7... | collective-permute-start | bytes 73736 | tf_op jit(solution)/shard_map/ppermute | solution.py:33
  42.6 16.6 %copy-start.4 = (bf16[256,2048]{1,0:T(8,128)(2,1)S(1)}, bf16[256,2048]{1,0:T(8,128)(2,1)}, u32[]{:S(2)}) copy-start(bf16[256,2048]{1,0:T(8,128)(2,1)} %copy-done.3) | copy-start | bytes 3145732
  46.8 0.6 copy-start.12
  53.3 15.4 %all-to-all-start = ((bf16[8,16,640]{2,1,0:T(8,128)(2,1)}), bf16[8,16,640]{2,1,0:T(8,128)(2,1)S(1)}, u32[]{:S(2)}, u32[]{:S(2)}) async-start(bf16[8,16,640]{2,1,0:T(8,128)(2,1)} %bitcast.22), calls=%async_computation | async-start | bytes 327680 | tf_op jit(solution)/shard_map/all_to_all | solution.py:516
  60.7 15.7 %copy-start.9 = (f32[512]{0:T(512)S(1)}, f32[512]{0:T(512)}, u32[]{:S(2)}) copy-start(f32[512]{0:T(512)} %param.22) | copy-start | bytes 6148
  68.9 10.9 %collective-permute-start.16 = (bf16[16,640]{1,0:T(8,128)(2,1)S(1)}, bf16[16,640]{1,0:T(8,128)(2,1)S(1)}, u32[]{:S(2)}, u32[]{:S(2)}) collective-permute-start(bf16[16,640]{1,0:T(8,128)(2,1)S(1)} %get-tuple-element.54), channel_id=1, source_target_pairs={{0,192},{1,193},{2,194},{3,195},{4,196},{5,197},{6,198},{7,199},{8... | collective-permute-start | bytes 61448 | tf_op jit(solution)/shard_map/ppermute | solution.py:33
  69.6 10.2 %collective-permute-start.15 = (bf16[16,640]{1,0:T(8,128)(2,1)S(1)}, bf16[16,640]{1,0:T(8,128)(2,1)S(1)}, u32[]{:S(2)}, u32[]{:S(2)}) collective-permute-start(bf16[16,640]{1,0:T(8,128)(2,1)S(1)} %get-tuple-element.54), channel_id=1, source_target_pairs={{0,128},{64,192},{1,129},{65,193},{2,130},{66,194},{3,131},{67,195... | collective-permute-start | bytes 61448 | tf_op jit(solution)/shard_map/ppermute | solution.py:33
  74.4 5.7 %collective-permute-start.14 = (bf16[16,640]{1,0:T(8,128)(2,1)S(1)}, bf16[16,640]{1,0:T(8,128)(2,1)S(1)}, u32[]{:S(2)}, u32[]{:S(2)}) collective-permute-start(bf16[16,640]{1,0:T(8,128)(2,1)S(1)} %get-tuple-element.54), channel_id=1, source_target_pairs={{0,64},{64,128},{128,192},{1,65},{65,129},{129,193},{2,66},{66,130... | collective-permute-start | bytes 61448 | tf_op jit(solution)/shard_map/ppermute | solution.py:33
  79.3 20.9 %collective-permute-start.19 = (bf16[512,1024]{1,0:T(8,128)(2,1)S(1)}, bf16[512,1024]{1,0:T(8,128)(2,1)}, u32[]{:S(2)}, u32[]{:S(2)}) collective-permute-start(bf16[512,1024]{1,0:T(8,128)(2,1)S(1)} %get-tuple-element.65.own_high), channel_id=1, source_target_pairs={{0,1},{1,0},{2,3},{3,2},{4,5},{5,4},{6,7},{7,6},{8,9},{9,8},{10,11... | collective-permute-start | bytes 3145736 | tf_op jit(solution)/shard_map/ppermute | solution.py:28
  79.3 20.9 %collective-permute-start.18 = (bf16[512,1024]{1,0:T(8,128)(2,1)}, bf16[512,1024]{1,0:T(8,128)(2,1)}, u32[]{:S(2)}, u32[]{:S(2)}) collective-permute-start(bf16[512,1024]{1,0:T(8,128)(2,1)} %get-tuple-element.66.own_low), channel_id=1, source_target_pairs={{0,1},{1,0},{2,3},{3,2},{4,5},{5,4},{6,7},{7,6},{8,9},{9,8},{10,11... | collective-permute-start | bytes 3145736 | tf_op jit(solution)/shard_map/ppermute | solution.py:28
  81.0 13.3 %all-to-all-start.1 = ((bf16[8,16,512]{2,1,0:T(8,128)(2,1)}), bf16[8,16,512]{2,1,0:T(8,128)(2,1)S(1)}, u32[]{:S(2)}, u32[]{:S(2)}) async-start(bf16[8,16,512]{2,1,0:T(8,128)(2,1)} %join_rows.1), calls=%async_computation.1 | async-start | bytes 262144 | tf_op jit(solution)/shard_map/all_to_all | solution.py:537
  94.3 0.7 copy-start.2
  97.5 2.7 %collective-permute-start.17 = (bf16[512,512]{1,0:T(8,128)(2,1)}, bf16[512,512]{1,0:T(8,128)(2,1)}, u32[]{:S(2)}, u32[]{:S(2)}) collective-permute-start(bf16[512,512]{1,0:T(8,128)(2,1)} %finish.3), channel_id=1, source_target_pairs={{0,1},{1,0},{2,3},{3,2},{4,5},{5,4},{6,7},{7,6},{8,9},{9,8},{10,11... | collective-permute-start | bytes 1572872 | tf_op jit(solution)/shard_map/ppermute | solution.py:28
  100.2 1.0 copy-start.1
  104.0 10.7 %collective-permute-start.20 = (bf16[128,1152]{1,0:T(8,128)(2,1)S(1)}, bf16[128,1152]{1,0:T(8,128)(2,1)S(1)}, u32[]{:S(2)}, u32[]{:S(2)}) collective-permute-start(bf16[128,1152]{1,0:T(8,128)(2,1)S(1)} %get-tuple-element.60), channel_id=1, source_target_pairs={{0,2},{2,4},{4,6},{6,0},{1,3},{3,5},{5,7},{7,1},{8,10},{10,12},{12... | collective-permute-start | bytes 884744 | tf_op jit(solution)/shard_map/ppermute | solution.py:28
  104.1 10.8 %collective-permute-start.24 = (bf16[128,1024]{1,0:T(8,128)(2,1)S(1)}, bf16[128,1024]{1,0:T(8,128)(2,1)S(1)}, u32[]{:S(2)}, u32[]{:S(2)}) collective-permute-start(bf16[128,1024]{1,0:T(8,128)(2,1)S(1)} %get-tuple-element.64), channel_id=1, source_target_pairs={{0,6},{2,0},{4,2},{6,4},{1,7},{3,1},{5,3},{7,5},{8,14},{10,8},{12,... | collective-permute-start | bytes 786440 | tf_op jit(solution)/shard_map/ppermute | solution.py:28
  111.2 10.5 %collective-permute-start.23 = (bf16[128,1024]{1,0:T(8,128)(2,1)S(1)}, bf16[128,1024]{1,0:T(8,128)(2,1)S(1)}, u32[]{:S(2)}, u32[]{:S(2)}) collective-permute-start(bf16[128,1024]{1,0:T(8,128)(2,1)S(1)} %get-tuple-element.62), channel_id=1, source_target_pairs={{0,2},{2,4},{4,6},{6,0},{1,3},{3,5},{5,7},{7,1},{8,10},{10,12},{12... | collective-permute-start | bytes 786440 | tf_op jit(solution)/shard_map/ppermute | solution.py:28
  111.2 10.6 %collective-permute-start.22 = (bf16[128,1152]{1,0:T(8,128)(2,1)S(1)}, bf16[128,1152]{1,0:T(8,128)(2,1)S(1)}, u32[]{:S(2)}, u32[]{:S(2)}) collective-permute-start(bf16[128,1152]{1,0:T(8,128)(2,1)S(1)} %get-tuple-element.61), channel_id=1, source_target_pairs={{0,6},{2,0},{4,2},{6,4},{1,7},{3,1},{5,3},{7,5},{8,14},{10,8},{12,... | collective-permute-start | bytes 884744 | tf_op jit(solution)/shard_map/ppermute | solution.py:28
  114.8 12.1 %collective-permute-start.21 = (bf16[128,1152]{1,0:T(8,128)(2,1)S(1)}, bf16[128,1152]{1,0:T(8,128)(2,1)S(1)}, u32[]{:S(2)}, u32[]{:S(2)}) collective-permute-start(bf16[128,1152]{1,0:T(8,128)(2,1)S(1)} %add_convert_fusion), channel_id=1, source_target_pairs={{0,2},{2,4},{4,6},{6,0},{1,3},{3,5},{5,7},{7,1},{8,10},{10,12},{12... | collective-permute-start | bytes 884744 | tf_op jit(solution)/shard_map/ppermute | solution.py:28
  115.0 11.2 %collective-permute-start.25 = (bf16[128,1024]{1,0:T(8,128)(2,1)S(1)}, bf16[128,1024]{1,0:T(8,128)(2,1)S(1)}, u32[]{:S(2)}, u32[]{:S(2)}) collective-permute-start(bf16[128,1024]{1,0:T(8,128)(2,1)S(1)} %add_convert_fusion.1), channel_id=1, source_target_pairs={{0,6},{2,0},{4,2},{6,4},{1,7},{3,1},{5,3},{7,5},{8,14},{10,8},{12,... | collective-permute-start | bytes 786440 | tf_op jit(solution)/shard_map/ppermute | solution.py:28
